TPU v7x, 32 devices: a whole 2x2x4 slice. The times are simulated.
32 devices in a mesh: groups: 2 (over x), dp: 4 (over y, core), fsdp: 4 (over z).
Axes of the slice: x: 2, y: 2, z: 4, core: 2. Of those that a mesh axis runs over, the one named last changes fastest.
Arguments:
- tokens: bfloat16 [4096, 4096], P(('groups', 'dp', 'fsdp')), parts along dimension 0, may hold values from -6 to 6
- up_weight: bfloat16 [4096, 14336], P('fsdp', 'dp'), may hold values from -0.09375 to 0.09375
- first_adapter_factors: bfloat16 [32, 32, 4096], P(('groups', 'dp', 'fsdp')), parts along dimension 0, may hold values from -0.09375 to 0.09375
- second_adapter_factors: bfloat16 [32, 32, 14336], P(('groups', 'dp', 'fsdp')), parts along dimension 0, may hold values from -1 to 1
- counts: int32 [32], P(('groups', 'dp', 'fsdp')), parts along dimension 0, may hold values from 1 to 128, as said below
- output_gradient: bfloat16 [4096, 14336], P(('groups', 'dp', 'fsdp')), parts along dimension 0, may hold values from -6 to 6
Outputs:
- act_out: bfloat16 [4096, 14336], P(('groups', 'dp', 'fsdp')), parts along dimension 0
- grad_a: float32 [32, 32, 4096], P(('groups', 'dp', 'fsdp')), parts along dimension 0
- second_factor_gradient: float32 [32, 32, 14336], P(('groups', 'dp', 'fsdp')), parts along dimension 0
There are 2 independent parts, one for each index of `groups`. A program takes and returns all parts, laid end to end along the dimension named above; an argument that names none is the same for every part. Nothing has to cross between parts.
Inputs may be any that keep to these rules, and one draw needn't show every extreme that they name: counts[d] is the number of live rows of adapter d. For d < 8, counts[d] + counts[d + 8] <= 160; in every draw some such pair has the counts 128 and 32.
All inputs are finite; a program needn't handle non-finite values.
Results may differ from a plain program's by a relative error of at most 0.0058.
Values may be sent and summed in bfloat16 or wider, within the bound.
No kernel may reach another device: no remote copies, remote signals or barrier semaphores. Data moves between devices by JAX's collectives and lax.ppermute only.
A program may use at most 128 MiB of HBM per device.

v0:
```python
import jax
import jax.numpy as jnp
from jax import lax
from jax.sharding import PartitionSpec as P

SLOTS = 128
PAIR_ROWS = 80


LOWRANK_SCALE = 2.0


def partner(x, axis, distance):
    return lax.ppermute(x, axis, [(i, i ^ 1 << distance) for i in range(lax.axis_size(axis))])


def silu_slope(inputs):
    gate_value = jax.nn.sigmoid(inputs)
    return gate_value * (1.0 + inputs * (1.0 - gate_value))


def take_block(rows_all, offset, row_count):
    filler = jnp.zeros((row_count,) + rows_all.shape[1:], rows_all.dtype)
    padded = jnp.concatenate([rows_all, filler], 0)
    return lax.dynamic_slice_in_dim(padded, offset, row_count, 0)


def place_block(rows_kept, block, offset, row_total):
    filler = jnp.zeros((block.shape[0],) + rows_kept.shape[1:], rows_kept.dtype)
    padded = jnp.concatenate([rows_kept, filler], 0)
    placed = lax.dynamic_update_slice_in_dim(padded, block, offset, 0)
    return placed[:row_total]


def per_device(
    tokens, up_weight, first_adapter_factors, second_adapter_factors, counts, output_gradient
):
    down_factor = first_adapter_factors[0]
    up_factor = second_adapter_factors[0]
    slot_total = tokens.shape[0]
    own_count = counts[0]
    live_rows = jnp.arange(slot_total, dtype=jnp.int32)[:, None] < own_count
    spare_rows = SLOTS - PAIR_ROWS
    half_bit = lax.axis_size("dp").bit_length() - 2
    kept_rows = jnp.minimum(own_count, PAIR_ROWS)
    outgoing = take_block(tokens, kept_rows, spare_rows)
    guest = partner(outgoing, "dp", half_bit)
    paired_rows = place_block(tokens[:PAIR_ROWS], guest, kept_rows, PAIR_ROWS)
    weight = lax.all_gather(up_weight, "fsdp", axis=0, tiled=True)
    blocks = jnp.dot(
        lax.all_gather(paired_rows, "dp", axis=0, tiled=True),
        weight,
        preferred_element_type=jnp.float32,
    ).astype(jnp.bfloat16)
    paired_base = lax.all_to_all(blocks, "dp", split_axis=0, concat_axis=1, tiled=True)
    returned = partner(take_block(paired_base, kept_rows, spare_rows), "dp", half_bit)
    base_output = place_block(paired_base, returned, kept_rows, SLOTS)
    rank_projection = lax.dot_general(
        tokens, down_factor, (((1,), (1,)), ((), ())), preferred_element_type=jnp.float32
    ).astype(jnp.bfloat16)
    adapter_update = jnp.dot(rank_projection, up_factor, preferred_element_type=jnp.float32)
    hidden_preactivation = base_output.astype(jnp.float32) + LOWRANK_SCALE * adapter_update
    act_out = jnp.where(live_rows, jax.nn.silu(hidden_preactivation), 0.0).astype(jnp.bfloat16)
    grad_pre = jnp.where(
        live_rows, output_gradient.astype(jnp.float32) * silu_slope(hidden_preactivation), 0.0
    ).astype(jnp.bfloat16)
    low_rank_gradient = (
        LOWRANK_SCALE
        * lax.dot_general(
            grad_pre, up_factor, (((1,), (1,)), ((), ())), preferred_element_type=jnp.float32
        )
    ).astype(jnp.bfloat16)
    second_factor_gradient = LOWRANK_SCALE * lax.dot_general(
        rank_projection, grad_pre, (((0,), (0,)), ((), ())), preferred_element_type=jnp.float32
    )
    grad_a = lax.dot_general(
        low_rank_gradient, tokens, (((0,), (0,)), ((), ())), preferred_element_type=jnp.float32
    )
    return (act_out, grad_a[None], second_factor_gradient[None])


def solution(mesh):
    placed = (
        P(("groups", "dp", "fsdp"), None),
        P("fsdp", "dp"),
        P(("groups", "dp", "fsdp"), None, None),
        P(("groups", "dp", "fsdp"), None, None),
        P(("groups", "dp", "fsdp")),
        P(("groups", "dp", "fsdp"), None),
    )
    return jax.shard_map(
        per_device,
        mesh=mesh,
        in_specs=placed,
        out_specs=(
            P(("groups", "dp", "fsdp"), None),
            P(("groups", "dp", "fsdp"), None, None),
            P(("groups", "dp", "fsdp"), None, None),
        ),
        check_vma=False,
    )
```

profile of v0, /device:TPU:0, one launch (start us, length us, event | category | flops | bytes accessed | tf_op | source)
XLA Modules:
  0.0 656.3 jit_solution(15328126115022104857)
XLA Ops:
  7.2 0.0 copy-start
  7.2 0.0 all-gather.3.cloned.1.call-start
  8.0 1.1 pad_dynamic-slice_fusion
  9.1 3.1 collective-permute-start
  12.2 1.4 broadcast_select_fusion
  13.6 7.7 %collective-permute-done = bf16[48,4096]{1,0:T(8,128)(2,1)S(1)} collective-permute-done((bf16[48,4096]{1,0:T(8,128)(2,1)S(1)}, bf16[48,4096]{1,0:T(8,128)(2,1)S(1)}, u32[]{:S(2)}, u32[]{:S(2)}) %collective-permute-start) | collective-permute-done | bytes 393248 | tf_op jit(solution)/shard_map/ppermute | solution.py:14
  21.3 1.8 dynamic_update_slice.6
  23.1 0.9 slice.6
  24.0 0.0 all-gather.3.cloned.1.call-update
  24.0 0.0 all-gather.5.cloned.1.call-start
  24.1 0.7 all-gather.5.cloned.1.call-update
  24.8 26.8 %all-gather.3.cloned.1.call-done = bf16[320,4096]{1,0:T(8,128)(2,1)} async-done(((bf16[80,4096]{1,0:T(8,128)(2,1)}), bf16[320,4096]{1,0:T(8,128)(2,1)}) %all-gather.3.cloned.1.call-update) | async-done | bytes 2621456 | tf_op jit(solution)/shard_map/all_gather | solution.py:51
  51.6 494.7 %all-gather.5.cloned.1.call-done = bf16[4096,3584]{1,0:T(8,128)(2,1)} async-done(((bf16[1024,3584]{1,0:T(8,128)(2,1)}), bf16[4096,3584]{1,0:T(8,128)(2,1)}) %all-gather.5.cloned.1.call-update) | async-done | bytes 29360144 | tf_op jit(solution)/shard_map/all_gather | solution.py:49
  546.3 15.8 %convolution_convert_fusion = bf16[320,3584]{1,0:T(8,128)(2,1)S(1)} fusion(bf16[320,4096]{1,0:T(8,128)(2,1)} %all-gather.3.cloned.1.call-done, bf16[4096,3584]{1,0:T(8,128)(2,1)} %all-gather.5.cloned.1.call-done), kind=kOutput, calls=%fused_computation.7 | convolution fusion | flops 9396387840 | bytes 34275328 | tf_op jit(solution)/shard_map/dot_general | solution.py:50
  562.1 30.3 %all_to_all.19 = bf16[4,80,3584]{2,1,0:T(8,128)(2,1)S(1)} all-to-all(bf16[4,80,3584]{2,1,0:T(8,128)(2,1)S(1)} %bitcast.34), channel_id=1, replica_groups=mesh['groups'=2,'dp'=4,'fsdp'=4] {'dp'}, dimensions={0} | all-to-all | bytes 4587520 | tf_op jit(solution)/shard_map/all_to_all | solution.py:55
  592.5 0.0 copy-start.1
  592.5 0.0 copy-start.3
  592.5 0.2 copy.10
  592.7 0.4 pad_dynamic-slice_fusion.1
  593.1 0.5 collective-permute-start.1
  593.6 0.1 copy-done.1
  593.7 0.0 copy-done.3
  593.7 0.5 convolution_convert_fusion.1
  594.2 2.1 concatenate.12
  596.3 28.7 %collective-permute-done.1 = bf16[48,14336]{1,0:T(8,128)(2,1)S(1)} collective-permute-done((bf16[48,14336]{1,0:T(8,128)(2,1)S(1)}, bf16[48,14336]{1,0:T(8,128)(2,1)S(1)}, u32[]{:S(2)}, u32[]{:S(2)}) %collective-permute-start.1) | collective-permute-done | bytes 1376288 | tf_op jit(solution)/shard_map/ppermute | solution.py:14
  625.1 8.1 %dynamic_update_slice.7 = bf16[128,14336]{1,0:T(8,128)(2,1)} dynamic-update-slice(bf16[128,14336]{1,0:T(8,128)(2,1)} %concatenate.12, bf16[48,14336]{1,0:T(8,128)(2,1)S(1)} %collective-permute-done.1, s32[]{:T(128)S(6)} %select_n.16, s32[]{:T(128)} %constant.2.clone.1) | dynamic-update-slice | bytes 2752516 | tf_op jit(solution)/shard_map/dynamic_update_slice | solution.py:31
  633.1 0.0 copy-done
  633.2 8.2 %select_convert_fusion = (bf16[128,14336]{1,0:T(8,128)(2,1)S(1)}, bf16[128,14336]{1,0:T(8,128)(2,1)}) fusion(bf16[128,14336]{1,0:T(8,128)(2,1)} %param.11, bf16[128,14336]{1,0:T(8,128)(2,1)} %dynamic_update_slice.7, pred[128]{0:T(512)(128)(4,1)S(1)} %iota_compare_fusion, bf16[128,32]{0,1:T(8,128)(2,1)S(1)} %convolution_convert_fusion.1, ...), kind=kOutput, calls=%fused_computation.3 | convolution fusion | flops 148635648 | bytes 15605888 | tf_op jit(solution)/shard_map/dot_general | solution.py:61
  641.3 0.0 copy-start.2
  641.3 1.8 copy-done.2
  643.1 1.8 fusion
  645.0 4.5 convolution_bitcast_fusion
  (1 shorter events, 0.0 us)
Async XLA Ops:
  7.2 626.0 %copy-start = (bf16[1,32,14336]{2,1,0:T(8,128)(2,1)S(1)}, bf16[1,32,14336]{2,1,0:T(8,128)(2,1)}, u32[]{:S(2)}) copy-start(bf16[1,32,14336]{2,1,0:T(8,128)(2,1)} %param.9) | copy-start | bytes 2752516
  7.2 44.4 %all-gather.3.cloned.1.call-start = ((), (), s32[]{:S(2)}) async-start(), calls=%async_computation.1 | async-start | bytes 3276800 | tf_op jit(solution)/shard_map/all_gather | solution.py:51
  9.1 12.2 %collective-permute-start = (bf16[48,4096]{1,0:T(8,128)(2,1)S(1)}, bf16[48,4096]{1,0:T(8,128)(2,1)S(1)}, u32[]{:S(2)}, u32[]{:S(2)}) collective-permute-start(bf16[48,4096]{1,0:T(8,128)(2,1)S(1)} %pad_dynamic-slice_fusion), channel_id=1, source_target_pairs={{0,8},{4,12},{8,0},{12,4},{1,9},{5,13},{9,1},{13,5},{2,10},{6,14},... | collective-permute-start | bytes 1179656 | tf_op jit(solution)/shard_map/ppermute | solution.py:14
  24.0 522.3 %all-gather.5.cloned.1.call-start = ((), (), s32[]{:S(2)}) async-start(), calls=%async_computation.2 | async-start | bytes 36700160 | tf_op jit(solution)/shard_map/all_gather | solution.py:49
  592.5 1.2 copy-start.1
  592.5 1.3 copy-start.3
  593.1 31.9 %collective-permute-start.1 = (bf16[48,14336]{1,0:T(8,128)(2,1)S(1)}, bf16[48,14336]{1,0:T(8,128)(2,1)S(1)}, u32[]{:S(2)}, u32[]{:S(2)}) collective-permute-start(bf16[48,14336]{1,0:T(8,128)(2,1)S(1)} %pad_dynamic-slice_fusion.1), channel_id=1, source_target_pairs={{0,8},{4,12},{8,0},{12,4},{1,9},{5,13},{9,1},{13,5},{2,10},{6,14},... | collective-permute-start | bytes 4128776 | tf_op jit(solution)/shard_map/ppermute | solution.py:14
  641.3 1.8 copy-start.2
Sparse Core Ops, SparseCore 0:
  24.2 27.3 all-gather.2
  53.2 493.0 all-gather.4
where the time goes:
time: 657 us; the launch traced here: 656 us
  waiting for transfers between devices  559 us (85%)
  matrix products  30.8 us (5%)
  blocking collectives  30.3 us (5%)
  local copies, waits for them, and re-layouts  16.7 us (3%)
  between operations  14.8 us (2%)
    all_gather x1, waiting for transfers between devices, per_device(): weight = lax.all_gather(up_weight, 'fsdp', axis=0, tiled=True)  495 us
    ppermute x2, waiting for transfers between devices, partner(): lax.ppermute(x, axis, [(i, i ^ 1 << distance) for i in range(lax.axis_siz...  36.5 us
    all_to_all x1, blocking collectives, per_device(): lax.all_to_all(blocks, 'dp', split_axis=0, concat_axis=1, tiled=True)  30.3 us
    all_gather x1, waiting for transfers between devices, per_device(): lax.all_gather(paired_rows, 'dp', axis=0, tiled=True)  26.8 us
    dot_general x1, matrix products, per_device(): jnp.dot(lax.all_gather(paired_rows, 'dp', axis=0, tiled=True), weight, pr...  15.8 us
  transfers between devices with their start and end apart: 4, of which 4 were waited for; matrix products, arithmetic and copies ran while one was open for 1% of the time, Pallas kernels for 0%

commit v1 on v0

--- a/solution.py
+++ b/solution.py
@@ -46,12 +46,15 @@
     outgoing = take_block(tokens, kept_rows, spare_rows)
     guest = partner(outgoing, "dp", half_bit)
     paired_rows = place_block(tokens[:PAIR_ROWS], guest, kept_rows, PAIR_ROWS)
-    weight = lax.all_gather(up_weight, "fsdp", axis=0, tiled=True)
-    blocks = jnp.dot(
-        lax.all_gather(paired_rows, "dp", axis=0, tiled=True),
-        weight,
-        preferred_element_type=jnp.float32,
+    dp_total, fsdp_total = lax.axis_size("dp"), lax.axis_size("fsdp")
+    sliced_rows = lax.all_to_all(paired_rows, "fsdp", split_axis=1, concat_axis=0, tiled=True)
+    slice_width = sliced_rows.shape[1]
+    all_rows = lax.all_gather(sliced_rows, "dp", axis=0, tiled=True)
+    all_rows = all_rows.reshape(dp_total, fsdp_total, PAIR_ROWS, slice_width).swapaxes(0, 1)
+    partial_blocks = jnp.dot(
+        all_rows.reshape(-1, slice_width), up_weight, preferred_element_type=jnp.float32
     ).astype(jnp.bfloat16)
+    blocks = lax.psum_scatter(partial_blocks, "fsdp", scatter_dimension=0, tiled=True)
     paired_base = lax.all_to_all(blocks, "dp", split_axis=0, concat_axis=1, tiled=True)
     returned = partner(take_block(paired_base, kept_rows, spare_rows), "dp", half_bit)
     base_output = place_block(paired_base, returned, kept_rows, SLOTS)

time: 657 us -> 341 us (0.52)
  waiting for transfers between devices: 559 us -> 218 us
  blocking collectives: 30.3 us -> 52.4 us
    all_gather x2 -> x1, waiting for transfers between devices: 522 us -> 24.7 us  [per_device(): all_rows = lax.all_gather(sliced_rows, 'dp', axis=0, tiled=True)]
    reduce_scatter x0 -> x1, waiting for transfers between devices: none -> 157 us  [per_device(): lax.psum_scatter(partial_blocks, 'fsdp', scatter_dimension=0, tiled=True)]
    all_to_all x0 -> x1, blocking collectives: none -> 21 us  [per_device(): lax.all_to_all(paired_rows, 'fsdp', split_axis=1, concat_axis=0, tiled=True)]
where the time goes in v1:
time: 341 us; the launch traced here: 340 us
  waiting for transfers between devices  218 us (64%)
  blocking collectives  52.4 us (15%)
  matrix products  30 us (9%)
  local copies, waits for them, and re-layouts  19.3 us (6%)
  between operations  14.8 us (4%)
  starting transfers between devices  3.6 us (1%)
    reduce_scatter x1, waiting for transfers between devices, per_device(): lax.psum_scatter(partial_blocks, 'fsdp', scatter_dimension=0, tiled=True)  157 us
    ppermute x2, waiting for transfers between devices, partner(): lax.ppermute(x, axis, [(i, i ^ 1 << distance) for i in range(lax.axis_siz...  36.5 us
    all_to_all x1, blocking collectives, per_device(): lax.all_to_all(blocks, 'dp', split_axis=0, concat_axis=1, tiled=True)  31.4 us
    all_gather x1, waiting for transfers between devices, per_device(): all_rows = lax.all_gather(sliced_rows, 'dp', axis=0, tiled=True)  24.7 us
    all_to_all x1, blocking collectives, per_device(): lax.all_to_all(paired_rows, 'fsdp', split_axis=1, concat_axis=0, tiled=True)  21 us
    dot_general x1, matrix products, per_device(): jnp.dot(all_rows.reshape(-1, slice_width), up_weight, preferred_element_t...  14.9 us
    dynamic_update_slice x2, local copies, waits for them, and re-layouts, place_block(): placed = lax.dynamic_update_slice_in_dim(padded, block, offset, 0)  11.3 us
    dot_general x1, matrix products, per_device(): jnp.dot(rank_projection, up_factor, preferred_element_type=jnp.float32)  8.16 us
  transfers between devices with their start and end apart: 4, of which 4 were waited for; matrix products, arithmetic and copies ran while one was open for 1% of the time, Pallas kernels for 0%

profile of v1, /device:TPU:0, one launch (start us, length us, event | category | flops | bytes accessed | tf_op | source)
XLA Modules:
  0.0 339.9 jit_solution(10477999457115856074)
XLA Ops:
  7.2 0.0 copy-start
  7.2 0.0 all-gather.2.cloned.1.call-start
  8.0 1.2 pad_dynamic-slice_fusion
  9.1 3.1 collective-permute-start
  12.2 1.4 broadcast_select_fusion
  13.6 7.7 %collective-permute-done = bf16[48,4096]{1,0:T(8,128)(2,1)S(1)} collective-permute-done((bf16[48,4096]{1,0:T(8,128)(2,1)S(1)}, bf16[48,4096]{1,0:T(8,128)(2,1)S(1)}, u32[]{:S(2)}, u32[]{:S(2)}) %collective-permute-start) | collective-permute-done | bytes 393248 | tf_op jit(solution)/shard_map/ppermute | solution.py:14
  21.3 2.3 dynamic_update_slice.6
  23.7 21.0 %all_to_all.38 = bf16[80,4,1024]{2,0,1:T(8,128)(2,1)} all-to-all(bf16[80,4,1024]{2,0,1:T(8,128)(2,1)S(1)} %bitcast.49), channel_id=1, replica_groups=mesh['groups'=2,'dp'=4,'fsdp'=4] {'fsdp'}, dimensions={1} | all-to-all | bytes 1310720 | tf_op jit(solution)/shard_map/all_to_all | solution.py:50
  44.6 0.0 all-gather.2.cloned.1.call-update
  44.7 0.0 reduce-scatter.2.cloned.1.call-start
  44.7 24.7 %all-gather.2.cloned.1.call-done = bf16[1280,1024]{1,0:T(8,128)(2,1)} async-done(((bf16[320,1024]{1,0:T(8,128)(2,1)}), bf16[1280,1024]{1,0:T(8,128)(2,1)}) %all-gather.2.cloned.1.call-update) | async-done | bytes 2621456 | tf_op jit(solution)/shard_map/all_gather | solution.py:52
  69.5 2.1 copy.16
  71.5 14.9 %convolution_convert_fusion = bf16[1280,3584]{1,0:T(8,128)(2,1)} fusion(bf16[1280,1024]{1,0:T(8,128)(2,1)S(1)} %bitcast.46, bf16[1024,3584]{1,0:T(8,128)(2,1)} %param.7), kind=kOutput, calls=%fused_computation.3 | convolution fusion | flops 9399828480 | bytes 19136512 | tf_op jit(solution)/shard_map/dot_general | solution.py:54
  86.4 0.0 reduce-scatter.2.cloned.1.call-update
  86.4 157.2 %reduce-scatter.2.cloned.1.call-done = bf16[320,3584]{1,0:T(8,128)(2,1)} async-done(((bf16[1280,3584]{1,0:T(8,128)(2,1)}), bf16[320,3584]{1,0:T(8,128)(2,1)}) %reduce-scatter.2.cloned.1.call-update) | async-done | bytes 2293776 | tf_op jit(solution)/shard_map/reduce_scatter | solution.py:57
  243.6 31.4 %all_to_all.39 = bf16[4,80,3584]{2,1,0:T(8,128)(2,1)S(1)} all-to-all(bf16[4,80,3584]{2,1,0:T(8,128)(2,1)} %bitcast.50), channel_id=1, replica_groups=mesh['groups'=2,'dp'=4,'fsdp'=4] {'dp'}, dimensions={0} | all-to-all | bytes 4587520 | tf_op jit(solution)/shard_map/all_to_all | solution.py:58
  275.0 0.0 copy-start.1
  275.0 0.0 copy-start.3
  275.0 0.2 copy.19
  275.2 0.4 pad_dynamic-slice_fusion.1
  275.7 0.5 collective-permute-start.1
  276.1 0.1 copy-done.1
  276.2 0.0 copy-done.3
  276.3 0.5 convolution_convert_fusion.1
  276.7 2.1 concatenate.12
  278.8 28.7 %collective-permute-done.1 = bf16[48,14336]{1,0:T(8,128)(2,1)S(1)} collective-permute-done((bf16[48,14336]{1,0:T(8,128)(2,1)S(1)}, bf16[48,14336]{1,0:T(8,128)(2,1)S(1)}, u32[]{:S(2)}, u32[]{:S(2)}) %collective-permute-start.1) | collective-permute-done | bytes 1376288 | tf_op jit(solution)/shard_map/ppermute | solution.py:14
  307.6 9.0 %dynamic_update_slice.7 = bf16[128,14336]{1,0:T(8,128)(2,1)} dynamic-update-slice(bf16[128,14336]{1,0:T(8,128)(2,1)} %concatenate.12, bf16[48,14336]{1,0:T(8,128)(2,1)S(1)} %collective-permute-done.1, s32[]{:T(128)S(6)} %select_n.16, s32[]{:T(128)} %constant.2.clone.1) | dynamic-update-slice | bytes 2752516 | tf_op jit(solution)/shard_map/dynamic_update_slice | solution.py:31
  316.6 0.0 copy-done
  316.6 8.2 %select_convert_fusion = (bf16[128,14336]{1,0:T(8,128)(2,1)S(1)}, bf16[128,14336]{1,0:T(8,128)(2,1)}) fusion(bf16[128,14336]{1,0:T(8,128)(2,1)} %param.11, bf16[128,14336]{1,0:T(8,128)(2,1)} %dynamic_update_slice.7, pred[128]{0:T(512)(128)(4,1)S(1)} %iota_compare_fusion, bf16[128,32]{0,1:T(8,128)(2,1)S(1)} %convolution_convert_fusion.1, ...), kind=kOutput, calls=%fused_computation.4 | convolution fusion | flops 148635648 | bytes 15605888 | tf_op jit(solution)/shard_map/dot_general | solution.py:64
  324.8 0.0 copy-start.2
  324.8 1.8 copy-done.2
  326.6 1.8 fusion
  328.4 4.6 %convolution_bitcast_fusion = f32[1,32,4096]{2,1,0:T(8,128)} fusion(bf16[128,4096]{1,0:T(8,128)(2,1)S(1)} %copy-done.1, bf16[128,14336]{1,0:T(8,128)(2,1)} %copy-done.2, bf16[1,32,14336]{2,1,0:T(8,128)(2,1)S(1)} %copy-done), kind=kOutput, calls=%fused_computation.8 | convolution fusion | flops 151003136 | bytes 6160384 | tf_op jit(solution)/shard_map/dot_general | solution.py:79
  (3 shorter events, 0.1 us)
Async XLA Ops:
  7.2 309.5 %copy-start = (bf16[1,32,14336]{2,1,0:T(8,128)(2,1)S(1)}, bf16[1,32,14336]{2,1,0:T(8,128)(2,1)}, u32[]{:S(2)}) copy-start(bf16[1,32,14336]{2,1,0:T(8,128)(2,1)} %param.9) | copy-start | bytes 2752516
  7.2 62.3 %all-gather.2.cloned.1.call-start = ((), (), s32[]{:S(2)}) async-start(), calls=%async_computation.3 | async-start | bytes 3276800 | tf_op jit(solution)/shard_map/all_gather | solution.py:52
  9.1 12.2 %collective-permute-start = (bf16[48,4096]{1,0:T(8,128)(2,1)S(1)}, bf16[48,4096]{1,0:T(8,128)(2,1)S(1)}, u32[]{:S(2)}, u32[]{:S(2)}) collective-permute-start(bf16[48,4096]{1,0:T(8,128)(2,1)S(1)} %pad_dynamic-slice_fusion), channel_id=1, source_target_pairs={{0,8},{4,12},{8,0},{12,4},{1,9},{5,13},{9,1},{13,5},{2,10},{6,14},... | collective-permute-start | bytes 1179656 | tf_op jit(solution)/shard_map/ppermute | solution.py:14
  44.7 199.0 %reduce-scatter.2.cloned.1.call-start = ((), (), s32[]{:S(2)}) async-start(), calls=%async_computation.4 | async-start | bytes 11468800 | tf_op jit(solution)/shard_map/reduce_scatter | solution.py:57
  275.0 1.2 copy-start.1
  275.0 1.3 copy-start.3
  275.7 31.9 %collective-permute-start.1 = (bf16[48,14336]{1,0:T(8,128)(2,1)S(1)}, bf16[48,14336]{1,0:T(8,128)(2,1)S(1)}, u32[]{:S(2)}, u32[]{:S(2)}) collective-permute-start(bf16[48,14336]{1,0:T(8,128)(2,1)S(1)} %pad_dynamic-slice_fusion.1), channel_id=1, source_target_pairs={{0,8},{4,12},{8,0},{12,4},{1,9},{5,13},{9,1},{13,5},{2,10},{6,14},... | collective-permute-start | bytes 4128776 | tf_op jit(solution)/shard_map/ppermute | solution.py:14
  324.8 1.8 copy-start.2
Sparse Core Ops, SparseCore 0:
  44.8 24.6 all-gather.1
  86.5 157.0 reduce-scatter.1

commit v2 on v1

--- a/solution.py
+++ b/solution.py
@@ -1,7 +1,12 @@
+import functools
+
 import jax
 import jax.numpy as jnp
 from jax import lax
+from jax.experimental import pallas as pl
+from jax.experimental.pallas import tpu as pltpu
 from jax.sharding import PartitionSpec as P
+
 
 SLOTS = 128
 PAIR_ROWS = 80
@@ -32,22 +37,21 @@
     return placed[:row_total]
 
 
-def per_device(
-    tokens, up_weight, first_adapter_factors, second_adapter_factors, counts, output_gradient
+def after(x, *others):
+    return lax.optimization_barrier((x,) + others)[0]
+
+
+def scattered_plan(
+    tokens, up_weight, down_factor, up_factor, own_count, output_gradient
 ):
-    down_factor = first_adapter_factors[0]
-    up_factor = second_adapter_factors[0]
-    slot_total = tokens.shape[0]
-    own_count = counts[0]
-    live_rows = jnp.arange(slot_total, dtype=jnp.int32)[:, None] < own_count
+    dp_total, fsdp_total = lax.axis_size("dp"), lax.axis_size("fsdp")
+    live_rows = jnp.arange(tokens.shape[0], dtype=jnp.int32)[:, None] < own_count
     spare_rows = SLOTS - PAIR_ROWS
-    half_bit = lax.axis_size("dp").bit_length() - 2
+    half_bit = dp_total.bit_length() - 2
     kept_rows = jnp.minimum(own_count, PAIR_ROWS)
-    outgoing = take_block(tokens, kept_rows, spare_rows)
-    guest = partner(outgoing, "dp", half_bit)
-    paired_rows = place_block(tokens[:PAIR_ROWS], guest, kept_rows, PAIR_ROWS)
-    dp_total, fsdp_total = lax.axis_size("dp"), lax.axis_size("fsdp")
-    sliced_rows = lax.all_to_all(paired_rows, "fsdp", split_axis=1, concat_axis=0, tiled=True)
+    guest = partner(take_block(tokens, kept_rows, spare_rows), "dp", half_bit)
+    packed = place_block(tokens[:PAIR_ROWS], guest, kept_rows, PAIR_ROWS)
+    sliced_rows = lax.all_to_all(packed, "fsdp", split_axis=1, concat_axis=0, tiled=True)
     slice_width = sliced_rows.shape[1]
     all_rows = lax.all_gather(sliced_rows, "dp", axis=0, tiled=True)
     all_rows = all_rows.reshape(dp_total, fsdp_total, PAIR_ROWS, slice_width).swapaxes(0, 1)
@@ -67,15 +71,317 @@
     grad_pre = jnp.where(
         live_rows, output_gradient.astype(jnp.float32) * silu_slope(hidden_preactivation), 0.0
     ).astype(jnp.bfloat16)
-    low_rank_gradient = (
-        LOWRANK_SCALE
-        * lax.dot_general(
-            grad_pre, up_factor, (((1,), (1,)), ((), ())), preferred_element_type=jnp.float32
-        )
-    ).astype(jnp.bfloat16)
+    low_sum = lax.dot_general(
+        grad_pre, up_factor, (((1,), (1,)), ((), ())), preferred_element_type=jnp.float32
+    )
     second_factor_gradient = LOWRANK_SCALE * lax.dot_general(
         rank_projection, grad_pre, (((0,), (0,)), ((), ())), preferred_element_type=jnp.float32
     )
+    return act_out, low_sum, second_factor_gradient
+
+
+def tail_kernel(
+    slots_ref, counts_ref, own_ref, beside_ref, across_ref, diagonal_ref, rank_ref, rank_t_ref,
+    turn_ref, factor_ref, cotangent_ref, low_in_ref, *rest
+):
+    act_ref, second_ref, low_ref, base_ref = rest[-4:]
+    which, tile = pl.program_id(0), pl.program_id(1)
+
+    @pl.when((which == 0) & (tile == 0))
+    def _():
+        low_ref[...] = low_in_ref[...]
+
+    for index, source_ref in enumerate((own_ref, beside_ref, across_ref, diagonal_ref)):
+
+        @pl.when(which == index)
+        def _(source_ref=source_ref):
+            base_ref[...] = source_ref[...]
+
+    base = jnp.dot(turn_ref[...], base_ref[...], preferred_element_type=jnp.float32)
+    factor = factor_ref[...]
+    update = jnp.dot(rank_ref[...], factor, preferred_element_type=jnp.float32)
+    inputs = base + LOWRANK_SCALE * update
+    gate_value = jax.nn.sigmoid(inputs)
+    live = lax.broadcasted_iota(jnp.int32, inputs.shape, 0) < counts_ref[0]
+    act_ref[...] = jnp.where(live, inputs * gate_value, 0.0).astype(jnp.bfloat16)
+    slope = gate_value * (1.0 + inputs * (1.0 - gate_value))
+    grad_pre = cotangent_ref[...].astype(jnp.float32) * slope
+    grad_pre = jnp.where(live, grad_pre, 0.0).astype(jnp.bfloat16)
+    second_ref[...] = LOWRANK_SCALE * jnp.dot(
+        rank_t_ref[...], grad_pre, preferred_element_type=jnp.float32
+    )
+    low_ref[...] += lax.dot_general(
+        grad_pre, factor, (((1,), (1,)), ((), ())), preferred_element_type=jnp.float32
+    )
+
+
+def tail(bases, rank, rank_t, turn, factor, cotangent, low, made, slots, count, offset, unit):
+    width = bases[0].shape[1]
+    rank_total, hidden = factor.shape
+    start = offset // unit
+
+    def local(i, t, slots, counts):
+        return (0, t)
+
+    def whole(i, t, slots, counts):
+        return (0, 0)
+
+    def placed(i, t, slots, counts):
+        return (0, slots[i] + start + t)
+
+    in_specs = [pl.BlockSpec((SLOTS, unit), local)] * 4 + [
+        pl.BlockSpec(rank.shape, whole),
+        pl.BlockSpec(rank_t.shape, whole),
+        pl.BlockSpec(turn.shape, whole),
+        pl.BlockSpec((rank_total, unit), placed),
+        pl.BlockSpec((SLOTS, unit), placed),
+        pl.BlockSpec(low.shape, whole),
+    ]
+    operands = [*bases, rank, rank_t, turn, factor, cotangent, low]
+    aliases = {}
+    if made is not None:
+        in_specs += [pl.BlockSpec(memory_space=pl.ANY)] * 2
+        aliases = {2 + len(operands): 0, 3 + len(operands): 1}
+        operands += list(made)
+    act_out, second, low = pl.pallas_call(
+        tail_kernel,
+        name="tail",
+        out_shape=(
+            jax.ShapeDtypeStruct((SLOTS, hidden), jnp.bfloat16),
+            jax.ShapeDtypeStruct((rank_total, hidden), jnp.float32),
+            jax.ShapeDtypeStruct(low.shape, jnp.float32),
+        ),
+        grid_spec=pltpu.PrefetchScalarGridSpec(
+            num_scalar_prefetch=2,
+            grid=(4, width // unit),
+            in_specs=in_specs,
+            out_specs=(
+                pl.BlockSpec((SLOTS, unit), placed),
+                pl.BlockSpec((rank_total, unit), placed),
+                pl.BlockSpec(low.shape, whole),
+            ),
+            scratch_shapes=[pltpu.VMEM((SLOTS, unit), jnp.bfloat16)],
+        ),
+        input_output_aliases=aliases,
+        cost_estimate=pl.CostEstimate(
+            flops=2 * 4 * width * SLOTS * (SLOTS + 3 * rank_total),
+            bytes_accessed=4 * width * SLOTS * 8,
+            transcendentals=4 * width * SLOTS,
+        ),
+        compiler_params=pltpu.CompilerParams(
+            dimension_semantics=("arbitrary", "arbitrary"), vmem_limit_bytes=6 * 2**20
+        ),
+    )(slots, count, *operands)
+    return (act_out, second), low
+
+
+def chunk_plan(width):
+    if width % (7 * 128) == 0:
+        return width // 7, (1,) * 7, (2, 2, 2, 1)
+    for total in (8, 4, 2):
+        if width % (total * 128) == 0:
+            return width // total, (1,) * total, (1,) * total
+    return width, (1,), (1,)
+
+
+def plane_plan(
+    tokens, up_weight, down_factor, up_factor, own_count, output_gradient
+):
+    groups = lax.axis_size("groups")
+    place, group = lax.axis_index("fsdp"), lax.axis_index("groups")
+    position = lax.axis_index("dp")
+    upper = position >= 2
+    inner = (place == 1) | (place == 2)
+    near = jnp.where(place < 2, 1, 2)
+    far = 3 - near
+    slice_width, width = up_weight.shape
+    part = slice_width // groups
+    unit, sizes, batches = chunk_plan(width)
+    chunks = len(sizes)
+    offsets = [sum(sizes[:c]) * unit for c in range(chunks)]
+    spare = SLOTS - PAIR_ROWS
+    pair_total = 2 * PAIR_ROWS
+    home_total = 2 * pair_total
+    beside = [(0, 1), (1, 0), (2, 3), (3, 2)]
+    across = [(0, 2), (2, 0), (1, 3), (3, 1)]
+    diagonal = [(0, 3), (3, 0), (1, 2), (2, 1)]
+    inward = [(0, 1), (3, 2)]
+    outward = [(1, 0), (2, 3)]
+    middle = [(1, 2), (2, 1)]
+    crossing = [(0, 2), (3, 1)]
+
+    row = jnp.arange(SLOTS, dtype=jnp.int32)
+    source = jnp.where(upper, SLOTS - 1 - row, row)
+    turn = (source[:, None] == row[None, :]).astype(jnp.bfloat16)
+    ordered = jnp.dot(turn, tokens, preferred_element_type=jnp.float32).astype(jnp.bfloat16)
+    spill = jnp.where(upper, ordered[:spare], ordered[PAIR_ROWS:])
+    guest = lax.ppermute(spill, "dp", across)
+
+    def own_part(weight, c):
+        return lax.dynamic_slice(
+            weight, (group * part, offsets[c]), (part, sizes[c] * unit)
+        )
+
+    first_part = own_part(after(up_weight, spill), 0)
+    lines = {0: lax.ppermute(first_part, "fsdp", inward)}
+    rest_weight = after(up_weight, first_part)
+    parts = [first_part] + [own_part(rest_weight, c) for c in range(1, chunks)]
+    column_weights = [
+        rest_weight[:, offsets[c] : offsets[c] + sizes[c] * unit] for c in range(chunks)
+    ]
+    guest, *column_weights = lax.optimization_barrier((guest, *column_weights))
+
+    spot = jnp.where(upper, PAIR_ROWS, 0) + jnp.arange(PAIR_ROWS, dtype=jnp.int32)[:, None]
+    is_own = jnp.where(upper, pair_total - 1 - spot, spot) < own_count
+    kept = jnp.where(upper, ordered[spare:], ordered[:PAIR_ROWS])
+    blank = jnp.zeros((PAIR_ROWS - spare, guest.shape[1]), guest.dtype)
+    placed = jnp.where(
+        upper, jnp.concatenate([guest, blank], 0), jnp.concatenate([blank, guest], 0)
+    )
+    touched = (spot >= PAIR_ROWS - spare) & (spot < SLOTS)
+    packed = jnp.where(touched & ~is_own, placed, kept)
+
+    def columns(target):
+        outer = jnp.where(target < 2, 0, 3)
+        pieces = [lax.dynamic_slice_in_dim(packed, target * slice_width, slice_width, 1)]
+        for step in range(groups):
+            origin = outer * slice_width + lax.rem(group + step, groups) * part
+            pieces.append(lax.dynamic_slice_in_dim(packed, origin, part, 1))
+        return jnp.concatenate(pieces, 1)
+
+    def start_weight(c, *order):
+        return lax.ppermute(after(parts[c], *order), "fsdp", inward)
+
+    def share_weight(c, *order):
+        line = lines[c]
+        pieces = [line]
+        line = after(line, *order)
+        for step in range(1, groups):
+            pairs = [(i, (i - step) % groups) for i in range(groups)]
+            pieces.append(lax.ppermute(line, "groups", pairs))
+        return pieces
+
+    def ordered_pair(mine):
+        theirs = lax.ppermute(mine, "dp", across)
+        return jnp.concatenate(
+            [jnp.where(upper, theirs, mine), jnp.where(upper, mine, theirs)], 0
+        )
+
+    far_columns = columns(far)
+    from_far = lax.ppermute(far_columns, "fsdp", middle)
+    near_columns = columns(near)
+    from_outer = lax.ppermute(near_columns, "fsdp", inward)
+    from_far_outer = lax.ppermute(far_columns, "fsdp", crossing)
+    shared = {0: share_weight(0, near_columns)}
+    near_pair = ordered_pair(near_columns)
+    for c in range(1, min(3, chunks)):
+        lines[c] = start_weight(c, near_columns)
+    far_pair = ordered_pair(from_far)
+    far_outer_pair = ordered_pair(from_far_outer)
+    far_pairs = jnp.concatenate([far_pair, far_outer_pair], 0)
+    far_others = lax.ppermute(far_pairs, "dp", beside)
+    if chunks > 1:
+        shared[1] = share_weight(1, far_pairs)
+    far_rows = jnp.concatenate(
+        [far_pair, far_others[:pair_total], far_outer_pair, far_others[pair_total:]], 0
+    )
+    outer_pair = ordered_pair(after(from_outer, far_pairs))
+    near_pairs = jnp.concatenate([near_pair, outer_pair], 0)
+    near_others = lax.ppermute(after(near_pairs, far_rows), "dp", beside)
+
+    rank = lax.dot_general(
+        tokens, down_factor, (((1,), (1,)), ((), ())), preferred_element_type=jnp.float32
+    ).astype(jnp.bfloat16)
+    rank_t = rank.T
+    slots = (position ^ jnp.arange(4, dtype=jnp.int32)) * (width // unit)
+    low = jnp.zeros((SLOTS, rank.shape[1]), jnp.float32)
+    count = own_count.reshape(1)
+
+    def send(c, *order):
+        weight = jnp.concatenate([column_weights[c]] + shared[c], 0)
+        rows = after(far_rows, *order) if order else far_rows
+        outgoing = jnp.dot(rows, weight, preferred_element_type=jnp.float32)
+        outgoing = outgoing.astype(jnp.bfloat16)
+        return weight, outgoing, lax.ppermute(outgoing, "fsdp", middle)
+
+    sent = {0: send(0)}
+    last = sent[0][1]
+    near_others = after(near_others, last)
+    near_rows = jnp.concatenate(
+        [near_pair, near_others[:pair_total], outer_pair, near_others[pair_total:]], 0
+    )
+
+    def finish(c, *order):
+        weight, _, incoming = sent[c]
+        rows = after(near_rows, *order)
+        summed = jnp.dot(rows, weight, preferred_element_type=jnp.float32)
+        summed = (summed + incoming.astype(jnp.float32)).astype(jnp.bfloat16)
+        return summed, lax.ppermute(summed[home_total:], "fsdp", outward)
+
+    def hand_out(members, *order):
+        handed = [after(handed, *order) for _, handed in members]
+        homes = [
+            jnp.where(inner, summed[:home_total], back)
+            for (summed, _), back in zip(members, handed, strict=True)
+        ]
+        home = jnp.concatenate(homes, 1).reshape(2, pair_total, -1)
+        shape = (1, SLOTS, home.shape[2])
+        same, other = jnp.where(upper, pair_total - SLOTS, 0), jnp.where(upper, 0, pair_total - SLOTS)
+        cuts = [
+            lax.dynamic_slice(home, (pair, row_at, 0), shape)[0]
+            for pair, row_at in ((0, same), (1, same), (0, other), (1, other))
+        ]
+        opposite = lax.ppermute(cuts[2], "dp", across)
+        cornered = lax.ppermute(cuts[3], "dp", diagonal)
+        adjacent = lax.ppermute(cuts[1], "dp", beside)
+        return cuts, [cuts[0], adjacent, opposite, cornered]
+
+    batch_ends = [sum(batches[: b + 1]) - 1 for b in range(len(batches))]
+    made = None
+    summed, pending = {}, []
+    for i in range(chunks + 1):
+        if i + 3 < chunks:
+            lines[i + 3] = start_weight(i + 3, last)
+        if i + 2 < chunks:
+            shared[i + 2] = share_weight(i + 2, last)
+        if i + 1 < chunks:
+            sent[i + 1] = send(i + 1, last)
+            last = sent[i + 1][1]
+        if i < chunks:
+            summed[i] = finish(i, last)
+            last = summed[i][0]
+        if pending and (i < chunks or len(pending) > 1):
+            bases, offset = pending.pop(0)
+            bases[3] = after(bases[3], last)
+            made, low = tail(
+                bases, rank, rank_t, turn, up_factor, output_gradient, low, made, slots, count,
+                offset, unit,
+            )
+            last = low
+        if i - 1 in batch_ends:
+            b = batch_ends.index(i - 1)
+            begin = batch_ends[b] - batches[b] + 1
+            cuts, bases = hand_out([summed[c] for c in range(begin, i)], last)
+            pending.append((bases, offsets[begin]))
+            last = cuts[0]
+    for bases, offset in pending:
+        bases[3] = after(bases[3], last)
+        made, low = tail(
+            bases, rank, rank_t, turn, up_factor, output_gradient, low, made, slots, count,
+            offset, unit,
+        )
+        last = low
+    return made[0], low, made[1]
+
+
+def per_device(
+    plan, tokens, up_weight, first_adapter_factors, second_adapter_factors, counts, output_gradient
+):
+    act_out, low_sum, second_factor_gradient = plan(
+        tokens, up_weight, first_adapter_factors[0], second_adapter_factors[0], counts[0],
+        output_gradient,
+    )
+    low_rank_gradient = (LOWRANK_SCALE * low_sum).astype(jnp.bfloat16)
     grad_a = lax.dot_general(
         low_rank_gradient, tokens, (((0,), (0,)), ((), ())), preferred_element_type=jnp.float32
     )
@@ -91,14 +397,20 @@
         P(("groups", "dp", "fsdp")),
         P(("groups", "dp", "fsdp"), None),
     )
-    return jax.shard_map(
-        per_device,
-        mesh=mesh,
-        in_specs=placed,
-        out_specs=(
-            P(("groups", "dp", "fsdp"), None),
-            P(("groups", "dp", "fsdp"), None, None),
-            P(("groups", "dp", "fsdp"), None, None),
-        ),
-        check_vma=False,
-    )
+
+    def mapped(plan):
+        return jax.shard_map(
+            functools.partial(per_device, plan),
+            mesh=mesh,
+            in_specs=placed,
+            out_specs=(
+                P(("groups", "dp", "fsdp"), None),
+                P(("groups", "dp", "fsdp"), None, None),
+                P(("groups", "dp", "fsdp"), None, None),
+            ),
+            check_vma=False,
+        )
+
+    if mesh.shape["fsdp"] == 4 and mesh.shape["dp"] == 4:
+        return mapped(plane_plan)
+    return mapped(scattered_plan)

time: 341 us -> 237 us (0.70)
  waiting for transfers between devices: 218 us -> 85.8 us
  starting transfers between devices: 3.6 us -> 84.5 us
  blocking collectives: 52.4 us -> 0 us
  Pallas kernels: 0 us -> 21.8 us
  between operations: 14.8 us -> 2.43 us
  matrix products: 30 us -> 23.2 us
  local copies, waits for them, and re-layouts: 19.3 us -> 14.1 us
    reduce_scatter x1 -> x0, waiting for transfers between devices: 157 us -> none  [per_device(): lax.psum_scatter(partial_blocks, 'fsdp', scatter_dimension=0, tiled=True)]
    ppermute x2 -> x50, starting transfers between devices: 3.52 us -> 84.5 us  [the longest x6 33.9 us: start_weight(): return lax.ppermute(after(parts[c], *order), 'fsdp', inward)]
    all_to_all x2 -> x0, blocking collectives: 52.4 us -> none  [the longest x1 31.4 us: per_device(): lax.all_to_all(blocks, 'dp', split_axis=0, concat_axis=1, tiled=True)]
    ppermute x2 -> x50, waiting for transfers between devices: 36.5 us -> 85.8 us  [the longest x7 21.8 us: finish(): return (summed, lax.ppermute(summed[home_total:], 'fsdp', outward))]
    all_gather x1 -> x0, waiting for transfers between devices: 24.7 us -> none  [per_device(): all_rows = lax.all_gather(sliced_rows, 'dp', axis=0, tiled=True)]
    pallas_call x0 -> x4, Pallas kernels: none -> 21.8 us  [tail(): pl.pallas_call(tail_kernel, name='tail', out_shape=(jax.ShapeDtypeStruct(...]
    dynamic_update_slice x2 -> x0, local copies, waits for them, and re-layouts: 11.3 us -> none  [place_block(): placed = lax.dynamic_update_slice_in_dim(padded, block, offset, 0)]
    slice x1 -> x8, local copies, waits for them, and re-layouts: 0.04 us -> 3.92 us  [the longest x1 3.76 us: plane_plan(): rest_weight[:, offsets[c]:offsets[c] + sizes[c] * unit]]
  transfers between devices with their start and end apart: 4 -> 50, of which waited for: 4 -> 16; matrix products, arithmetic and copies ran while one was open for 1% -> 15% of each run, Pallas kernels for 0% -> 8%
where the time goes in v2:
time: 237 us; the launch traced here: 236 us
  waiting for transfers between devices  85.8 us (36%)
  starting transfers between devices  84.5 us (36%)
  matrix products  23.2 us (10%)
  Pallas kernels  21.8 us (9%)
  local copies, waits for them, and re-layouts  14.1 us (6%)
  other arithmetic  3.67 us (2%)
  between operations  2.43 us (1%)
    ppermute x6, starting transfers between devices, start_weight(): return lax.ppermute(after(parts[c], *order), 'fsdp', inward)  33.9 us
    ppermute x7, waiting for transfers between devices, finish(): return (summed, lax.ppermute(summed[home_total:], 'fsdp', outward))  21.8 us
    pallas_call x4, Pallas kernels, tail(): pl.pallas_call(tail_kernel, name='tail', out_shape=(jax.ShapeDtypeStruct(...  21.8 us
    ppermute x6, waiting for transfers between devices, start_weight(): return lax.ppermute(after(parts[c], *order), 'fsdp', inward)  20.6 us
    ppermute x4, waiting for transfers between devices, ordered_pair(): theirs = lax.ppermute(mine, 'dp', across)  15.5 us
    ppermute x4, waiting for transfers between devices, hand_out(): cornered = lax.ppermute(cuts[3], 'dp', diagonal)  12.5 us
    ppermute x7, starting transfers between devices, share_weight(): pieces.append(lax.ppermute(line, 'groups', pairs))  11.6 us
    dot_general x7, matrix products, finish(): summed = jnp.dot(rows, weight, preferred_element_type=jnp.float32)  10.6 us
  transfers between devices with their start and end apart: 50, of which 16 were waited for; matrix products, arithmetic and copies ran while one was open for 15% of the time, Pallas kernels for 8%

profile of v2, /device:TPU:0, one launch (start us, length us, event | category | flops | bytes accessed | tf_op | source)
XLA Modules:
  0.0 235.5 jit_solution(2484497714003550618)
XLA Ops:
  3.2 3.0 %collective-permute-start = (bf16[48,4096]{1,0:T(8,128)(2,1)}, bf16[48,4096]{1,0:T(8,128)(2,1)}, u32[]{:S(2)}, u32[]{:S(2)}) collective-permute-start(bf16[48,4096]{1,0:T(8,128)(2,1)} %slice_select_fusion.1), channel_id=1, source_target_pairs={{0,8},{8,0},{4,12},{12,4},{1,9},{9,1},{5,13},{13,5},{2,10},{10,2},... | collective-permute-start | bytes 1179656 | tf_op jit(solution)/shard_map/ppermute | solution.py:218
  6.2 1.9 constant_dynamic-slice_fusion.6
  8.0 4.3 %collective-permute-start.10 = (bf16[512,512]{1,0:T(8,128)(2,1)}, bf16[512,512]{1,0:T(8,128)(2,1)}, u32[]{:S(2)}, u32[]{:S(2)}) collective-permute-start(bf16[512,512]{1,0:T(8,128)(2,1)} %constant_dynamic-slice_fusion.6), channel_id=1, source_target_pairs={{0,1},{3,2},{4,5},{7,6},{8,9},{11,10},{12,13},{15,14},{16,17},{19,... | collective-permute-start | bytes 1572872 | tf_op jit(solution)/shard_map/ppermute | solution.py:226
  13.1 3.3 %constant_dynamic-slice_fusion.7 = (bf16[512,512]{1,0:T(8,128)(2,1)S(1)}, bf16[512,512]{1,0:T(8,128)(2,1)S(1)}, bf16[512,512]{1,0:T(8,128)(2,1)}, bf16[512,512]{...) fusion(bf16[1024,3584]{1,0:T(8,128)(2,1)} %param.7, s32[]{:T(128)S(6)} %select_n.196), kind=kLoop, calls=%fused_computation.114 | loop fusion | bytes 6291460 | tf_op jit(solution)/shard_map/dynamic_slice | solution.py:221
  17.0 3.8 %fusion.13 = (bf16[1024,512]{1,0:T(8,128)(2,1)S(1)}, bf16[1024,512]{1,0:T(8,128)(2,1)S(1)}, bf16[1024,512]{1,0:T(8,128)(2,1)S(1)}, bf16[1024,512]{1,0:T(8,128)(2...) fusion(bf16[1024,3584]{1,0:T(8,128)(2,1)} %param.7), kind=kLoop, calls=%fused_computation.122 | loop fusion | bytes 14680064 | tf_op jit(solution)/shard_map/slice | solution.py:230
  24.3 1.6 collective-permute-start.5
  28.0 3.1 %collective-permute-start.12 = (bf16[512,512]{1,0:T(8,128)(2,1)S(1)}, bf16[512,512]{1,0:T(8,128)(2,1)S(1)}, u32[]{:S(2)}, u32[]{:S(2)}) collective-permute-start(bf16[512,512]{1,0:T(8,128)(2,1)S(1)} %copy-done.6), channel_id=1, source_target_pairs={{0,1},{3,2},{4,5},{7,6},{8,9},{11,10},{12,13},{15,14},{16,17},{19,... | collective-permute-start | bytes 1572872 | tf_op jit(solution)/shard_map/ppermute | solution.py:253
  33.5 5.9 %collective-permute-done.5 = bf16[80,2048]{1,0:T(8,128)(2,1)S(1)} collective-permute-done((bf16[80,2048]{1,0:T(8,128)(2,1)S(1)}, bf16[80,2048]{1,0:T(8,128)(2,1)S(1)}, u32[]{:S(2)}, u32[]{:S(2)}) %collective-permute-start.5) | collective-permute-done | bytes 327712 | tf_op jit(solution)/shard_map/ppermute | solution.py:274
  39.4 1.5 collective-permute-start.6
  41.1 1.6 collective-permute-start.11
  42.6 5.7 %collective-permute-done.6 = bf16[80,2048]{1,0:T(8,128)(2,1)S(1)} collective-permute-done((bf16[80,2048]{1,0:T(8,128)(2,1)S(1)}, bf16[80,2048]{1,0:T(8,128)(2,1)S(1)}, u32[]{:S(2)}, u32[]{:S(2)}) %collective-permute-start.6) | collective-permute-done | bytes 327712 | tf_op jit(solution)/shard_map/ppermute | solution.py:265
  48.3 1.5 collective-permute-start.4
  49.9 5.5 %collective-permute-done.4 = bf16[80,2048]{1,0:T(8,128)(2,1)S(1)} collective-permute-done((bf16[80,2048]{1,0:T(8,128)(2,1)S(1)}, bf16[80,2048]{1,0:T(8,128)(2,1)S(1)}, u32[]{:S(2)}, u32[]{:S(2)}) %collective-permute-start.4) | collective-permute-done | bytes 327712 | tf_op jit(solution)/shard_map/ppermute | solution.py:265
  55.9 1.6 collective-permute-start.7
  57.6 2.6 %collective-permute-done.15 = bf16[512,512]{1,0:T(8,128)(2,1)S(1)} collective-permute-done((bf16[512,512]{1,0:T(8,128)(2,1)S(1)}, bf16[512,512]{1,0:T(8,128)(2,1)S(1)}, u32[]{:S(2)}, u32[]{:S(2)}) %collective-permute-start.15) | collective-permute-done | bytes 524320 | tf_op jit(solution)/shard_map/ppermute | solution.py:253
  60.3 1.6 collective-permute-start.13
  61.9 4.3 %collective-permute-done.7 = bf16[80,2048]{1,0:T(8,128)(2,1)S(1)} collective-permute-done((bf16[80,2048]{1,0:T(8,128)(2,1)S(1)}, bf16[80,2048]{1,0:T(8,128)(2,1)S(1)}, u32[]{:S(2)}, u32[]{:S(2)}) %collective-permute-start.7) | collective-permute-done | bytes 327712 | tf_op jit(solution)/shard_map/ppermute | solution.py:265
  68.1 1.6 collective-permute-start.16
  69.7 4.2 %collective-permute-done.13 = bf16[512,512]{1,0:T(8,128)(2,1)S(1)} collective-permute-done((bf16[512,512]{1,0:T(8,128)(2,1)S(1)}, bf16[512,512]{1,0:T(8,128)(2,1)S(1)}, u32[]{:S(2)}, u32[]{:S(2)}) %collective-permute-start.13) | collective-permute-done | bytes 524320 | tf_op jit(solution)/shard_map/ppermute | solution.py:261
  74.7 7.6 %collective-permute-start.18 = (bf16[512,512]{1,0:T(8,128)(2,1)S(1)}, bf16[512,512]{1,0:T(8,128)(2,1)S(1)}, u32[]{:S(2)}, u32[]{:S(2)}) collective-permute-start(bf16[512,512]{1,0:T(8,128)(2,1)S(1)} %copy-done.4), channel_id=1, source_target_pairs={{0,1},{3,2},{4,5},{7,6},{8,9},{11,10},{12,13},{15,14},{16,17},{19,... | collective-permute-start | bytes 1572872 | tf_op jit(solution)/shard_map/ppermute | solution.py:253
  84.6 4.6 %collective-permute-done.18 = bf16[512,512]{1,0:T(8,128)(2,1)S(1)} collective-permute-done((bf16[512,512]{1,0:T(8,128)(2,1)S(1)}, bf16[512,512]{1,0:T(8,128)(2,1)S(1)}, u32[]{:S(2)}, u32[]{:S(2)}) %collective-permute-start.18) | collective-permute-done | bytes 524320 | tf_op jit(solution)/shard_map/ppermute | solution.py:253
  89.4 1.5 fusion
  90.9 1.6 collective-permute-start.19
  94.0 1.5 fusion.1
  98.9 16.0 %collective-permute-start.27 = (bf16[512,512]{1,0:T(8,128)(2,1)S(1)}, bf16[512,512]{1,0:T(8,128)(2,1)S(1)}, u32[]{:S(2)}, u32[]{:S(2)}) collective-permute-start(bf16[512,512]{1,0:T(8,128)(2,1)S(1)} %copy-done.3), channel_id=1, source_target_pairs={{0,1},{3,2},{4,5},{7,6},{8,9},{11,10},{12,13},{15,14},{16,17},{19,... | collective-permute-start | bytes 1572872 | tf_op jit(solution)/shard_map/ppermute | solution.py:253
  116.5 1.5 convolution_convert_fusion.4
  118.0 8.6 %collective-permute-done.27 = bf16[512,512]{1,0:T(8,128)(2,1)S(1)} collective-permute-done((bf16[512,512]{1,0:T(8,128)(2,1)S(1)}, bf16[512,512]{1,0:T(8,128)(2,1)S(1)}, u32[]{:S(2)}, u32[]{:S(2)}) %collective-permute-start.27) | collective-permute-done | bytes 524320 | tf_op jit(solution)/shard_map/ppermute | solution.py:253
  127.3 4.9 %collective-permute-done.30 = bf16[512,512]{1,0:T(8,128)(2,1)S(1)} collective-permute-done((bf16[512,512]{1,0:T(8,128)(2,1)S(1)}, bf16[512,512]{1,0:T(8,128)(2,1)S(1)}, u32[]{:S(2)}, u32[]{:S(2)}) %collective-permute-start.30) | collective-permute-done | bytes 524320 | tf_op jit(solution)/shard_map/ppermute | solution.py:253
  133.7 1.5 fusion.2
  135.6 1.6 collective-permute-start.25
  137.5 4.8 %collective-permute-done.28 = bf16[512,512]{1,0:T(8,128)(2,1)S(1)} collective-permute-done((bf16[512,512]{1,0:T(8,128)(2,1)S(1)}, bf16[512,512]{1,0:T(8,128)(2,1)S(1)}, u32[]{:S(2)}, u32[]{:S(2)}) %collective-permute-start.28) | collective-permute-done | bytes 524320 | tf_op jit(solution)/shard_map/ppermute | solution.py:261
  142.3 2.4 %collective-permute-start.31 = (bf16[512,512]{1,0:T(8,128)(2,1)S(1)}, bf16[512,512]{1,0:T(8,128)(2,1)S(1)}, u32[]{:S(2)}, u32[]{:S(2)}) collective-permute-start(bf16[512,512]{1,0:T(8,128)(2,1)S(1)} %collective-permute-done.30), channel_id=1, source_target_pairs={{0,16},{16,0},{1,17},{17,1},{2,18},{18,2},{3,19},{19,3},{4,20},{20... | collective-permute-start | bytes 1572872 | tf_op jit(solution)/shard_map/ppermute | solution.py:261
  146.3 4.4 %collective-permute-start.37 = (bf16[512,512]{1,0:T(8,128)(2,1)S(1)}, bf16[512,512]{1,0:T(8,128)(2,1)S(1)}, u32[]{:S(2)}, u32[]{:S(2)}) collective-permute-start(bf16[512,512]{1,0:T(8,128)(2,1)S(1)} %get-tuple-element.106), channel_id=1, source_target_pairs={{0,1},{3,2},{4,5},{7,6},{8,9},{11,10},{12,13},{15,14},{16,17},{19,... | collective-permute-start | bytes 1572872 | tf_op jit(solution)/shard_map/ppermute | solution.py:253
  150.7 1.5 fusion.3
  154.8 6.1 %tail.4 = (bf16[128,14336]{1,0:T(8,128)(2,1)}, f32[32,14336]{1,0:T(8,128)}, f32[128,32]{1,0:T(8,128)S(1)}) custom-call(s32[4]{0:T(128)S(1)} %xor_multiply_fusion.slots_ref, s32[1]{0:T(128)} %copy.49.counts_ref, bf16[128,1024]{1,0:T(8,128)(2,1)S(1)} %get-tuple-element.159.own_ref, bf16[128,1024]{1,0:T(8,128)(2,1)S(1)} %collective-permute-done.24.beside_ref, ...), custom_call_target="tpu_custom_call" | custom-call | flops 234881024 | bytes 4194304 | tf_op jit(solution)/shard_map/tail/pallas_call | solution.py:146
  164.4 1.5 collective-permute-start.38
  166.0 1.5 fusion.4
  167.5 8.8 %collective-permute-done.33 = bf16[320,512]{1,0:T(8,128)(2,1)S(1)} collective-permute-done((bf16[320,512]{1,0:T(8,128)(2,1)S(1)}, bf16[320,512]{1,0:T(8,128)(2,1)S(1)}, u32[]{:S(2)}, u32[]{:S(2)}) %collective-permute-start.33) | collective-permute-done | bytes 327712 | tf_op jit(solution)/shard_map/ppermute | solution.py:319
  179.0 1.6 collective-permute-start.35
  182.2 1.5 fusion.5
  183.7 9.1 %collective-permute-done.36.diagonal_ref = bf16[128,1024]{1,0:T(8,128)(2,1)S(1)} collective-permute-done((bf16[128,1024]{1,0:T(8,128)(2,1)S(1)}, bf16[128,1024]{1,0:T(8,128)(2,1)S(1)}, u32[]{:S(2)}, u32[]{:S(2)}) %collective-permute-start.36) | collective-permute-done | bytes 262176 | tf_op jit(solution)/shard_map/ppermute | solution.py:335
  194.1 6.1 %tail.5 = (bf16[128,14336]{1,0:T(8,128)(2,1)}, f32[32,14336]{1,0:T(8,128)}, f32[128,32]{1,0:T(8,128)S(1)}) custom-call(s32[4]{0:T(128)S(1)} %xor_multiply_fusion.slots_ref, s32[1]{0:T(128)} %copy.49.counts_ref, bf16[128,1024]{1,0:T(8,128)(2,1)S(1)} %get-tuple-element.155.own_ref, ...), custom_call_target="tpu_custom_call", output_to_operand_aliasing={{0}: (12, {}), {1}: (13, {})} | custom-call | flops 234881024 | bytes 4194304 | tf_op jit(solution)/shard_map/tail/pallas_call | solution.py:146
  203.1 6.1 %collective-permute-done.43 = bf16[320,512]{1,0:T(8,128)(2,1)S(1)} collective-permute-done((bf16[320,512]{1,0:T(8,128)(2,1)S(1)}, bf16[320,512]{1,0:T(8,128)(2,1)S(1)}, u32[]{:S(2)}, u32[]{:S(2)}) %collective-permute-start.43) | collective-permute-done | bytes 327712 | tf_op jit(solution)/shard_map/ppermute | solution.py:319
  209.5 1.6 collective-permute-start.48
  211.4 6.9 %collective-permute-done.41 = bf16[320,512]{1,0:T(8,128)(2,1)S(1)} collective-permute-done((bf16[320,512]{1,0:T(8,128)(2,1)S(1)}, bf16[320,512]{1,0:T(8,128)(2,1)S(1)}, u32[]{:S(2)}, u32[]{:S(2)}) %collective-permute-start.41) | collective-permute-done | bytes 327712 | tf_op jit(solution)/shard_map/ppermute | solution.py:319
  220.1 3.4 %collective-permute-done.49.diagonal_ref = bf16[128,1024]{1,0:T(8,128)(2,1)S(1)} collective-permute-done((bf16[128,1024]{1,0:T(8,128)(2,1)S(1)}, bf16[128,1024]{1,0:T(8,128)(2,1)S(1)}, u32[]{:S(2)}, u32[]{:S(2)}) %collective-permute-start.49) | collective-permute-done | bytes 262176 | tf_op jit(solution)/shard_map/ppermute | solution.py:335
  224.9 6.1 %tail.6 = (bf16[128,14336]{1,0:T(8,128)(2,1)}, f32[32,14336]{1,0:T(8,128)}, f32[128,32]{1,0:T(8,128)S(1)}) custom-call(s32[4]{0:T(128)S(1)} %xor_multiply_fusion.slots_ref, s32[1]{0:T(128)} %copy.49.counts_ref, bf16[128,1024]{1,0:T(8,128)(2,1)S(1)} %get-tuple-element.151.own_ref, ...), custom_call_target="tpu_custom_call", output_to_operand_aliasing={{0}: (12, {}), {1}: (13, {})} | custom-call | flops 234881024 | bytes 4194304 | tf_op jit(solution)/shard_map/tail/pallas_call | solution.py:146
  231.0 3.4 %tail.7 = (bf16[128,14336]{1,0:T(8,128)(2,1)}, f32[32,14336]{1,0:T(8,128)}, f32[128,32]{1,0:T(8,128)S(1)}) custom-call(s32[4]{0:T(128)S(1)} %xor_multiply_fusion.slots_ref, s32[1]{0:T(128)} %copy.49.counts_ref, bf16[128,512]{1,0:T(8,128)(2,1)S(1)} %get-tuple-element.173.own_ref, ...), custom_call_target="tpu_custom_call", output_to_operand_aliasing={{0}: (12, {}), {1}: (13, {})} | custom-call | flops 117440512 | bytes 2097152 | tf_op jit(solution)/shard_map/tail/pallas_call | solution.py:146
  (161 shorter events, 46.8 us)
Async XLA Ops:
  3.2 17.7 %collective-permute-start = (bf16[48,4096]{1,0:T(8,128)(2,1)}, bf16[48,4096]{1,0:T(8,128)(2,1)}, u32[]{:S(2)}, u32[]{:S(2)}) collective-permute-start(bf16[48,4096]{1,0:T(8,128)(2,1)} %slice_select_fusion.1), channel_id=1, source_target_pairs={{0,8},{8,0},{4,12},{12,4},{1,9},{9,1},{5,13},{13,5},{2,10},{10,2},... | collective-permute-start | bytes 1179656 | tf_op jit(solution)/shard_map/ppermute | solution.py:218
  8.0 19.1 %collective-permute-start.10 = (bf16[512,512]{1,0:T(8,128)(2,1)}, bf16[512,512]{1,0:T(8,128)(2,1)}, u32[]{:S(2)}, u32[]{:S(2)}) collective-permute-start(bf16[512,512]{1,0:T(8,128)(2,1)} %constant_dynamic-slice_fusion.6), channel_id=1, source_target_pairs={{0,1},{3,2},{4,5},{7,6},{8,9},{11,10},{12,13},{15,14},{16,17},{19,... | collective-permute-start | bytes 1572872 | tf_op jit(solution)/shard_map/ppermute | solution.py:226
  22.4 9.8 %collective-permute-start.1 = (bf16[80,2048]{1,0:T(8,128)(2,1)S(1)}, bf16[80,2048]{1,0:T(8,128)(2,1)S(1)}, u32[]{:S(2)}, u32[]{:S(2)}) collective-permute-start(bf16[80,2048]{1,0:T(8,128)(2,1)S(1)} %pad_maximum_fusion.5), channel_id=1, source_target_pairs={{0,8},{8,0},{4,12},{12,4},{1,9},{9,1},{5,13},{13,5},{2,10},{10,2},... | collective-permute-start | bytes 983048 | tf_op jit(solution)/shard_map/ppermute | solution.py:265
  23.0 32.9 %collective-permute-start.2 = (bf16[80,2048]{1,0:T(8,128)(2,1)S(1)}, bf16[80,2048]{1,0:T(8,128)(2,1)S(1)}, u32[]{:S(2)}, u32[]{:S(2)}) collective-permute-start(bf16[80,2048]{1,0:T(8,128)(2,1)S(1)} %pad_maximum_fusion.5), channel_id=1, source_target_pairs={{0,1},{3,2},{4,5},{7,6},{8,9},{11,10},{12,13},{15,14},{16,17},{19,... | collective-permute-start | bytes 983048 | tf_op jit(solution)/shard_map/ppermute | solution.py:273
  24.3 15.1 %collective-permute-start.5 = (bf16[80,2048]{1,0:T(8,128)(2,1)S(1)}, bf16[80,2048]{1,0:T(8,128)(2,1)S(1)}, u32[]{:S(2)}, u32[]{:S(2)}) collective-permute-start(bf16[80,2048]{1,0:T(8,128)(2,1)S(1)} %pad_maximum_fusion.6), channel_id=1, source_target_pairs={{0,2},{3,1},{4,6},{7,5},{8,10},{11,9},{12,14},{15,13},{16,18},{19,... | collective-permute-start | bytes 983048 | tf_op jit(solution)/shard_map/ppermute | solution.py:274
  25.9 15.2 %collective-permute-start.3 = (bf16[80,2048]{1,0:T(8,128)(2,1)S(1)}, bf16[80,2048]{1,0:T(8,128)(2,1)S(1)}, u32[]{:S(2)}, u32[]{:S(2)}) collective-permute-start(bf16[80,2048]{1,0:T(8,128)(2,1)S(1)} %pad_maximum_fusion.6), channel_id=1, source_target_pairs={{1,2},{2,1},{5,6},{6,5},{9,10},{10,9},{13,14},{14,13},{17,18},{18,... | collective-permute-start | bytes 983048 | tf_op jit(solution)/shard_map/ppermute | solution.py:271
  28.0 29.5 %collective-permute-start.12 = (bf16[512,512]{1,0:T(8,128)(2,1)S(1)}, bf16[512,512]{1,0:T(8,128)(2,1)S(1)}, u32[]{:S(2)}, u32[]{:S(2)}) collective-permute-start(bf16[512,512]{1,0:T(8,128)(2,1)S(1)} %copy-done.6), channel_id=1, source_target_pairs={{0,1},{3,2},{4,5},{7,6},{8,9},{11,10},{12,13},{15,14},{16,17},{19,... | collective-permute-start | bytes 1572872 | tf_op jit(solution)/shard_map/ppermute | solution.py:253
  32.2 28.0 %collective-permute-start.15 = (bf16[512,512]{1,0:T(8,128)(2,1)S(1)}, bf16[512,512]{1,0:T(8,128)(2,1)S(1)}, u32[]{:S(2)}, u32[]{:S(2)}) collective-permute-start(bf16[512,512]{1,0:T(8,128)(2,1)S(1)} %copy-done.5), channel_id=1, source_target_pairs={{0,1},{3,2},{4,5},{7,6},{8,9},{11,10},{12,13},{15,14},{16,17},{19,... | collective-permute-start | bytes 1572872 | tf_op jit(solution)/shard_map/ppermute | solution.py:253
  39.4 8.9 %collective-permute-start.6 = (bf16[80,2048]{1,0:T(8,128)(2,1)S(1)}, bf16[80,2048]{1,0:T(8,128)(2,1)S(1)}, u32[]{:S(2)}, u32[]{:S(2)}) collective-permute-start(bf16[80,2048]{1,0:T(8,128)(2,1)S(1)} %collective-permute-done.5), channel_id=1, source_target_pairs={{0,8},{8,0},{4,12},{12,4},{1,9},{9,1},{5,13},{13,5},{2,10},{10,2},... | collective-permute-start | bytes 983048 | tf_op jit(solution)/shard_map/ppermute | solution.py:265
  41.1 19.2 %collective-permute-start.11 = (bf16[512,512]{1,0:T(8,128)(2,1)}, bf16[512,512]{1,0:T(8,128)(2,1)S(1)}, u32[]{:S(2)}, u32[]{:S(2)}) collective-permute-start(bf16[512,512]{1,0:T(8,128)(2,1)} %collective-permute-done.10), channel_id=1, source_target_pairs={{0,16},{16,0},{1,17},{17,1},{2,18},{18,2},{3,19},{19,3},{4,20},{20... | collective-permute-start | bytes 1572872 | tf_op jit(solution)/shard_map/ppermute | solution.py:261
  55.8 10.6 %collective-permute-start.8 = (bf16[320,2048]{1,0:T(8,128)(2,1)S(1)}, bf16[320,2048]{1,0:T(8,128)(2,1)S(1)}, u32[]{:S(2)}, u32[]{:S(2)}) collective-permute-start(bf16[320,2048]{1,0:T(8,128)(2,1)S(1)} %pad_maximum_fusion), channel_id=1, source_target_pairs={{0,4},{4,0},{8,12},{12,8},{1,5},{5,1},{9,13},{13,9},{2,6},{6,2},{1... | collective-permute-start | bytes 3932168 | tf_op jit(solution)/shard_map/ppermute | solution.py:282
  55.9 10.2 %collective-permute-start.7 = (bf16[80,2048]{1,0:T(8,128)(2,1)S(1)}, bf16[80,2048]{1,0:T(8,128)(2,1)S(1)}, u32[]{:S(2)}, u32[]{:S(2)}) collective-permute-start(bf16[80,2048]{1,0:T(8,128)(2,1)S(1)} %collective-permute-done.2), channel_id=1, source_target_pairs={{0,8},{8,0},{4,12},{12,4},{1,9},{9,1},{5,13},{13,5},{2,10},{10,2},... | collective-permute-start | bytes 983048 | tf_op jit(solution)/shard_map/ppermute | solution.py:265
  60.3 13.6 %collective-permute-start.13 = (bf16[512,512]{1,0:T(8,128)(2,1)S(1)}, bf16[512,512]{1,0:T(8,128)(2,1)S(1)}, u32[]{:S(2)}, u32[]{:S(2)}) collective-permute-start(bf16[512,512]{1,0:T(8,128)(2,1)S(1)} %collective-permute-done.12), channel_id=1, source_target_pairs={{0,16},{16,0},{1,17},{17,1},{2,18},{18,2},{3,19},{19,3},{4,20},{20... | collective-permute-start | bytes 1572872 | tf_op jit(solution)/shard_map/ppermute | solution.py:261
  66.5 22.7 %collective-permute-start.9 = (bf16[320,2048]{1,0:T(8,128)(2,1)S(1)}, bf16[320,2048]{1,0:T(8,128)(2,1)S(1)}, u32[]{:S(2)}, u32[]{:S(2)}) collective-permute-start(bf16[320,2048]{1,0:T(8,128)(2,1)S(1)} %pad_maximum_fusion.1), channel_id=1, source_target_pairs={{0,4},{4,0},{8,12},{12,8},{1,5},{5,1},{9,13},{13,9},{2,6},{6,2},{1... | collective-permute-start | bytes 3932168 | tf_op jit(solution)/shard_map/ppermute | solution.py:290
  68.1 16.4 %collective-permute-start.16 = (bf16[512,512]{1,0:T(8,128)(2,1)S(1)}, bf16[512,512]{1,0:T(8,128)(2,1)S(1)}, u32[]{:S(2)}, u32[]{:S(2)}) collective-permute-start(bf16[512,512]{1,0:T(8,128)(2,1)S(1)} %collective-permute-done.15), channel_id=1, source_target_pairs={{0,16},{16,0},{1,17},{17,1},{2,18},{18,2},{3,19},{19,3},{4,20},{20... | collective-permute-start | bytes 1572872 | tf_op jit(solution)/shard_map/ppermute | solution.py:261
  74.0 15.4 %collective-permute-start.14 = (bf16[640,512]{1,0:T(8,128)(2,1)S(1)}, bf16[640,512]{1,0:T(8,128)(2,1)S(1)}, u32[]{:S(2)}, u32[]{:S(2)}) collective-permute-start(bf16[640,512]{1,0:T(8,128)(2,1)S(1)} %convolution_convert_fusion.7), channel_id=1, source_target_pairs={{1,2},{2,1},{5,6},{6,5},{9,10},{10,9},{13,14},{14,13},{17,18},{18,... | collective-permute-start | bytes 1966088 | tf_op jit(solution)/shard_map/ppermute | solution.py:305
  74.7 14.4 %collective-permute-start.18 = (bf16[512,512]{1,0:T(8,128)(2,1)S(1)}, bf16[512,512]{1,0:T(8,128)(2,1)S(1)}, u32[]{:S(2)}, u32[]{:S(2)}) collective-permute-start(bf16[512,512]{1,0:T(8,128)(2,1)S(1)} %copy-done.4), channel_id=1, source_target_pairs={{0,1},{3,2},{4,5},{7,6},{8,9},{11,10},{12,13},{15,14},{16,17},{19,... | collective-permute-start | bytes 1572872 | tf_op jit(solution)/shard_map/ppermute | solution.py:253
  83.8 10.2 %collective-permute-start.17 = (bf16[640,512]{1,0:T(8,128)(2,1)S(1)}, bf16[640,512]{1,0:T(8,128)(2,1)S(1)}, u32[]{:S(2)}, u32[]{:S(2)}) collective-permute-start(bf16[640,512]{1,0:T(8,128)(2,1)S(1)} %convolution_convert_fusion.6), channel_id=1, source_target_pairs={{1,2},{2,1},{5,6},{6,5},{9,10},{10,9},{13,14},{14,13},{17,18},{18,... | collective-permute-start | bytes 1966088 | tf_op jit(solution)/shard_map/ppermute | solution.py:305
  90.9 24.0 %collective-permute-start.19 = (bf16[512,512]{1,0:T(8,128)(2,1)S(1)}, bf16[512,512]{1,0:T(8,128)(2,1)S(1)}, u32[]{:S(2)}, u32[]{:S(2)}) collective-permute-start(bf16[512,512]{1,0:T(8,128)(2,1)S(1)} %collective-permute-done.18), channel_id=1, source_target_pairs={{0,16},{16,0},{1,17},{17,1},{2,18},{18,2},{3,19},{19,3},{4,20},{20... | collective-permute-start | bytes 1572872 | tf_op jit(solution)/shard_map/ppermute | solution.py:261
  95.6 38.1 %collective-permute-start.20 = (bf16[640,512]{1,0:T(8,128)(2,1)S(1)}, bf16[640,512]{1,0:T(8,128)(2,1)S(1)}, u32[]{:S(2)}, u32[]{:S(2)}) collective-permute-start(bf16[640,512]{1,0:T(8,128)(2,1)S(1)} %convolution_convert_fusion.5), channel_id=1, source_target_pairs={{1,2},{2,1},{5,6},{6,5},{9,10},{10,9},{13,14},{14,13},{17,18},{18,... | collective-permute-start | bytes 1966088 | tf_op jit(solution)/shard_map/ppermute | solution.py:305
  96.3 38.9 %collective-permute-start.23 = (bf16[320,512]{1,0:T(8,128)(2,1)S(1)}, bf16[320,512]{1,0:T(8,128)(2,1)S(1)}, u32[]{:S(2)}, u32[]{:S(2)}) collective-permute-start(bf16[320,512]{1,0:T(8,128)(2,1)S(1)} %slice.127), channel_id=1, source_target_pairs={{1,0},{2,3},{5,4},{6,7},{9,8},{10,11},{13,12},{14,15},{17,16},{18,... | collective-permute-start | bytes 983048 | tf_op jit(solution)/shard_map/ppermute | solution.py:319
  97.6 37.7 %collective-permute-start.22 = (bf16[320,512]{1,0:T(8,128)(2,1)S(1)}, bf16[320,512]{1,0:T(8,128)(2,1)S(1)}, u32[]{:S(2)}, u32[]{:S(2)}) collective-permute-start(bf16[320,512]{1,0:T(8,128)(2,1)S(1)} %slice.125), channel_id=1, source_target_pairs={{1,0},{2,3},{5,4},{6,7},{9,8},{10,11},{13,12},{14,15},{17,16},{18,... | collective-permute-start | bytes 983048 | tf_op jit(solution)/shard_map/ppermute | solution.py:319
  98.9 27.7 %collective-permute-start.27 = (bf16[512,512]{1,0:T(8,128)(2,1)S(1)}, bf16[512,512]{1,0:T(8,128)(2,1)S(1)}, u32[]{:S(2)}, u32[]{:S(2)}) collective-permute-start(bf16[512,512]{1,0:T(8,128)(2,1)S(1)} %copy-done.3), channel_id=1, source_target_pairs={{0,1},{3,2},{4,5},{7,6},{8,9},{11,10},{12,13},{15,14},{16,17},{19,... | collective-permute-start | bytes 1572872 | tf_op jit(solution)/shard_map/ppermute | solution.py:253
  114.9 17.3 %collective-permute-start.30 = (bf16[512,512]{1,0:T(8,128)(2,1)S(1)}, bf16[512,512]{1,0:T(8,128)(2,1)S(1)}, u32[]{:S(2)}, u32[]{:S(2)}) collective-permute-start(bf16[512,512]{1,0:T(8,128)(2,1)S(1)} %get-tuple-element.99), channel_id=1, source_target_pairs={{0,1},{3,2},{4,5},{7,6},{8,9},{11,10},{12,13},{15,14},{16,17},{19,... | collective-permute-start | bytes 1572872 | tf_op jit(solution)/shard_map/ppermute | solution.py:253
  126.6 19.7 %collective-permute-start.29 = (bf16[640,512]{1,0:T(8,128)(2,1)S(1)}, bf16[640,512]{1,0:T(8,128)(2,1)S(1)}, u32[]{:S(2)}, u32[]{:S(2)}) collective-permute-start(bf16[640,512]{1,0:T(8,128)(2,1)S(1)} %convolution_convert_fusion.4), channel_id=1, source_target_pairs={{1,2},{2,1},{5,6},{6,5},{9,10},{10,9},{13,14},{14,13},{17,18},{18,... | collective-permute-start | bytes 1966088 | tf_op jit(solution)/shard_map/ppermute | solution.py:305
  132.2 10.1 %collective-permute-start.28 = (bf16[512,512]{1,0:T(8,128)(2,1)S(1)}, bf16[512,512]{1,0:T(8,128)(2,1)S(1)}, u32[]{:S(2)}, u32[]{:S(2)}) collective-permute-start(bf16[512,512]{1,0:T(8,128)(2,1)S(1)} %collective-permute-done.27), channel_id=1, source_target_pairs={{0,16},{16,0},{1,17},{17,1},{2,18},{18,2},{3,19},{19,3},{4,20},{20... | collective-permute-start | bytes 1572872 | tf_op jit(solution)/shard_map/ppermute | solution.py:261
  135.6 19.1 %collective-permute-start.24 = (bf16[128,1024]{1,0:T(8,128)(2,1)S(1)}, bf16[128,1024]{1,0:T(8,128)(2,1)S(1)}, u32[]{:S(2)}, u32[]{:S(2)}) collective-permute-start(bf16[128,1024]{1,0:T(8,128)(2,1)S(1)} %get-tuple-element.158), channel_id=1, source_target_pairs={{0,4},{4,0},{8,12},{12,8},{1,5},{5,1},{9,13},{13,9},{2,6},{6,2},{1... | collective-permute-start | bytes 786440 | tf_op jit(solution)/shard_map/ppermute | solution.py:336
  135.6 19.1 %collective-permute-start.25 = (bf16[128,1024]{1,0:T(8,128)(2,1)S(1)}, bf16[128,1024]{1,0:T(8,128)(2,1)S(1)}, u32[]{:S(2)}, u32[]{:S(2)}) collective-permute-start(bf16[128,1024]{1,0:T(8,128)(2,1)S(1)} %get-tuple-element.157), channel_id=1, source_target_pairs={{0,8},{8,0},{4,12},{12,4},{1,9},{9,1},{5,13},{13,5},{2,10},{10,2},... | collective-permute-start | bytes 786440 | tf_op jit(solution)/shard_map/ppermute | solution.py:334
  137.2 16.2 %collective-permute-start.26 = (bf16[128,1024]{1,0:T(8,128)(2,1)S(1)}, bf16[128,1024]{1,0:T(8,128)(2,1)S(1)}, u32[]{:S(2)}, u32[]{:S(2)}) collective-permute-start(bf16[128,1024]{1,0:T(8,128)(2,1)S(1)} %get-tuple-element.156), channel_id=1, source_target_pairs={{0,12},{12,0},{4,8},{8,4},{1,13},{13,1},{5,9},{9,5},{2,14},{14,2},... | collective-permute-start | bytes 786440 | tf_op jit(solution)/shard_map/ppermute | solution.py:335
  142.3 10.3 %collective-permute-start.31 = (bf16[512,512]{1,0:T(8,128)(2,1)S(1)}, bf16[512,512]{1,0:T(8,128)(2,1)S(1)}, u32[]{:S(2)}, u32[]{:S(2)}) collective-permute-start(bf16[512,512]{1,0:T(8,128)(2,1)S(1)} %collective-permute-done.30), channel_id=1, source_target_pairs={{0,16},{16,0},{1,17},{17,1},{2,18},{18,2},{3,19},{19,3},{4,20},{20... | collective-permute-start | bytes 1572872 | tf_op jit(solution)/shard_map/ppermute | solution.py:261
  146.3 18.1 %collective-permute-start.37 = (bf16[512,512]{1,0:T(8,128)(2,1)S(1)}, bf16[512,512]{1,0:T(8,128)(2,1)S(1)}, u32[]{:S(2)}, u32[]{:S(2)}) collective-permute-start(bf16[512,512]{1,0:T(8,128)(2,1)S(1)} %get-tuple-element.106), channel_id=1, source_target_pairs={{0,1},{3,2},{4,5},{7,6},{8,9},{11,10},{12,13},{15,14},{16,17},{19,... | collective-permute-start | bytes 1572872 | tf_op jit(solution)/shard_map/ppermute | solution.py:253
  152.6 13.3 %collective-permute-start.32 = (bf16[640,512]{1,0:T(8,128)(2,1)S(1)}, bf16[640,512]{1,0:T(8,128)(2,1)S(1)}, u32[]{:S(2)}, u32[]{:S(2)}) collective-permute-start(bf16[640,512]{1,0:T(8,128)(2,1)S(1)} %convolution_convert_fusion.3), channel_id=1, source_target_pairs={{1,2},{2,1},{5,6},{6,5},{9,10},{10,9},{13,14},{14,13},{17,18},{18,... | collective-permute-start | bytes 1966088 | tf_op jit(solution)/shard_map/ppermute | solution.py:305
  153.4 23.0 %collective-permute-start.21 = (bf16[320,512]{1,0:T(8,128)(2,1)S(1)}, bf16[320,512]{1,0:T(8,128)(2,1)S(1)}, u32[]{:S(2)}, u32[]{:S(2)}) collective-permute-start(bf16[320,512]{1,0:T(8,128)(2,1)S(1)} %slice.123), channel_id=1, source_target_pairs={{1,0},{2,3},{5,4},{6,7},{9,8},{10,11},{13,12},{14,15},{17,16},{18,... | collective-permute-start | bytes 983048 | tf_op jit(solution)/shard_map/ppermute | solution.py:319
  162.4 18.5 %collective-permute-start.39 = (bf16[640,512]{1,0:T(8,128)(2,1)S(1)}, bf16[640,512]{1,0:T(8,128)(2,1)S(1)}, u32[]{:S(2)}, u32[]{:S(2)}) collective-permute-start(bf16[640,512]{1,0:T(8,128)(2,1)S(1)} %convolution_convert_fusion.2), channel_id=1, source_target_pairs={{1,2},{2,1},{5,6},{6,5},{9,10},{10,9},{13,14},{14,13},{17,18},{18,... | collective-permute-start | bytes 1966088 | tf_op jit(solution)/shard_map/ppermute | solution.py:305
  163.1 13.3 %collective-permute-start.33 = (bf16[320,512]{1,0:T(8,128)(2,1)S(1)}, bf16[320,512]{1,0:T(8,128)(2,1)S(1)}, u32[]{:S(2)}, u32[]{:S(2)}) collective-permute-start(bf16[320,512]{1,0:T(8,128)(2,1)S(1)} %slice.129), channel_id=1, source_target_pairs={{1,0},{2,3},{5,4},{6,7},{9,8},{10,11},{13,12},{14,15},{17,16},{18,... | collective-permute-start | bytes 983048 | tf_op jit(solution)/shard_map/ppermute | solution.py:319
  164.4 12.2 %collective-permute-start.38 = (bf16[512,512]{1,0:T(8,128)(2,1)S(1)}, bf16[512,512]{1,0:T(8,128)(2,1)S(1)}, u32[]{:S(2)}, u32[]{:S(2)}) collective-permute-start(bf16[512,512]{1,0:T(8,128)(2,1)S(1)} %collective-permute-done.37), channel_id=1, source_target_pairs={{0,16},{16,0},{1,17},{17,1},{2,18},{18,2},{3,19},{19,3},{4,20},{20... | collective-permute-start | bytes 1572872 | tf_op jit(solution)/shard_map/ppermute | solution.py:261
  178.2 22.0 %collective-permute-start.40 = (bf16[640,512]{1,0:T(8,128)(2,1)S(1)}, bf16[640,512]{1,0:T(8,128)(2,1)S(1)}, u32[]{:S(2)}, u32[]{:S(2)}) collective-permute-start(bf16[640,512]{1,0:T(8,128)(2,1)S(1)} %convolution_convert_fusion.1), channel_id=1, source_target_pairs={{1,2},{2,1},{5,6},{6,5},{9,10},{10,9},{13,14},{14,13},{17,18},{18,... | collective-permute-start | bytes 1966088 | tf_op jit(solution)/shard_map/ppermute | solution.py:305
  178.9 15.2 %collective-permute-start.34 = (bf16[128,1024]{1,0:T(8,128)(2,1)S(1)}, bf16[128,1024]{1,0:T(8,128)(2,1)S(1)}, u32[]{:S(2)}, u32[]{:S(2)}) collective-permute-start(bf16[128,1024]{1,0:T(8,128)(2,1)S(1)} %get-tuple-element.154), channel_id=1, source_target_pairs={{0,4},{4,0},{8,12},{12,8},{1,5},{5,1},{9,13},{13,9},{2,6},{6,2},{1... | collective-permute-start | bytes 786440 | tf_op jit(solution)/shard_map/ppermute | solution.py:336
  179.0 15.1 %collective-permute-start.35 = (bf16[128,1024]{1,0:T(8,128)(2,1)S(1)}, bf16[128,1024]{1,0:T(8,128)(2,1)S(1)}, u32[]{:S(2)}, u32[]{:S(2)}) collective-permute-start(bf16[128,1024]{1,0:T(8,128)(2,1)S(1)} %get-tuple-element.153), channel_id=1, source_target_pairs={{0,8},{8,0},{4,12},{12,4},{1,9},{9,1},{5,13},{13,5},{2,10},{10,2},... | collective-permute-start | bytes 786440 | tf_op jit(solution)/shard_map/ppermute | solution.py:334
  180.7 12.2 %collective-permute-start.36 = (bf16[128,1024]{1,0:T(8,128)(2,1)S(1)}, bf16[128,1024]{1,0:T(8,128)(2,1)S(1)}, u32[]{:S(2)}, u32[]{:S(2)}) collective-permute-start(bf16[128,1024]{1,0:T(8,128)(2,1)S(1)} %get-tuple-element.152), channel_id=1, source_target_pairs={{0,12},{12,0},{4,8},{8,4},{1,13},{13,1},{5,9},{9,5},{2,14},{14,2},... | collective-permute-start | bytes 786440 | tf_op jit(solution)/shard_map/ppermute | solution.py:335
  180.9 28.3 %collective-permute-start.42 = (bf16[320,512]{1,0:T(8,128)(2,1)S(1)}, bf16[320,512]{1,0:T(8,128)(2,1)S(1)}, u32[]{:S(2)}, u32[]{:S(2)}) collective-permute-start(bf16[320,512]{1,0:T(8,128)(2,1)S(1)} %slice.133), channel_id=1, source_target_pairs={{1,0},{2,3},{5,4},{6,7},{9,8},{10,11},{13,12},{14,15},{17,16},{18,... | collective-permute-start | bytes 983048 | tf_op jit(solution)/shard_map/ppermute | solution.py:319
  192.8 16.4 %collective-permute-start.43 = (bf16[320,512]{1,0:T(8,128)(2,1)S(1)}, bf16[320,512]{1,0:T(8,128)(2,1)S(1)}, u32[]{:S(2)}, u32[]{:S(2)}) collective-permute-start(bf16[320,512]{1,0:T(8,128)(2,1)S(1)} %slice.135), channel_id=1, source_target_pairs={{1,0},{2,3},{5,4},{6,7},{9,8},{10,11},{13,12},{14,15},{17,16},{18,... | collective-permute-start | bytes 983048 | tf_op jit(solution)/shard_map/ppermute | solution.py:319
  201.8 16.4 %collective-permute-start.41 = (bf16[320,512]{1,0:T(8,128)(2,1)S(1)}, bf16[320,512]{1,0:T(8,128)(2,1)S(1)}, u32[]{:S(2)}, u32[]{:S(2)}) collective-permute-start(bf16[320,512]{1,0:T(8,128)(2,1)S(1)} %slice.131), channel_id=1, source_target_pairs={{1,0},{2,3},{5,4},{6,7},{9,8},{10,11},{13,12},{14,15},{17,16},{18,... | collective-permute-start | bytes 983048 | tf_op jit(solution)/shard_map/ppermute | solution.py:319
  209.4 15.4 %collective-permute-start.47 = (bf16[128,1024]{1,0:T(8,128)(2,1)S(1)}, bf16[128,1024]{1,0:T(8,128)(2,1)S(1)}, u32[]{:S(2)}, u32[]{:S(2)}) collective-permute-start(bf16[128,1024]{1,0:T(8,128)(2,1)S(1)} %get-tuple-element.150), channel_id=1, source_target_pairs={{0,4},{4,0},{8,12},{12,8},{1,5},{5,1},{9,13},{13,9},{2,6},{6,2},{1... | collective-permute-start | bytes 786440 | tf_op jit(solution)/shard_map/ppermute | solution.py:336
  209.5 15.3 %collective-permute-start.48 = (bf16[128,1024]{1,0:T(8,128)(2,1)S(1)}, bf16[128,1024]{1,0:T(8,128)(2,1)S(1)}, u32[]{:S(2)}, u32[]{:S(2)}) collective-permute-start(bf16[128,1024]{1,0:T(8,128)(2,1)S(1)} %get-tuple-element.149), channel_id=1, source_target_pairs={{0,8},{8,0},{4,12},{12,4},{1,9},{9,1},{5,13},{13,5},{2,10},{10,2},... | collective-permute-start | bytes 786440 | tf_op jit(solution)/shard_map/ppermute | solution.py:334
  211.1 12.3 %collective-permute-start.49 = (bf16[128,1024]{1,0:T(8,128)(2,1)S(1)}, bf16[128,1024]{1,0:T(8,128)(2,1)S(1)}, u32[]{:S(2)}, u32[]{:S(2)}) collective-permute-start(bf16[128,1024]{1,0:T(8,128)(2,1)S(1)} %get-tuple-element.148), channel_id=1, source_target_pairs={{0,12},{12,0},{4,8},{8,4},{1,13},{13,1},{5,9},{9,5},{2,14},{14,2},... | collective-permute-start | bytes 786440 | tf_op jit(solution)/shard_map/ppermute | solution.py:335
  218.3 12.7 %collective-permute-start.46 = (bf16[128,512]{1,0:T(8,128)(2,1)S(1)}, bf16[128,512]{1,0:T(8,128)(2,1)S(1)}, u32[]{:S(2)}, u32[]{:S(2)}) collective-permute-start(bf16[128,512]{1,0:T(8,128)(2,1)S(1)} %get-tuple-element.170), channel_id=1, source_target_pairs={{0,12},{12,0},{4,8},{8,4},{1,13},{13,1},{5,9},{9,5},{2,14},{14,2},... | collective-permute-start | bytes 393224 | tf_op jit(solution)/shard_map/ppermute | solution.py:335
  219.3 11.7 %collective-permute-start.44 = (bf16[128,512]{1,0:T(8,128)(2,1)S(1)}, bf16[128,512]{1,0:T(8,128)(2,1)S(1)}, u32[]{:S(2)}, u32[]{:S(2)}) collective-permute-start(bf16[128,512]{1,0:T(8,128)(2,1)S(1)} %get-tuple-element.172), channel_id=1, source_target_pairs={{0,4},{4,0},{8,12},{12,8},{1,5},{5,1},{9,13},{13,9},{2,6},{6,2},{1... | collective-permute-start | bytes 393224 | tf_op jit(solution)/shard_map/ppermute | solution.py:336
  (10 other events, 45.0 us)

commit v3 on v2

v3 whole, which is shorter than its diff:
```python
import functools

import jax
import jax.numpy as jnp
from jax import lax
from jax.experimental import pallas as pl
from jax.experimental.pallas import tpu as pltpu
from jax.sharding import PartitionSpec as P


SLOTS = 128
PAIR_ROWS = 80


LOWRANK_SCALE = 2.0


def partner(x, axis, distance):
    return lax.ppermute(x, axis, [(i, i ^ 1 << distance) for i in range(lax.axis_size(axis))])


def silu_slope(inputs):
    gate_value = jax.nn.sigmoid(inputs)
    return gate_value * (1.0 + inputs * (1.0 - gate_value))


def take_block(rows_all, offset, row_count):
    filler = jnp.zeros((row_count,) + rows_all.shape[1:], rows_all.dtype)
    padded = jnp.concatenate([rows_all, filler], 0)
    return lax.dynamic_slice_in_dim(padded, offset, row_count, 0)


def place_block(rows_kept, block, offset, row_total):
    filler = jnp.zeros((block.shape[0],) + rows_kept.shape[1:], rows_kept.dtype)
    padded = jnp.concatenate([rows_kept, filler], 0)
    placed = lax.dynamic_update_slice_in_dim(padded, block, offset, 0)
    return placed[:row_total]


def after(x, *others):
    return lax.optimization_barrier((x,) + others)[0]


def scattered_plan(
    tokens, up_weight, down_factor, up_factor, own_count, output_gradient
):
    dp_total, fsdp_total = lax.axis_size("dp"), lax.axis_size("fsdp")
    live_rows = jnp.arange(tokens.shape[0], dtype=jnp.int32)[:, None] < own_count
    spare_rows = SLOTS - PAIR_ROWS
    half_bit = dp_total.bit_length() - 2
    kept_rows = jnp.minimum(own_count, PAIR_ROWS)
    guest = partner(take_block(tokens, kept_rows, spare_rows), "dp", half_bit)
    packed = place_block(tokens[:PAIR_ROWS], guest, kept_rows, PAIR_ROWS)
    sliced_rows = lax.all_to_all(packed, "fsdp", split_axis=1, concat_axis=0, tiled=True)
    slice_width = sliced_rows.shape[1]
    all_rows = lax.all_gather(sliced_rows, "dp", axis=0, tiled=True)
    all_rows = all_rows.reshape(dp_total, fsdp_total, PAIR_ROWS, slice_width).swapaxes(0, 1)
    partial_blocks = jnp.dot(
        all_rows.reshape(-1, slice_width), up_weight, preferred_element_type=jnp.float32
    ).astype(jnp.bfloat16)
    blocks = lax.psum_scatter(partial_blocks, "fsdp", scatter_dimension=0, tiled=True)
    paired_base = lax.all_to_all(blocks, "dp", split_axis=0, concat_axis=1, tiled=True)
    returned = partner(take_block(paired_base, kept_rows, spare_rows), "dp", half_bit)
    base_output = place_block(paired_base, returned, kept_rows, SLOTS)
    rank_projection = lax.dot_general(
        tokens, down_factor, (((1,), (1,)), ((), ())), preferred_element_type=jnp.float32
    ).astype(jnp.bfloat16)
    adapter_update = jnp.dot(rank_projection, up_factor, preferred_element_type=jnp.float32)
    hidden_preactivation = base_output.astype(jnp.float32) + LOWRANK_SCALE * adapter_update
    act_out = jnp.where(live_rows, jax.nn.silu(hidden_preactivation), 0.0).astype(jnp.bfloat16)
    grad_pre = jnp.where(
        live_rows, output_gradient.astype(jnp.float32) * silu_slope(hidden_preactivation), 0.0
    ).astype(jnp.bfloat16)
    low_sum = lax.dot_general(
        grad_pre, up_factor, (((1,), (1,)), ((), ())), preferred_element_type=jnp.float32
    )
    second_factor_gradient = LOWRANK_SCALE * lax.dot_general(
        rank_projection, grad_pre, (((0,), (0,)), ((), ())), preferred_element_type=jnp.float32
    )
    return act_out, low_sum, second_factor_gradient


def tail_kernel(
    slots_ref, counts_ref, own_ref, beside_ref, across_ref, diagonal_ref, mix_ref, rank_t_ref,
    factor_ref, cotangent_ref, low_in_ref, *rest
):
    act_ref, second_ref, low_ref, base_ref = rest[-4:]
    which, tile = pl.program_id(0), pl.program_id(1)

    @pl.when((which == 0) & (tile == 0))
    def _():
        low_ref[...] = low_in_ref[...]

    for index, source_ref in enumerate((own_ref, beside_ref, across_ref, diagonal_ref)):

        @pl.when(which == index)
        def _(source_ref=source_ref):
            base_ref[:SLOTS] = source_ref[...]

    factor = factor_ref[...]
    base_ref[SLOTS:] = factor
    inputs = jnp.dot(mix_ref[...], base_ref[...], preferred_element_type=jnp.float32)
    gate_value = jax.nn.sigmoid(inputs)
    live = lax.broadcasted_iota(jnp.int32, inputs.shape, 0) < counts_ref[0]
    kept = jnp.where(live, gate_value, 0.0)
    act = inputs * kept
    act_ref[...] = act.astype(jnp.bfloat16)
    slope = kept + act * (1.0 - gate_value)
    grad_pre = (cotangent_ref[...].astype(jnp.float32) * slope).astype(jnp.bfloat16)
    second_ref[...] = jnp.dot(rank_t_ref[...], grad_pre, preferred_element_type=jnp.float32)
    low_ref[...] += lax.dot_general(
        grad_pre, factor, (((1,), (1,)), ((), ())), preferred_element_type=jnp.float32
    )


def tail(bases, mix, rank_t, factor, cotangent, low, made, slots, count, offset, unit):
    width = bases[0].shape[1]
    rank_total, hidden = factor.shape
    start = offset // unit

    def local(i, t, slots, counts):
        return (0, t)

    def whole(i, t, slots, counts):
        return (0, 0)

    def placed(i, t, slots, counts):
        return (0, slots[i] + start + t)

    in_specs = [pl.BlockSpec((SLOTS, unit), local)] * 4 + [
        pl.BlockSpec(mix.shape, whole),
        pl.BlockSpec(rank_t.shape, whole),
        pl.BlockSpec((rank_total, unit), placed),
        pl.BlockSpec((SLOTS, unit), placed),
        pl.BlockSpec(low.shape, whole),
    ]
    operands = [*bases, mix, rank_t, factor, cotangent, low]
    aliases = {}
    if made is not None:
        in_specs += [pl.BlockSpec(memory_space=pl.ANY)] * 2
        aliases = {2 + len(operands): 0, 3 + len(operands): 1}
        operands += list(made)
    act_out, second, low = pl.pallas_call(
        tail_kernel,
        name="tail",
        out_shape=(
            jax.ShapeDtypeStruct((SLOTS, hidden), jnp.bfloat16),
            jax.ShapeDtypeStruct((rank_total, hidden), jnp.float32),
            jax.ShapeDtypeStruct(low.shape, jnp.float32),
        ),
        grid_spec=pltpu.PrefetchScalarGridSpec(
            num_scalar_prefetch=2,
            grid=(4, width // unit),
            in_specs=in_specs,
            out_specs=(
                pl.BlockSpec((SLOTS, unit), placed),
                pl.BlockSpec((rank_total, unit), placed),
                pl.BlockSpec(low.shape, whole),
            ),
            scratch_shapes=[pltpu.VMEM((SLOTS + rank_total, unit), jnp.bfloat16)],
        ),
        input_output_aliases=aliases,
        cost_estimate=pl.CostEstimate(
            flops=2 * 4 * width * SLOTS * (SLOTS + 3 * rank_total),
            bytes_accessed=4 * width * SLOTS * 8,
            transcendentals=4 * width * SLOTS,
        ),
        compiler_params=pltpu.CompilerParams(
            dimension_semantics=("arbitrary", "arbitrary"), vmem_limit_bytes=6 * 2**20
        ),
    )(slots, count, *operands)
    return (act_out, second), low


CHUNKS = 7
BATCHES = (2, 2, 1, 1, 1)


def prepare_kernel(widths, places_ref, arrange_ref, tokens_ref, *outs):
    index = 0
    for kept_ref, spill_ref in (outs[:2], outs[2:]):
        begin = 0
        for width in widths:
            at = pl.multiple_of(places_ref[index], 128)
            rows = jnp.dot(
                arrange_ref[...], tokens_ref[:, pl.ds(at, width)],
                preferred_element_type=jnp.float32,
            ).astype(jnp.bfloat16)
            kept_ref[:, begin : begin + width] = rows[:PAIR_ROWS]
            spill_ref[:, begin : begin + width] = rows[PAIR_ROWS:]
            begin += width
            index += 1


def prepare(places, widths, arrange, tokens):
    columns = sum(widths)
    kept = jax.ShapeDtypeStruct((PAIR_ROWS, columns), tokens.dtype)
    spill = jax.ShapeDtypeStruct((SLOTS - PAIR_ROWS, columns), tokens.dtype)
    return pl.pallas_call(
        functools.partial(prepare_kernel, widths),
        name="prepare",
        out_shape=(kept, spill, kept, spill),
        grid_spec=pltpu.PrefetchScalarGridSpec(
            num_scalar_prefetch=1,
            grid=(1,),
            in_specs=[
                pl.BlockSpec(arrange.shape, lambda i, places: (0, 0)),
                pl.BlockSpec(tokens.shape, lambda i, places: (0, 0)),
            ],
            out_specs=[
                pl.BlockSpec(out.shape, lambda i, places: (0, 0))
                for out in (kept, spill, kept, spill)
            ],
        ),
        cost_estimate=pl.CostEstimate(
            flops=4 * SLOTS * SLOTS * columns, bytes_accessed=8 * SLOTS * columns, transcendentals=0
        ),
        compiler_params=pltpu.CompilerParams(vmem_limit_bytes=8 * 2**20),
    )(places, arrange, tokens)


def plane_plan(
    tokens, up_weight, down_factor, up_factor, own_count, output_gradient
):
    groups = lax.axis_size("groups")
    place, group = lax.axis_index("fsdp"), lax.axis_index("groups")
    position = lax.axis_index("dp")
    upper = position >= 2
    inner = (place == 1) | (place == 2)
    near = jnp.where(place < 2, 1, 2)
    far = 3 - near
    slice_width, width = up_weight.shape
    part = slice_width // groups
    chunks, batches = CHUNKS, BATCHES
    unit = width // chunks
    spare = SLOTS - PAIR_ROWS
    pair_total = 2 * PAIR_ROWS
    home_total = 2 * pair_total
    beside = [(0, 1), (1, 0), (2, 3), (3, 2)]
    across = [(0, 2), (2, 0), (1, 3), (3, 1)]
    diagonal = [(0, 3), (3, 0), (1, 2), (2, 1)]
    inward = [(0, 1), (3, 2)]
    outward = [(1, 0), (2, 3)]
    middle = [(1, 2), (2, 1)]
    crossing = [(0, 2), (3, 1)]

    row = jnp.arange(SLOTS, dtype=jnp.int32)
    flipped = jnp.where(row < PAIR_ROWS, PAIR_ROWS - 1 - row, SLOTS + PAIR_ROWS - 1 - row)
    arranged = jnp.where(upper, flipped, row)
    arrange = (arranged[:, None] == row[None, :]).astype(jnp.bfloat16)

    def origins(target):
        outer = jnp.where(target < 2, 0, 3)
        return [target * slice_width] + [
            outer * slice_width + lax.rem(group + step, groups) * part for step in range(groups)
        ]

    places = jnp.stack(origins(far) + origins(near)).astype(jnp.int32)
    widths = [slice_width] + [part] * groups
    far_kept, far_spill, near_kept, near_spill = prepare(places, widths, arrange, tokens)
    far_guest = lax.ppermute(far_spill, "dp", across)

    def own_part(weight, c):
        return lax.dynamic_slice(weight, (group * part, c * unit), (part, unit))

    first_weight = after(up_weight, far_spill)
    parts = [own_part(first_weight, c) for c in (0, 1)]
    lines = {0: lax.ppermute(parts[0], "fsdp", inward)}
    near_guest = lax.ppermute(near_spill, "dp", across)

    spot = jnp.where(upper, PAIR_ROWS, 0) + jnp.arange(PAIR_ROWS, dtype=jnp.int32)[:, None]
    is_own = jnp.where(upper, pair_total - 1 - spot, spot) < own_count
    is_guest = (spot >= PAIR_ROWS - spare) & (spot < SLOTS) & ~is_own

    def pack(kept, guest):
        blank = jnp.zeros((PAIR_ROWS - spare, guest.shape[1]), guest.dtype)
        front, back = jnp.concatenate([guest, blank], 0), jnp.concatenate([blank, guest], 0)
        return jnp.where(is_guest, jnp.where(upper, front, back), kept)

    def start_weight(c, *order):
        return lax.ppermute(after(parts[c], *order), "fsdp", inward)

    def share_weight(c, *order):
        line = lines[c]
        pieces = [line]
        line = after(line, *order)
        for step in range(1, groups):
            pairs = [(i, (i - step) % groups) for i in range(groups)]
            pieces.append(lax.ppermute(line, "groups", pairs))
        return pieces

    def ordered_pair(mine):
        theirs = lax.ppermute(mine, "dp", across)
        return jnp.concatenate(
            [jnp.where(upper, theirs, mine), jnp.where(upper, mine, theirs)], 0
        )

    far_columns = pack(far_kept, after(far_guest, parts[0]))
    from_far = lax.ppermute(far_columns, "fsdp", middle)
    near_columns = pack(near_kept, after(near_guest, far_columns))
    near_pair = ordered_pair(near_columns)
    rest_weight = after(up_weight, near_columns)
    parts += [own_part(rest_weight, c) for c in range(2, chunks)]
    rest_weight = after(rest_weight, parts[-1])
    column_weights = [rest_weight[:, :unit]]
    shared = {0: share_weight(0, near_columns)}
    from_far_outer = lax.ppermute(after(far_columns, near_columns), "fsdp", crossing)
    for c in (1, 2):
        lines[c] = start_weight(c, near_columns)
    from_outer = lax.ppermute(near_columns, "fsdp", inward)
    far_pair = ordered_pair(from_far)
    far_rows = jnp.concatenate([far_pair, lax.ppermute(far_pair, "dp", beside)], 0)
    lines[3] = start_weight(3, far_pair)
    outer_pair = ordered_pair(from_far_outer)
    far_outer_rows = jnp.concatenate([outer_pair, lax.ppermute(outer_pair, "dp", beside)], 0)

    def multiply(rows, weight):
        product = jnp.dot(rows, weight, preferred_element_type=jnp.float32)
        return product.astype(jnp.bfloat16)

    weights, sent = {}, {}

    def gather_weight(c):
        weights[c] = jnp.concatenate([column_weights[c]] + shared[c], 0)
        return weights[c]

    rank = lax.dot_general(
        tokens, down_factor, (((1,), (1,)), ((), ())), preferred_element_type=jnp.float32
    ).astype(jnp.bfloat16)
    scaled = (LOWRANK_SCALE * rank).astype(jnp.bfloat16)
    rank_t = scaled.T
    source = jnp.where(upper, SLOTS - 1 - row, row)
    turn = (source[:, None] == row[None, :]).astype(jnp.bfloat16)
    mix = jnp.concatenate([turn, scaled], 1)
    slots = (position ^ jnp.arange(4, dtype=jnp.int32)) * chunks
    low = jnp.zeros((SLOTS, rank.shape[1]), jnp.float32)
    count = own_count.reshape(1)

    first = multiply(far_rows, gather_weight(0))
    first_in = lax.ppermute(first, "fsdp", middle)
    shared[1] = share_weight(1, first)
    rest_weight = after(rest_weight, first)
    column_weights += [rest_weight[:, c * unit : (c + 1) * unit] for c in (1, 2)]
    second = multiply(after(far_outer_rows, first), weights[0])
    second_in = lax.ppermute(second, "fsdp", middle)
    sent[0] = second, jnp.concatenate([first_in, second_in], 0)
    last = second
    rest_weight = after(rest_weight, second)
    column_weights += [rest_weight[:, c * unit : (c + 1) * unit] for c in range(3, chunks)]
    all_far_rows = jnp.concatenate([far_rows, far_outer_rows], 0)
    shared[2] = share_weight(2, last)

    def send_last(c, *order):
        outer = multiply(after(far_outer_rows, *order), gather_weight(c))
        outer_in = lax.ppermute(outer, "fsdp", middle)
        own = multiply(after(far_rows, outer), weights[c])
        sent[c] = outer_in, lax.ppermute(own, "fsdp", middle)
        return own

    def finish_half(c, half, *order):
        rows = after(near_rows[home_total:] if half == 0 else near_rows[:home_total], *order)
        summed = jnp.dot(rows, weights[c], preferred_element_type=jnp.float32)
        return (summed + sent[c][half].astype(jnp.float32)).astype(jnp.bfloat16)

    def send(c, *order):
        outgoing = multiply(after(all_far_rows, *order), gather_weight(c))
        sent[c] = outgoing, lax.ppermute(outgoing, "fsdp", middle)
        return outgoing

    last = send(1, last)
    lines[4] = start_weight(4, last)
    near_outer_pair = ordered_pair(after(from_outer, last))
    last = send(2, last)
    lines[5] = start_weight(5, last)
    shared[3] = share_weight(3, last)
    near_pairs = jnp.concatenate([near_pair, after(near_outer_pair, last)], 0)
    near_others = lax.ppermute(near_pairs, "dp", beside)
    near_rows = jnp.concatenate(
        [near_pair, near_others[:pair_total], near_outer_pair, near_others[pair_total:]], 0
    )

    def finish(c, *order):
        rows = after(near_rows, *order)
        summed = jnp.dot(rows, weights[c], preferred_element_type=jnp.float32)
        summed = (summed + sent[c][1].astype(jnp.float32)).astype(jnp.bfloat16)
        return summed, lax.ppermute(summed[home_total:], "fsdp", outward)

    def hand_out(members, *order):
        handed = [after(handed, *order) for _, handed in members]
        homes = [
            jnp.where(inner, summed[:home_total], back)
            for (summed, _), back in zip(members, handed, strict=True)
        ]
        home = jnp.concatenate(homes, 1).reshape(2, pair_total, -1)
        shape = (1, SLOTS, home.shape[2])
        low_at, high_at = jnp.int32(0), jnp.int32(pair_total - SLOTS)
        same, other = jnp.where(upper, high_at, low_at), jnp.where(upper, low_at, high_at)
        cuts = [
            lax.dynamic_slice(home, (pair, row_at, 0), shape)[0]
            for pair, row_at in ((0, same), (1, same), (0, other), (1, other))
        ]
        opposite = lax.ppermute(cuts[2], "dp", across)
        cornered = lax.ppermute(cuts[3], "dp", diagonal)
        adjacent = lax.ppermute(cuts[1], "dp", beside)
        return cuts, [cuts[0], adjacent, opposite, cornered]

    batch_ends = [sum(batches[: b + 1]) - 1 for b in range(len(batches))]
    made = None
    summed, pending = {}, []

    def finish_tail(last):
        nonlocal made, low
        bases, offset = pending.pop(0)
        bases[3] = after(bases[3], last)
        made, low = tail(
            bases, mix, rank_t, up_factor, output_gradient, low, made, slots, count,
            offset, unit,
        )
        return low

    def hand_batch(c, last):
        if c not in batch_ends:
            return last
        b = batch_ends.index(c)
        begin = batch_ends[b] - batches[b] + 1
        cuts, bases = hand_out([summed[c] for c in range(begin, c + 1)], last)
        pending.append((bases, begin * unit))
        return cuts[0]

    final = chunks - 1
    for i in range(final):
        summed[i] = finish(i, last)
        last = summed[i][0]
        if i + 6 < chunks:
            lines[i + 6] = start_weight(i + 6, last)
        if i + 4 < chunks:
            shared[i + 4] = share_weight(i + 4, last)
        if i + 3 < final:
            last = send(i + 3, last)
        elif i + 3 == final:
            last = send_last(final, last)
        if i > 0:
            last = hand_batch(i - 1, last)
    outer_sum = finish_half(final, 0, last)
    handed = lax.ppermute(outer_sum, "fsdp", outward)
    last = finish_tail(outer_sum)
    last = hand_batch(final - 1, last)
    own_sum = finish_half(final, 1, last)
    summed[final] = own_sum, handed
    last = hand_batch(final, own_sum)
    while pending:
        last = finish_tail(last)
    return made[0], low, made[1]


def per_device(
    plane, tokens, up_weight, first_adapter_factors, second_adapter_factors, counts, output_gradient
):
    slice_width, width = up_weight.shape
    fits = width % (CHUNKS * 128) == 0 and slice_width % (128 * lax.axis_size("groups")) == 0
    plan = plane_plan if plane and fits else scattered_plan
    act_out, low_sum, second_factor_gradient = plan(
        tokens, up_weight, first_adapter_factors[0], second_adapter_factors[0], counts[0],
        output_gradient,
    )
    low_rank_gradient = (LOWRANK_SCALE * low_sum).astype(jnp.bfloat16)
    grad_a = lax.dot_general(
        low_rank_gradient, tokens, (((0,), (0,)), ((), ())), preferred_element_type=jnp.float32
    )
    return (act_out, grad_a[None], second_factor_gradient[None])


def solution(mesh):
    placed = (
        P(("groups", "dp", "fsdp"), None),
        P("fsdp", "dp"),
        P(("groups", "dp", "fsdp"), None, None),
        P(("groups", "dp", "fsdp"), None, None),
        P(("groups", "dp", "fsdp")),
        P(("groups", "dp", "fsdp"), None),
    )

    plane = mesh.shape["fsdp"] == 4 and mesh.shape["dp"] == 4
    return jax.shard_map(
        functools.partial(per_device, plane),
        mesh=mesh,
        in_specs=placed,
        out_specs=(
            P(("groups", "dp", "fsdp"), None),
            P(("groups", "dp", "fsdp"), None, None),
            P(("groups", "dp", "fsdp"), None, None),
        ),
        check_vma=False,
    )
```

time: 237 us -> 263 us (1.11)
  starting transfers between devices: 84.5 us -> 97.1 us
  matrix products: 23.2 us -> 30.1 us
  other arithmetic: 3.67 us -> 8.25 us
    ppermute x12 -> x17, starting transfers between devices: 13.9 us -> 35.8 us  [the longest x1 14.2 us: plane_plan(): lines = {0: lax.ppermute(parts[0], 'fsdp', inward)}]
    ppermute x7, waiting for transfers between devices: 9.47 us -> 24.8 us  [share_weight(): pieces.append(lax.ppermute(line, 'groups', pairs))]
    ppermute x4, waiting for transfers between devices: 15.5 us -> 4.25 us  [ordered_pair(): theirs = lax.ppermute(mine, 'dp', across)]
    ppermute x4 -> x5, waiting for transfers between devices: 12.5 us -> 1.89 us  [hand_out(): cornered = lax.ppermute(cuts[3], 'dp', diagonal)]
    ppermute x12 -> x17, waiting for transfers between devices: 5.93 us -> 15.5 us  [the longest x1 8.28 us: plane_plan(): handed = lax.ppermute(outer_sum, 'fsdp', outward)]
    ppermute x6, waiting for transfers between devices: 20.6 us -> 11.7 us  [start_weight(): return lax.ppermute(after(parts[c], *order), 'fsdp', inward)]
    ppermute x6, starting transfers between devices: 33.9 us -> 25.7 us  [start_weight(): return lax.ppermute(after(parts[c], *order), 'fsdp', inward)]
    dot_general x15 -> x17, matrix products: 21.7 us -> 28.6 us  [the longest x9 16.7 us: multiply(): product = jnp.dot(rows, weight, preferred_element_type=jnp.float32)]
  transfers between devices with their start and end apart: 50 -> 57, of which waited for: 16 -> 18; matrix products, arithmetic and copies ran while one was open for 15% -> 18% of each run, Pallas kernels for 8% -> 7%
where the time goes in v3:
time: 263 us; the launch traced here: 262 us
  starting transfers between devices  97.1 us (37%)
  waiting for transfers between devices  85.9 us (33%)
  matrix products  30.1 us (11%)
  Pallas kernels  22.2 us (8%)
  local copies, waits for them, and re-layouts  16.3 us (6%)
  other arithmetic  8.25 us (3%)
    ppermute x6, starting transfers between devices, start_weight(): return lax.ppermute(after(parts[c], *order), 'fsdp', inward)  25.7 us
    ppermute x6, waiting for transfers between devices, finish(): return (summed, lax.ppermute(summed[home_total:], 'fsdp', outward))  25.3 us
    ppermute x7, waiting for transfers between devices, share_weight(): pieces.append(lax.ppermute(line, 'groups', pairs))  24.8 us
    pallas_call x5, Pallas kernels, tail(): pl.pallas_call(tail_kernel, name='tail', out_shape=(jax.ShapeDtypeStruct(...  21.2 us
    dot_general x9, matrix products, multiply(): product = jnp.dot(rows, weight, preferred_element_type=jnp.float32)  16.7 us
    ppermute x1, starting transfers between devices, plane_plan(): lines = {0: lax.ppermute(parts[0], 'fsdp', inward)}  14.2 us
    ppermute x6, waiting for transfers between devices, start_weight(): return lax.ppermute(after(parts[c], *order), 'fsdp', inward)  11.7 us
    dot_general x6, matrix products, finish(): summed = jnp.dot(rows, weights[c], preferred_element_type=jnp.float32)  10.2 us
  transfers between devices with their start and end apart: 57, of which 18 were waited for; matrix products, arithmetic and copies ran while one was open for 18% of the time, Pallas kernels for 7%

profile of v3, /device:TPU:0, one launch (start us, length us, event | category | flops | bytes accessed | tf_op | source)
XLA Modules:
  0.0 262.3 jit_solution(6212184871510067540)
XLA Ops:
  3.1 3.1 %collective-permute-start.1 = (bf16[48,2048]{1,0:T(8,128)(2,1)S(1)}, bf16[48,2048]{1,0:T(8,128)(2,1)S(1)}, u32[]{:S(2)}, u32[]{:S(2)}) collective-permute-start(bf16[48,2048]{1,0:T(8,128)(2,1)S(1)} %get-tuple-element.74), channel_id=1, source_target_pairs={{0,8},{8,0},{4,12},{12,4},{1,9},{9,1},{5,13},{13,5},{2,10},{10,2},... | collective-permute-start | bytes 589832 | tf_op jit(solution)/shard_map/ppermute | solution.py:261
  6.8 2.1 constant_dynamic-slice_fusion.5
  8.9 2.1 collective-permute-done.1
  11.9 1.8 collective-permute-start.5
  14.0 14.2 %collective-permute-start.10 = (bf16[512,512]{1,0:T(8,128)(2,1)}, bf16[512,512]{1,0:T(8,128)(2,1)}, u32[]{:S(2)}, u32[]{:S(2)}) collective-permute-start(bf16[512,512]{1,0:T(8,128)(2,1)} %get-tuple-element.167), channel_id=1, source_target_pairs={{0,1},{3,2},{4,5},{7,6},{8,9},{11,10},{12,13},{15,14},{16,17},{19,... | collective-permute-start | bytes 1572872 | tf_op jit(solution)/shard_map/ppermute | solution.py:268
  30.9 10.1 %collective-permute-start.7 = (bf16[80,2048]{1,0:T(8,128)(2,1)S(1)}, bf16[80,2048]{1,0:T(8,128)(2,1)S(1)}, u32[]{:S(2)}, u32[]{:S(2)}) collective-permute-start(bf16[80,2048]{1,0:T(8,128)(2,1)S(1)} %select_select_fusion.1), channel_id=1, source_target_pairs={{0,2},{3,1},{4,6},{7,5},{8,10},{11,9},{12,14},{15,13},{16,18},{19,... | collective-permute-start | bytes 983048 | tf_op jit(solution)/shard_map/ppermute | solution.py:307
  42.5 1.6 collective-permute-start.2
  44.1 5.0 %collective-permute-done.7 = bf16[80,2048]{1,0:T(8,128)(2,1)S(1)} collective-permute-done((bf16[80,2048]{1,0:T(8,128)(2,1)S(1)}, bf16[80,2048]{1,0:T(8,128)(2,1)S(1)}, u32[]{:S(2)}, u32[]{:S(2)}) %collective-permute-start.7) | collective-permute-done | bytes 327712 | tf_op jit(solution)/shard_map/ppermute | solution.py:307
  50.6 3.1 %constant_dynamic-slice_fusion.1 = (bf16[512,512]{1,0:T(8,128)(2,1)}, bf16[512,512]{1,0:T(8,128)(2,1)}, bf16[512,512]{1,0:T(8,128)(2,1)}, bf16[512,512]{1,0:T(8,128)(2,1)S(1)}, bf16[512,512]{1,0:T(8,128)(2,1)}) fusion(bf16[1024,3584]{1,0:T(8,128)(2,1)} %param.7, s32[]{:T(128)S(6)} %select_n.193), kind=kLoop, calls=%fused_computation.111 | loop fusion | bytes 5242884 | tf_op jit(solution)/shard_map/dynamic_slice | solution.py:264
  55.0 4.3 %collective-permute-start.15 = (bf16[512,512]{1,0:T(8,128)(2,1)S(1)}, bf16[512,512]{1,0:T(8,128)(2,1)S(1)}, u32[]{:S(2)}, u32[]{:S(2)}) collective-permute-start(bf16[512,512]{1,0:T(8,128)(2,1)S(1)} %get-tuple-element.91), channel_id=1, source_target_pairs={{0,1},{3,2},{4,5},{7,6},{8,9},{11,10},{12,13},{15,14},{16,17},{19,... | collective-permute-start | bytes 1572872 | tf_op jit(solution)/shard_map/ppermute | solution.py:281
  60.7 1.6 collective-permute-start.11
  63.5 10.0 %collective-permute-done.11 = bf16[512,512]{1,0:T(8,128)(2,1)S(1)} collective-permute-done((bf16[512,512]{1,0:T(8,128)(2,1)}, bf16[512,512]{1,0:T(8,128)(2,1)S(1)}, u32[]{:S(2)}, u32[]{:S(2)}) %collective-permute-start.11) | collective-permute-done | bytes 524320 | tf_op jit(solution)/shard_map/ppermute | solution.py:289
  73.5 2.8 %convolution_convert_fusion.8 = bf16[320,512]{1,0:T(8,128)(2,1)} fusion(bf16[512,512]{1,0:T(8,128)(2,1)S(1)} %collective-permute-done.11, bf16[512,512]{1,0:T(8,128)(2,1)} %collective-permute-done.10, bf16[1024,512]{1,0:T(8,128)(2,1)S(1)} %slice.67, bf16[160,2048]{1,0:T(8,128)(2,1)S(1)} %collective-permute-done.6, ...), kind=kOutput, calls=%fused_computation.38 | convolution fusion | flops 681476096 | bytes 3735552 | tf_op jit(solution)/shard_map/dot_general | solution.py:318
  76.3 4.5 %collective-permute-done.12 = bf16[512,512]{1,0:T(8,128)(2,1)S(1)} collective-permute-done((bf16[512,512]{1,0:T(8,128)(2,1)S(1)}, bf16[512,512]{1,0:T(8,128)(2,1)S(1)}, u32[]{:S(2)}, u32[]{:S(2)}) %collective-permute-start.12) | collective-permute-done | bytes 524320 | tf_op jit(solution)/shard_map/ppermute | solution.py:281
  82.2 1.7 fusion.25
  84.2 3.0 %convolution_convert_fusion.7 = bf16[320,512]{1,0:T(8,128)(2,1)} fusion(bf16[320,2048]{1,0:T(8,128)(2,1)S(1)} %pad_maximum_fusion.7, bf16[512,512]{1,0:T(8,128)(2,1)S(1)} %collective-permute-done.11, bf16[512,512]{1,0:T(8,128)(2,1)} %collective-permute-done.10, bf16[1024,512]{1,0:T(8,128)(2,1)S(1)} %slice.67), kind=kOutput, calls=%fused_computation.37 | convolution fusion | flops 677543936 | bytes 3735552 | tf_op jit(solution)/shard_map/dot_general | solution.py:318
  87.2 5.5 %collective-permute-done.13 = bf16[512,512]{1,0:T(8,128)(2,1)S(1)} collective-permute-done((bf16[512,512]{1,0:T(8,128)(2,1)S(1)}, bf16[512,512]{1,0:T(8,128)(2,1)S(1)}, u32[]{:S(2)}, u32[]{:S(2)}) %collective-permute-start.13) | collective-permute-done | bytes 524320 | tf_op jit(solution)/shard_map/ppermute | solution.py:289
  92.6 2.4 convolution_convert_fusion.4
  97.8 4.2 %collective-permute-done.14 = bf16[80,2048]{1,0:T(8,128)(2,1)S(1)} collective-permute-done((bf16[80,2048]{1,0:T(8,128)(2,1)S(1)}, bf16[80,2048]{1,0:T(8,128)(2,1)S(1)}, u32[]{:S(2)}, u32[]{:S(2)}) %collective-permute-start.14) | collective-permute-done | bytes 327712 | tf_op jit(solution)/shard_map/ppermute | solution.py:293
  102.2 4.9 %collective-permute-done.16 = bf16[512,512]{1,0:T(8,128)(2,1)S(1)} collective-permute-done((bf16[512,512]{1,0:T(8,128)(2,1)S(1)}, bf16[512,512]{1,0:T(8,128)(2,1)S(1)}, u32[]{:S(2)}, u32[]{:S(2)}) %collective-permute-start.16) | collective-permute-done | bytes 524320 | tf_op jit(solution)/shard_map/ppermute | solution.py:289
  107.1 2.4 convolution_convert_fusion.3
  111.9 4.5 %collective-permute-start.20 = (bf16[512,512]{1,0:T(8,128)(2,1)}, bf16[512,512]{1,0:T(8,128)(2,1)S(1)}, u32[]{:S(2)}, u32[]{:S(2)}) collective-permute-start(bf16[512,512]{1,0:T(8,128)(2,1)} %get-tuple-element.97), channel_id=1, source_target_pairs={{0,1},{3,2},{4,5},{7,6},{8,9},{11,10},{12,13},{15,14},{16,17},{19,... | collective-permute-start | bytes 1572872 | tf_op jit(solution)/shard_map/ppermute | solution.py:281
  119.9 2.6 %fusion.24 = (bf16[1024,512]{1,0:T(8,128)(2,1)S(1)}, bf16[1024,512]{1,0:T(8,128)(2,1)S(1)}, bf16[1024,512]{1,0:T(8,128)(2,1)S(1)}, bf16[1024,512]{1,0:T(8,128)(2,1)S(1)}) fusion(bf16[1024,3584]{1,0:T(8,128)(2,1)} %param.7), kind=kLoop, calls=%fused_computation.129 | loop fusion | bytes 8388608 | tf_op jit(solution)/shard_map/slice | solution.py:349
  122.5 5.5 %collective-permute-done.20 = bf16[512,512]{1,0:T(8,128)(2,1)S(1)} collective-permute-done((bf16[512,512]{1,0:T(8,128)(2,1)}, bf16[512,512]{1,0:T(8,128)(2,1)S(1)}, u32[]{:S(2)}, u32[]{:S(2)}) %collective-permute-start.20) | collective-permute-done | bytes 524320 | tf_op jit(solution)/shard_map/ppermute | solution.py:281
  128.0 4.3 %collective-permute-start.23 = (bf16[512,512]{1,0:T(8,128)(2,1)S(1)}, bf16[512,512]{1,0:T(8,128)(2,1)S(1)}, u32[]{:S(2)}, u32[]{:S(2)}) collective-permute-start(bf16[512,512]{1,0:T(8,128)(2,1)S(1)} %copy-done.17), channel_id=1, source_target_pairs={{0,1},{3,2},{4,5},{7,6},{8,9},{11,10},{12,13},{15,14},{16,17},{19,... | collective-permute-start | bytes 1572872 | tf_op jit(solution)/shard_map/ppermute | solution.py:281
  132.4 1.5 collective-permute-start.21
  133.9 1.7 fusion.26
  137.7 4.1 %collective-permute-start.28 = (bf16[512,512]{1,0:T(8,128)(2,1)S(1)}, bf16[512,512]{1,0:T(8,128)(2,1)S(1)}, u32[]{:S(2)}, u32[]{:S(2)}) collective-permute-start(bf16[512,512]{1,0:T(8,128)(2,1)S(1)} %copy-done.16), channel_id=1, source_target_pairs={{0,1},{3,2},{4,5},{7,6},{8,9},{11,10},{12,13},{15,14},{16,17},{19,... | collective-permute-start | bytes 1572872 | tf_op jit(solution)/shard_map/ppermute | solution.py:281
  141.8 2.6 fusion
  150.2 7.2 %collective-permute-start.32 = (bf16[512,512]{1,0:T(8,128)(2,1)S(1)}, bf16[512,512]{1,0:T(8,128)(2,1)S(1)}, u32[]{:S(2)}, u32[]{:S(2)}) collective-permute-start(bf16[512,512]{1,0:T(8,128)(2,1)S(1)} %copy-done.15), channel_id=1, source_target_pairs={{0,1},{3,2},{4,5},{7,6},{8,9},{11,10},{12,13},{15,14},{16,17},{19,... | collective-permute-start | bytes 1572872 | tf_op jit(solution)/shard_map/ppermute | solution.py:281
  162.8 1.5 fusion.2
  166.6 2.6 collective-permute-done.29
  172.7 1.8 collective-permute-done.30
  177.6 1.8 collective-permute-done.33
  184.0 1.6 collective-permute-start.39
  185.6 13.3 %collective-permute-done.35 = bf16[320,512]{1,0:T(8,128)(2,1)S(1)} collective-permute-done((bf16[320,512]{1,0:T(8,128)(2,1)S(1)}, bf16[320,512]{1,0:T(8,128)(2,1)S(1)}, u32[]{:S(2)}, u32[]{:S(2)}) %collective-permute-start.35) | collective-permute-done | bytes 327712 | tf_op jit(solution)/shard_map/ppermute | solution.py:386
  202.7 10.2 %collective-permute-done.41 = bf16[320,512]{1,0:T(8,128)(2,1)S(1)} collective-permute-done((bf16[320,512]{1,0:T(8,128)(2,1)S(1)}, bf16[320,512]{1,0:T(8,128)(2,1)S(1)}, u32[]{:S(2)}, u32[]{:S(2)}) %collective-permute-start.41) | collective-permute-done | bytes 327712 | tf_op jit(solution)/shard_map/ppermute | solution.py:386
  213.8 1.6 collective-permute-start.37
  216.3 1.6 collective-permute-start.54
  218.5 5.7 %tail.5 = (bf16[128,14336]{1,0:T(8,128)(2,1)}, f32[32,14336]{1,0:T(8,128)}, f32[128,32]{1,0:T(8,128)S(1)}) custom-call(s32[4]{0:T(128)S(1)} %xor_multiply_fusion.slots_ref, s32[1]{0:T(128)} %copy.36.counts_ref, bf16[128,1024]{1,0:T(8,128)(2,1)S(1)} %get-tuple-element.178.own_ref, bf16[128,1024]{1,0:T(8,128)(2,1)S(1)} %collective-permute-done.38.beside_ref, ...), custom_call_target="tpu_custom_call" | custom-call | flops 234881024 | bytes 4194304 | tf_op jit(solution)/shard_map/tail/pallas_call | solution.py:143
  227.6 8.3 %collective-permute-done.44 = bf16[320,512]{1,0:T(8,128)(2,1)S(1)} collective-permute-done((bf16[320,512]{1,0:T(8,128)(2,1)S(1)}, bf16[320,512]{1,0:T(8,128)(2,1)S(1)}, u32[]{:S(2)}, u32[]{:S(2)}) %collective-permute-start.44) | collective-permute-done | bytes 327712 | tf_op jit(solution)/shard_map/ppermute | solution.py:445
  235.9 1.5 collective-permute-start.52
  239.8 2.4 collective-permute-done.52.across_ref
  242.3 1.9 collective-permute-done.50.diagonal_ref
  245.7 5.7 %tail.6 = (bf16[128,14336]{1,0:T(8,128)(2,1)}, f32[32,14336]{1,0:T(8,128)}, f32[128,32]{1,0:T(8,128)S(1)}) custom-call(s32[4]{0:T(128)S(1)} %xor_multiply_fusion.slots_ref, s32[1]{0:T(128)} %copy.36.counts_ref, bf16[128,1024]{1,0:T(8,128)(2,1)S(1)} %get-tuple-element.174.own_ref, ...), custom_call_target="tpu_custom_call", output_to_operand_aliasing={{0}: (11, {}), {1}: (12, {})} | custom-call | flops 234881024 | bytes 4194304 | tf_op jit(solution)/shard_map/tail/pallas_call | solution.py:143
  251.4 3.2 %tail.7 = (bf16[128,14336]{1,0:T(8,128)(2,1)}, f32[32,14336]{1,0:T(8,128)}, f32[128,32]{1,0:T(8,128)S(1)}) custom-call(s32[4]{0:T(128)S(1)} %xor_multiply_fusion.slots_ref, s32[1]{0:T(128)} %copy.36.counts_ref, bf16[128,512]{1,0:T(8,128)(2,1)S(1)} %get-tuple-element.184.own_ref, ...), custom_call_target="tpu_custom_call", output_to_operand_aliasing={{0}: (11, {}), {1}: (12, {})} | custom-call | flops 117440512 | bytes 2097152 | tf_op jit(solution)/shard_map/tail/pallas_call | solution.py:143
  254.7 3.3 %tail.8 = (bf16[128,14336]{1,0:T(8,128)(2,1)}, f32[32,14336]{1,0:T(8,128)}, f32[128,32]{1,0:T(8,128)S(1)}) custom-call(s32[4]{0:T(128)S(1)} %xor_multiply_fusion.slots_ref, s32[1]{0:T(128)} %copy.36.counts_ref, bf16[128,512]{1,0:T(8,128)(2,1)S(1)} %get-tuple-element.188.own_ref, ...), custom_call_target="tpu_custom_call", output_to_operand_aliasing={{0}: (11, {}), {1}: (12, {})} | custom-call | flops 117440512 | bytes 2097152 | tf_op jit(solution)/shard_map/tail/pallas_call | solution.py:143
  257.9 3.3 %tail.9 = (bf16[128,14336]{1,0:T(8,128)(2,1)}, f32[32,14336]{1,0:T(8,128)}, f32[128,32]{1,0:T(8,128)S(1)}) custom-call(s32[4]{0:T(128)S(1)} %xor_multiply_fusion.slots_ref, s32[1]{0:T(128)} %copy.36.counts_ref, bf16[128,512]{1,0:T(8,128)(2,1)S(1)} %get-tuple-element.192.own_ref, ...), custom_call_target="tpu_custom_call", output_to_operand_aliasing={{0}: (11, {}), {1}: (12, {})} | custom-call | flops 117440512 | bytes 2097152 | tf_op jit(solution)/shard_map/tail/pallas_call | solution.py:143
  (215 shorter events, 64.2 us)
Async XLA Ops:
  11.9 16.3 %collective-permute-start.5 = (bf16[80,2048]{1,0:T(8,128)(2,1)S(1)}, bf16[80,2048]{1,0:T(8,128)(2,1)S(1)}, u32[]{:S(2)}, u32[]{:S(2)}) collective-permute-start(bf16[80,2048]{1,0:T(8,128)(2,1)S(1)} %collective-permute-done.4), channel_id=1, source_target_pairs={{0,8},{8,0},{4,12},{12,4},{1,9},{9,1},{5,13},{13,5},{2,10},{10,2},... | collective-permute-start | bytes 983048 | tf_op jit(solution)/shard_map/ppermute | solution.py:293
  13.7 14.5 %collective-permute-start = (bf16[48,2048]{1,0:T(8,128)(2,1)S(1)}, bf16[48,2048]{1,0:T(8,128)(2,1)S(1)}, u32[]{:S(2)}, u32[]{:S(2)}) collective-permute-start(bf16[48,2048]{1,0:T(8,128)(2,1)S(1)} %get-tuple-element.73), channel_id=1, source_target_pairs={{0,8},{8,0},{4,12},{12,4},{1,9},{9,1},{5,13},{13,5},{2,10},{10,2},... | collective-permute-start | bytes 589832 | tf_op jit(solution)/shard_map/ppermute | solution.py:269
  14.0 41.0 %collective-permute-start.10 = (bf16[512,512]{1,0:T(8,128)(2,1)}, bf16[512,512]{1,0:T(8,128)(2,1)}, u32[]{:S(2)}, u32[]{:S(2)}) collective-permute-start(bf16[512,512]{1,0:T(8,128)(2,1)} %get-tuple-element.167), channel_id=1, source_target_pairs={{0,1},{3,2},{4,5},{7,6},{8,9},{11,10},{12,13},{15,14},{16,17},{19,... | collective-permute-start | bytes 1572872 | tf_op jit(solution)/shard_map/ppermute | solution.py:268
  30.7 28.6 %collective-permute-start.6 = (bf16[160,2048]{1,0:T(8,128)(2,1)}, bf16[160,2048]{1,0:T(8,128)(2,1)S(1)}, u32[]{:S(2)}, u32[]{:S(2)}) collective-permute-start(bf16[160,2048]{1,0:T(8,128)(2,1)} %pad_maximum_fusion.23), channel_id=1, source_target_pairs={{0,4},{4,0},{8,12},{12,8},{1,5},{5,1},{9,13},{13,9},{2,6},{6,2},{1... | collective-permute-start | bytes 1966088 | tf_op jit(solution)/shard_map/ppermute | solution.py:312
  30.9 18.2 %collective-permute-start.7 = (bf16[80,2048]{1,0:T(8,128)(2,1)S(1)}, bf16[80,2048]{1,0:T(8,128)(2,1)S(1)}, u32[]{:S(2)}, u32[]{:S(2)}) collective-permute-start(bf16[80,2048]{1,0:T(8,128)(2,1)S(1)} %select_select_fusion.1), channel_id=1, source_target_pairs={{0,2},{3,1},{4,6},{7,5},{8,10},{11,9},{12,14},{15,13},{16,18},{19,... | collective-permute-start | bytes 983048 | tf_op jit(solution)/shard_map/ppermute | solution.py:307
  41.1 53.9 %collective-permute-start.3 = (bf16[80,2048]{1,0:T(8,128)(2,1)S(1)}, bf16[80,2048]{1,0:T(8,128)(2,1)S(1)}, u32[]{:S(2)}, u32[]{:S(2)}) collective-permute-start(bf16[80,2048]{1,0:T(8,128)(2,1)S(1)} %select_select_fusion), channel_id=1, source_target_pairs={{0,1},{3,2},{4,5},{7,6},{8,9},{11,10},{12,13},{15,14},{16,17},{19,... | collective-permute-start | bytes 983048 | tf_op jit(solution)/shard_map/ppermute | solution.py:310
  42.5 20.0 %collective-permute-start.2 = (bf16[80,2048]{1,0:T(8,128)(2,1)S(1)}, bf16[80,2048]{1,0:T(8,128)(2,1)S(1)}, u32[]{:S(2)}, u32[]{:S(2)}) collective-permute-start(bf16[80,2048]{1,0:T(8,128)(2,1)S(1)} %select_select_fusion), channel_id=1, source_target_pairs={{0,8},{8,0},{4,12},{12,4},{1,9},{9,1},{5,13},{13,5},{2,10},{10,2},... | collective-permute-start | bytes 983048 | tf_op jit(solution)/shard_map/ppermute | solution.py:293
  49.1 11.6 %collective-permute-start.8 = (bf16[80,2048]{1,0:T(8,128)(2,1)S(1)}, bf16[80,2048]{1,0:T(8,128)(2,1)S(1)}, u32[]{:S(2)}, u32[]{:S(2)}) collective-permute-start(bf16[80,2048]{1,0:T(8,128)(2,1)S(1)} %collective-permute-done.7), channel_id=1, source_target_pairs={{0,8},{8,0},{4,12},{12,4},{1,9},{9,1},{5,13},{13,5},{2,10},{10,2},... | collective-permute-start | bytes 983048 | tf_op jit(solution)/shard_map/ppermute | solution.py:293
  55.0 41.4 %collective-permute-start.15 = (bf16[512,512]{1,0:T(8,128)(2,1)S(1)}, bf16[512,512]{1,0:T(8,128)(2,1)S(1)}, u32[]{:S(2)}, u32[]{:S(2)}) collective-permute-start(bf16[512,512]{1,0:T(8,128)(2,1)S(1)} %get-tuple-element.91), channel_id=1, source_target_pairs={{0,1},{3,2},{4,5},{7,6},{8,9},{11,10},{12,13},{15,14},{16,17},{19,... | collective-permute-start | bytes 1572872 | tf_op jit(solution)/shard_map/ppermute | solution.py:281
  59.3 21.4 %collective-permute-start.12 = (bf16[512,512]{1,0:T(8,128)(2,1)S(1)}, bf16[512,512]{1,0:T(8,128)(2,1)S(1)}, u32[]{:S(2)}, u32[]{:S(2)}) collective-permute-start(bf16[512,512]{1,0:T(8,128)(2,1)S(1)} %get-tuple-element.87), channel_id=1, source_target_pairs={{0,1},{3,2},{4,5},{7,6},{8,9},{11,10},{12,13},{15,14},{16,17},{19,... | collective-permute-start | bytes 1572872 | tf_op jit(solution)/shard_map/ppermute | solution.py:281
  60.7 12.7 %collective-permute-start.11 = (bf16[512,512]{1,0:T(8,128)(2,1)}, bf16[512,512]{1,0:T(8,128)(2,1)S(1)}, u32[]{:S(2)}, u32[]{:S(2)}) collective-permute-start(bf16[512,512]{1,0:T(8,128)(2,1)} %collective-permute-done.10), channel_id=1, source_target_pairs={{0,16},{16,0},{1,17},{17,1},{2,18},{18,2},{3,19},{19,3},{4,20},{20... | collective-permute-start | bytes 1572872 | tf_op jit(solution)/shard_map/ppermute | solution.py:289
  62.6 21.4 %collective-permute-start.9 = (bf16[160,2048]{1,0:T(8,128)(2,1)S(1)}, bf16[160,2048]{1,0:T(8,128)(2,1)S(1)}, u32[]{:S(2)}, u32[]{:S(2)}) collective-permute-start(bf16[160,2048]{1,0:T(8,128)(2,1)S(1)} %pad_maximum_fusion.24), channel_id=1, source_target_pairs={{0,4},{4,0},{8,12},{12,8},{1,5},{5,1},{9,13},{13,9},{2,6},{6,2},{1... | collective-permute-start | bytes 1966088 | tf_op jit(solution)/shard_map/ppermute | solution.py:315
  80.7 11.9 %collective-permute-start.13 = (bf16[512,512]{1,0:T(8,128)(2,1)S(1)}, bf16[512,512]{1,0:T(8,128)(2,1)S(1)}, u32[]{:S(2)}, u32[]{:S(2)}) collective-permute-start(bf16[512,512]{1,0:T(8,128)(2,1)S(1)} %collective-permute-done.12), channel_id=1, source_target_pairs={{0,16},{16,0},{1,17},{17,1},{2,18},{18,2},{3,19},{19,3},{4,20},{20... | collective-permute-start | bytes 1572872 | tf_op jit(solution)/shard_map/ppermute | solution.py:289
  96.3 10.7 %collective-permute-start.16 = (bf16[512,512]{1,0:T(8,128)(2,1)S(1)}, bf16[512,512]{1,0:T(8,128)(2,1)S(1)}, u32[]{:S(2)}, u32[]{:S(2)}) collective-permute-start(bf16[512,512]{1,0:T(8,128)(2,1)S(1)} %collective-permute-done.15), channel_id=1, source_target_pairs={{0,16},{16,0},{1,17},{17,1},{2,18},{18,2},{3,19},{19,3},{4,20},{20... | collective-permute-start | bytes 1572872 | tf_op jit(solution)/shard_map/ppermute | solution.py:289
  110.6 21.7 %collective-permute-start.17 = (bf16[320,2048]{1,0:T(8,128)(2,1)}, bf16[320,2048]{1,0:T(8,128)(2,1)}, u32[]{:S(2)}, u32[]{:S(2)}) collective-permute-start(bf16[320,2048]{1,0:T(8,128)(2,1)} %pad_maximum_fusion.9), channel_id=1, source_target_pairs={{0,4},{4,0},{8,12},{12,8},{1,5},{5,1},{9,13},{13,9},{2,6},{6,2},{1... | collective-permute-start | bytes 3932168 | tf_op jit(solution)/shard_map/ppermute | solution.py:377
  111.9 16.1 %collective-permute-start.20 = (bf16[512,512]{1,0:T(8,128)(2,1)}, bf16[512,512]{1,0:T(8,128)(2,1)S(1)}, u32[]{:S(2)}, u32[]{:S(2)}) collective-permute-start(bf16[512,512]{1,0:T(8,128)(2,1)} %get-tuple-element.97), channel_id=1, source_target_pairs={{0,1},{3,2},{4,5},{7,6},{8,9},{11,10},{12,13},{15,14},{16,17},{19,... | collective-permute-start | bytes 1572872 | tf_op jit(solution)/shard_map/ppermute | solution.py:281
  116.5 20.4 %collective-permute-start.18 = (bf16[320,512]{1,0:T(8,128)(2,1)}, bf16[320,512]{1,0:T(8,128)(2,1)S(1)}, u32[]{:S(2)}, u32[]{:S(2)}) collective-permute-start(bf16[320,512]{1,0:T(8,128)(2,1)} %convolution_convert_fusion.8), channel_id=1, source_target_pairs={{1,2},{2,1},{5,6},{6,5},{9,10},{10,9},{13,14},{14,13},{17,18},{18,... | collective-permute-start | bytes 983048 | tf_op jit(solution)/shard_map/ppermute | solution.py:340
  118.4 19.3 %collective-permute-start.19 = (bf16[320,512]{1,0:T(8,128)(2,1)}, bf16[320,512]{1,0:T(8,128)(2,1)S(1)}, u32[]{:S(2)}, u32[]{:S(2)}) collective-permute-start(bf16[320,512]{1,0:T(8,128)(2,1)} %convolution_convert_fusion.7), channel_id=1, source_target_pairs={{1,2},{2,1},{5,6},{6,5},{9,10},{10,9},{13,14},{14,13},{17,18},{18,... | collective-permute-start | bytes 983048 | tf_op jit(solution)/shard_map/ppermute | solution.py:345
  119.1 28.5 %collective-permute-start.22 = (bf16[640,512]{1,0:T(8,128)(2,1)S(1)}, bf16[640,512]{1,0:T(8,128)(2,1)S(1)}, u32[]{:S(2)}, u32[]{:S(2)}) collective-permute-start(bf16[640,512]{1,0:T(8,128)(2,1)S(1)} %copy-done.23), channel_id=1, source_target_pairs={{1,2},{2,1},{5,6},{6,5},{9,10},{10,9},{13,14},{14,13},{17,18},{18,... | collective-permute-start | bytes 1966088 | tf_op jit(solution)/shard_map/ppermute | solution.py:367
  128.0 16.6 %collective-permute-start.23 = (bf16[512,512]{1,0:T(8,128)(2,1)S(1)}, bf16[512,512]{1,0:T(8,128)(2,1)S(1)}, u32[]{:S(2)}, u32[]{:S(2)}) collective-permute-start(bf16[512,512]{1,0:T(8,128)(2,1)S(1)} %copy-done.17), channel_id=1, source_target_pairs={{0,1},{3,2},{4,5},{7,6},{8,9},{11,10},{12,13},{15,14},{16,17},{19,... | collective-permute-start | bytes 1572872 | tf_op jit(solution)/shard_map/ppermute | solution.py:281
  132.4 13.7 %collective-permute-start.21 = (bf16[512,512]{1,0:T(8,128)(2,1)S(1)}, bf16[512,512]{1,0:T(8,128)(2,1)S(1)}, u32[]{:S(2)}, u32[]{:S(2)}) collective-permute-start(bf16[512,512]{1,0:T(8,128)(2,1)S(1)} %collective-permute-done.20), channel_id=1, source_target_pairs={{0,16},{16,0},{1,17},{17,1},{2,18},{18,2},{3,19},{19,3},{4,20},{20... | collective-permute-start | bytes 1572872 | tf_op jit(solution)/shard_map/ppermute | solution.py:289
  136.8 24.6 %collective-permute-start.25 = (bf16[640,512]{1,0:T(8,128)(2,1)S(1)}, bf16[640,512]{1,0:T(8,128)(2,1)S(1)}, u32[]{:S(2)}, u32[]{:S(2)}) collective-permute-start(bf16[640,512]{1,0:T(8,128)(2,1)S(1)} %copy-done.22), channel_id=1, source_target_pairs={{1,2},{2,1},{5,6},{6,5},{9,10},{10,9},{13,14},{14,13},{17,18},{18,... | collective-permute-start | bytes 1966088 | tf_op jit(solution)/shard_map/ppermute | solution.py:367
  137.7 19.7 %collective-permute-start.28 = (bf16[512,512]{1,0:T(8,128)(2,1)S(1)}, bf16[512,512]{1,0:T(8,128)(2,1)S(1)}, u32[]{:S(2)}, u32[]{:S(2)}) collective-permute-start(bf16[512,512]{1,0:T(8,128)(2,1)S(1)} %copy-done.16), channel_id=1, source_target_pairs={{0,1},{3,2},{4,5},{7,6},{8,9},{11,10},{12,13},{15,14},{16,17},{19,... | collective-permute-start | bytes 1572872 | tf_op jit(solution)/shard_map/ppermute | solution.py:281
  144.6 14.0 %collective-permute-start.24 = (bf16[512,512]{1,0:T(8,128)(2,1)S(1)}, bf16[512,512]{1,0:T(8,128)(2,1)S(1)}, u32[]{:S(2)}, u32[]{:S(2)}) collective-permute-start(bf16[512,512]{1,0:T(8,128)(2,1)S(1)} %collective-permute-done.23), channel_id=1, source_target_pairs={{0,16},{16,0},{1,17},{17,1},{2,18},{18,2},{3,19},{19,3},{4,20},{20... | collective-permute-start | bytes 1572872 | tf_op jit(solution)/shard_map/ppermute | solution.py:289
  149.3 26.7 %collective-permute-start.31 = (bf16[640,512]{1,0:T(8,128)(2,1)S(1)}, bf16[640,512]{1,0:T(8,128)(2,1)S(1)}, u32[]{:S(2)}, u32[]{:S(2)}) collective-permute-start(bf16[640,512]{1,0:T(8,128)(2,1)S(1)} %convolution_convert_fusion.2), channel_id=1, source_target_pairs={{1,2},{2,1},{5,6},{6,5},{9,10},{10,9},{13,14},{14,13},{17,18},{18,... | collective-permute-start | bytes 1966088 | tf_op jit(solution)/shard_map/ppermute | solution.py:367
  150.2 15.7 %collective-permute-start.32 = (bf16[512,512]{1,0:T(8,128)(2,1)S(1)}, bf16[512,512]{1,0:T(8,128)(2,1)S(1)}, u32[]{:S(2)}, u32[]{:S(2)}) collective-permute-start(bf16[512,512]{1,0:T(8,128)(2,1)S(1)} %copy-done.15), channel_id=1, source_target_pairs={{0,1},{3,2},{4,5},{7,6},{8,9},{11,10},{12,13},{15,14},{16,17},{19,... | collective-permute-start | bytes 1572872 | tf_op jit(solution)/shard_map/ppermute | solution.py:281
  157.4 11.8 %collective-permute-start.29 = (bf16[512,512]{1,0:T(8,128)(2,1)S(1)}, bf16[512,512]{1,0:T(8,128)(2,1)S(1)}, u32[]{:S(2)}, u32[]{:S(2)}) collective-permute-start(bf16[512,512]{1,0:T(8,128)(2,1)S(1)} %collective-permute-done.28), channel_id=1, source_target_pairs={{0,16},{16,0},{1,17},{17,1},{2,18},{18,2},{3,19},{19,3},{4,20},{20... | collective-permute-start | bytes 1572872 | tf_op jit(solution)/shard_map/ppermute | solution.py:289
  158.6 13.3 %collective-permute-start.27 = (bf16[320,512]{1,0:T(8,128)(2,1)S(1)}, bf16[320,512]{1,0:T(8,128)(2,1)S(1)}, u32[]{:S(2)}, u32[]{:S(2)}) collective-permute-start(bf16[320,512]{1,0:T(8,128)(2,1)S(1)} %slice.93), channel_id=1, source_target_pairs={{1,0},{2,3},{5,4},{6,7},{9,8},{10,11},{13,12},{14,15},{17,16},{18,... | collective-permute-start | bytes 983048 | tf_op jit(solution)/shard_map/ppermute | solution.py:386
  161.5 12.9 %collective-permute-start.30 = (bf16[320,512]{1,0:T(8,128)(2,1)S(1)}, bf16[320,512]{1,0:T(8,128)(2,1)S(1)}, u32[]{:S(2)}, u32[]{:S(2)}) collective-permute-start(bf16[320,512]{1,0:T(8,128)(2,1)S(1)} %slice.95), channel_id=1, source_target_pairs={{1,0},{2,3},{5,4},{6,7},{9,8},{10,11},{13,12},{14,15},{17,16},{18,... | collective-permute-start | bytes 983048 | tf_op jit(solution)/shard_map/ppermute | solution.py:386
  165.9 15.3 %collective-permute-start.34 = (bf16[640,512]{1,0:T(8,128)(2,1)S(1)}, bf16[640,512]{1,0:T(8,128)(2,1)S(1)}, u32[]{:S(2)}, u32[]{:S(2)}) collective-permute-start(bf16[640,512]{1,0:T(8,128)(2,1)S(1)} %convolution_convert_fusion.1), channel_id=1, source_target_pairs={{1,2},{2,1},{5,6},{6,5},{9,10},{10,9},{13,14},{14,13},{17,18},{18,... | collective-permute-start | bytes 1966088 | tf_op jit(solution)/shard_map/ppermute | solution.py:367
  172.0 27.9 %collective-permute-start.36 = (bf16[640,512]{1,0:T(8,128)(2,1)S(1)}, bf16[640,512]{1,0:T(8,128)(2,1)S(1)}, u32[]{:S(2)}, u32[]{:S(2)}) collective-permute-start(bf16[640,512]{1,0:T(8,128)(2,1)S(1)} %convolution_convert_fusion), channel_id=1, source_target_pairs={{1,2},{2,1},{5,6},{6,5},{9,10},{10,9},{13,14},{14,13},{17,18},{18,... | collective-permute-start | bytes 1966088 | tf_op jit(solution)/shard_map/ppermute | solution.py:367
  176.0 40.2 %collective-permute-start.40 = (bf16[128,1024]{1,0:T(8,128)(2,1)S(1)}, bf16[128,1024]{1,0:T(8,128)(2,1)S(1)}, u32[]{:S(2)}, u32[]{:S(2)}) collective-permute-start(bf16[128,1024]{1,0:T(8,128)(2,1)S(1)} %get-tuple-element.175), channel_id=1, source_target_pairs={{0,12},{12,0},{4,8},{8,4},{1,13},{13,1},{5,9},{9,5},{2,14},{14,2},... | collective-permute-start | bytes 786440 | tf_op jit(solution)/shard_map/ppermute | solution.py:403
  179.5 36.8 %collective-permute-start.38 = (bf16[128,1024]{1,0:T(8,128)(2,1)S(1)}, bf16[128,1024]{1,0:T(8,128)(2,1)S(1)}, u32[]{:S(2)}, u32[]{:S(2)}) collective-permute-start(bf16[128,1024]{1,0:T(8,128)(2,1)S(1)} %get-tuple-element.177), channel_id=1, source_target_pairs={{0,4},{4,0},{8,12},{12,8},{1,5},{5,1},{9,13},{13,9},{2,6},{6,2},{1... | collective-permute-start | bytes 786440 | tf_op jit(solution)/shard_map/ppermute | solution.py:404
  181.2 17.8 %collective-permute-start.35 = (bf16[320,512]{1,0:T(8,128)(2,1)S(1)}, bf16[320,512]{1,0:T(8,128)(2,1)S(1)}, u32[]{:S(2)}, u32[]{:S(2)}) collective-permute-start(bf16[320,512]{1,0:T(8,128)(2,1)S(1)} %slice.97), channel_id=1, source_target_pairs={{1,0},{2,3},{5,4},{6,7},{9,8},{10,11},{13,12},{14,15},{17,16},{18,... | collective-permute-start | bytes 983048 | tf_op jit(solution)/shard_map/ppermute | solution.py:386
  184.0 33.9 %collective-permute-start.39 = (bf16[128,1024]{1,0:T(8,128)(2,1)S(1)}, bf16[128,1024]{1,0:T(8,128)(2,1)S(1)}, u32[]{:S(2)}, u32[]{:S(2)}) collective-permute-start(bf16[128,1024]{1,0:T(8,128)(2,1)S(1)} %get-tuple-element.176), channel_id=1, source_target_pairs={{0,8},{8,0},{4,12},{12,4},{1,9},{9,1},{5,13},{13,5},{2,10},{10,2},... | collective-permute-start | bytes 786440 | tf_op jit(solution)/shard_map/ppermute | solution.py:402
  198.9 14.9 %collective-permute-start.42 = (bf16[320,512]{1,0:T(8,128)(2,1)S(1)}, bf16[320,512]{1,0:T(8,128)(2,1)S(1)}, u32[]{:S(2)}, u32[]{:S(2)}) collective-permute-start(bf16[320,512]{1,0:T(8,128)(2,1)S(1)} %convolution_convert_fusion.6), channel_id=1, source_target_pairs={{1,2},{2,1},{5,6},{6,5},{9,10},{10,9},{13,14},{14,13},{17,18},{18,... | collective-permute-start | bytes 983048 | tf_op jit(solution)/shard_map/ppermute | solution.py:355
  199.9 13.1 %collective-permute-start.41 = (bf16[320,512]{1,0:T(8,128)(2,1)S(1)}, bf16[320,512]{1,0:T(8,128)(2,1)S(1)}, u32[]{:S(2)}, u32[]{:S(2)}) collective-permute-start(bf16[320,512]{1,0:T(8,128)(2,1)S(1)} %slice.101), channel_id=1, source_target_pairs={{1,0},{2,3},{5,4},{6,7},{9,8},{10,11},{13,12},{14,15},{17,16},{18,... | collective-permute-start | bytes 983048 | tf_op jit(solution)/shard_map/ppermute | solution.py:386
  213.0 12.8 %collective-permute-start.43 = (bf16[320,512]{1,0:T(8,128)(2,1)S(1)}, bf16[320,512]{1,0:T(8,128)(2,1)S(1)}, u32[]{:S(2)}, u32[]{:S(2)}) collective-permute-start(bf16[320,512]{1,0:T(8,128)(2,1)S(1)} %convolution_convert_fusion.5), channel_id=1, source_target_pairs={{1,2},{2,1},{5,6},{6,5},{9,10},{10,9},{13,14},{14,13},{17,18},{18,... | collective-permute-start | bytes 983048 | tf_op jit(solution)/shard_map/ppermute | solution.py:357
  216.2 19.7 %collective-permute-start.56 = (bf16[128,1024]{1,0:T(8,128)(2,1)S(1)}, bf16[128,1024]{1,0:T(8,128)(2,1)S(1)}, u32[]{:S(2)}, u32[]{:S(2)}) collective-permute-start(bf16[128,1024]{1,0:T(8,128)(2,1)S(1)} %get-tuple-element.171), channel_id=1, source_target_pairs={{0,12},{12,0},{4,8},{8,4},{1,13},{13,1},{5,9},{9,5},{2,14},{14,2},... | collective-permute-start | bytes 786440 | tf_op jit(solution)/shard_map/ppermute | solution.py:403
  216.3 21.1 %collective-permute-start.54 = (bf16[128,1024]{1,0:T(8,128)(2,1)S(1)}, bf16[128,1024]{1,0:T(8,128)(2,1)S(1)}, u32[]{:S(2)}, u32[]{:S(2)}) collective-permute-start(bf16[128,1024]{1,0:T(8,128)(2,1)S(1)} %get-tuple-element.173), channel_id=1, source_target_pairs={{0,4},{4,0},{8,12},{12,8},{1,5},{5,1},{9,13},{13,9},{2,6},{6,2},{1... | collective-permute-start | bytes 786440 | tf_op jit(solution)/shard_map/ppermute | solution.py:404
  217.9 19.9 %collective-permute-start.55 = (bf16[128,1024]{1,0:T(8,128)(2,1)S(1)}, bf16[128,1024]{1,0:T(8,128)(2,1)S(1)}, u32[]{:S(2)}, u32[]{:S(2)}) collective-permute-start(bf16[128,1024]{1,0:T(8,128)(2,1)S(1)} %get-tuple-element.172), channel_id=1, source_target_pairs={{0,8},{8,0},{4,12},{12,4},{1,9},{9,1},{5,13},{13,5},{2,10},{10,2},... | collective-permute-start | bytes 786440 | tf_op jit(solution)/shard_map/ppermute | solution.py:402
  224.2 11.7 %collective-permute-start.44 = (bf16[320,512]{1,0:T(8,128)(2,1)S(1)}, bf16[320,512]{1,0:T(8,128)(2,1)S(1)}, u32[]{:S(2)}, u32[]{:S(2)}) collective-permute-start(bf16[320,512]{1,0:T(8,128)(2,1)S(1)} %fusion.6), channel_id=1, source_target_pairs={{1,0},{2,3},{5,4},{6,7},{9,8},{10,11},{13,12},{14,15},{17,16},{18,... | collective-permute-start | bytes 983048 | tf_op jit(solution)/shard_map/ppermute | solution.py:445
  225.8 12.4 %collective-permute-start.53 = (bf16[128,512]{1,0:T(8,128)(2,1)S(1)}, bf16[128,512]{1,0:T(8,128)(2,1)S(1)}, u32[]{:S(2)}, u32[]{:S(2)}) collective-permute-start(bf16[128,512]{1,0:T(8,128)(2,1)S(1)} %get-tuple-element.181), channel_id=1, source_target_pairs={{0,12},{12,0},{4,8},{8,4},{1,13},{13,1},{5,9},{9,5},{2,14},{14,2},... | collective-permute-start | bytes 393224 | tf_op jit(solution)/shard_map/ppermute | solution.py:403
  237.8 16.9 %collective-permute-start.48 = (bf16[128,512]{1,0:T(8,128)(2,1)S(1)}, bf16[128,512]{1,0:T(8,128)(2,1)S(1)}, u32[]{:S(2)}, u32[]{:S(2)}) collective-permute-start(bf16[128,512]{1,0:T(8,128)(2,1)S(1)} %get-tuple-element.187), channel_id=1, source_target_pairs={{0,4},{4,0},{8,12},{12,8},{1,5},{5,1},{9,13},{13,9},{2,6},{6,2},{1... | collective-permute-start | bytes 393224 | tf_op jit(solution)/shard_map/ppermute | solution.py:404
  238.1 16.5 %collective-permute-start.49 = (bf16[128,512]{1,0:T(8,128)(2,1)S(1)}, bf16[128,512]{1,0:T(8,128)(2,1)S(1)}, u32[]{:S(2)}, u32[]{:S(2)}) collective-permute-start(bf16[128,512]{1,0:T(8,128)(2,1)S(1)} %get-tuple-element.186), channel_id=1, source_target_pairs={{0,8},{8,0},{4,12},{12,4},{1,9},{9,1},{5,13},{13,5},{2,10},{10,2},... | collective-permute-start | bytes 393224 | tf_op jit(solution)/shard_map/ppermute | solution.py:402
  239.7 18.2 %collective-permute-start.47 = (bf16[128,512]{1,0:T(8,128)(2,1)S(1)}, bf16[128,512]{1,0:T(8,128)(2,1)S(1)}, u32[]{:S(2)}, u32[]{:S(2)}) collective-permute-start(bf16[128,512]{1,0:T(8,128)(2,1)S(1)} %get-tuple-element.189), channel_id=1, source_target_pairs={{0,12},{12,0},{4,8},{8,4},{1,13},{13,1},{5,9},{9,5},{2,14},{14,2},... | collective-permute-start | bytes 393224 | tf_op jit(solution)/shard_map/ppermute | solution.py:403
  242.3 15.7 %collective-permute-start.45 = (bf16[128,512]{1,0:T(8,128)(2,1)S(1)}, bf16[128,512]{1,0:T(8,128)(2,1)S(1)}, u32[]{:S(2)}, u32[]{:S(2)}) collective-permute-start(bf16[128,512]{1,0:T(8,128)(2,1)S(1)} %get-tuple-element.191), channel_id=1, source_target_pairs={{0,4},{4,0},{8,12},{12,8},{1,5},{5,1},{9,13},{13,9},{2,6},{6,2},{1... | collective-permute-start | bytes 393224 | tf_op jit(solution)/shard_map/ppermute | solution.py:404
  244.1 13.8 %collective-permute-start.46 = (bf16[128,512]{1,0:T(8,128)(2,1)S(1)}, bf16[128,512]{1,0:T(8,128)(2,1)S(1)}, u32[]{:S(2)}, u32[]{:S(2)}) collective-permute-start(bf16[128,512]{1,0:T(8,128)(2,1)S(1)} %get-tuple-element.190), channel_id=1, source_target_pairs={{0,8},{8,0},{4,12},{12,4},{1,9},{9,1},{5,13},{13,5},{2,10},{10,2},... | collective-permute-start | bytes 393224 | tf_op jit(solution)/shard_map/ppermute | solution.py:402
  (43 other events, 431.2 us)

commit v4 on v3

--- a/solution.py
+++ b/solution.py
@@ -311,6 +311,7 @@
     far_pair = ordered_pair(from_far)
     far_rows = jnp.concatenate([far_pair, lax.ppermute(far_pair, "dp", beside)], 0)
     lines[3] = start_weight(3, far_pair)
+    near_others = lax.ppermute(near_pair, "dp", beside)
     outer_pair = ordered_pair(from_far_outer)
     far_outer_rows = jnp.concatenate([outer_pair, lax.ppermute(outer_pair, "dp", beside)], 0)
 
@@ -369,15 +370,17 @@
 
     last = send(1, last)
     lines[4] = start_weight(4, last)
-    near_outer_pair = ordered_pair(after(from_outer, last))
+    outer_pair = ordered_pair(after(from_outer, last))
     last = send(2, last)
     lines[5] = start_weight(5, last)
     shared[3] = share_weight(3, last)
-    near_pairs = jnp.concatenate([near_pair, after(near_outer_pair, last)], 0)
-    near_others = lax.ppermute(near_pairs, "dp", beside)
+    outer_pair = after(outer_pair, last)
     near_rows = jnp.concatenate(
-        [near_pair, near_others[:pair_total], near_outer_pair, near_others[pair_total:]], 0
-    )
+        [near_pair, near_others, outer_pair, lax.ppermute(outer_pair, "dp", beside)], 0
+    )
+    last = send(3, last)
+    lines[6] = start_weight(6, last)
+    shared[4] = share_weight(4, last)
 
     def finish(c, *order):
         rows = after(near_rows, *order)
@@ -428,26 +431,32 @@
         return cuts[0]
 
     final = chunks - 1
-    for i in range(final):
+
+    def finish_next(i, last):
         summed[i] = finish(i, last)
-        last = summed[i][0]
-        if i + 6 < chunks:
-            lines[i + 6] = start_weight(i + 6, last)
-        if i + 4 < chunks:
-            shared[i + 4] = share_weight(i + 4, last)
-        if i + 3 < final:
-            last = send(i + 3, last)
-        elif i + 3 == final:
-            last = send_last(final, last)
-        if i > 0:
-            last = hand_batch(i - 1, last)
+        return summed[i][0]
+
+    last = finish_next(0, last)
+    last = finish_next(1, last)
+    shared[5] = share_weight(5, last)
+    last = send(4, last)
+    last = finish_next(2, last)
+    shared[6] = share_weight(6, last)
+    last = send(5, last)
+    last = finish_next(3, last)
+    last = hand_batch(1, last)
+    last = finish_next(4, last)
+    last = send_last(final, last)
+    last = hand_batch(3, last)
+    last = finish_next(5, last)
     outer_sum = finish_half(final, 0, last)
     handed = lax.ppermute(outer_sum, "fsdp", outward)
-    last = finish_tail(outer_sum)
-    last = hand_batch(final - 1, last)
+    last = hand_batch(4, outer_sum)
+    last = finish_tail(last)
     own_sum = finish_half(final, 1, last)
     summed[final] = own_sum, handed
-    last = hand_batch(final, own_sum)
+    last = hand_batch(final - 1, own_sum)
+    last = hand_batch(final, last)
     while pending:
         last = finish_tail(last)
     return made[0], low, made[1]

time: 263 us -> 257 us (0.977)
  waiting for transfers between devices: 85.9 us -> 104 us
  local copies, waits for them, and re-layouts: 16.3 us -> 6.46 us
  starting transfers between devices: 97.1 us -> 89.4 us
  other arithmetic: 8.25 us -> 4.17 us
  matrix products: 30.1 us -> 26.4 us
    ppermute x7, waiting for transfers between devices: 24.8 us -> 37.5 us  [share_weight(): pieces.append(lax.ppermute(line, 'groups', pairs))]
    ppermute x6, waiting for transfers between devices: 25.3 us -> 36.7 us  [finish(): return (summed, lax.ppermute(summed[home_total:], 'fsdp', outward))]
    ppermute x4, waiting for transfers between devices: 4.25 us -> 14.6 us  [ordered_pair(): theirs = lax.ppermute(mine, 'dp', across)]
    ppermute x6, waiting for transfers between devices: 11.7 us -> 1.64 us  [start_weight(): return lax.ppermute(after(parts[c], *order), 'fsdp', inward)]
    ppermute x1, starting transfers between devices: 14.2 us -> 4.74 us  [plane_plan(): lines = {0: lax.ppermute(parts[0], 'fsdp', inward)}]
    ppermute x6, starting transfers between devices: 25.7 us -> 33 us  [start_weight(): return lax.ppermute(after(parts[c], *order), 'fsdp', inward)]
    ppermute x1, starting transfers between devices: 10.1 us -> 3.98 us  [plane_plan(): lax.ppermute(after(far_columns, near_columns), 'fsdp', crossing)]
    ppermute x1, waiting for transfers between devices: 5 us -> 0.01 us  [plane_plan(): lax.ppermute(after(far_columns, near_columns), 'fsdp', crossing)]
  transfers between devices with their start and end apart: 57 -> 58, of which waited for: 18 -> 16; matrix products, arithmetic and copies ran while one was open for 18% -> 13% of each run, Pallas kernels for 7% -> 7%
where the time goes in v4:
time: 257 us; the launch traced here: 255 us
  waiting for transfers between devices  104 us (40%)
  starting transfers between devices  89.4 us (35%)
  matrix products  26.4 us (10%)
  Pallas kernels  22.2 us (9%)
  local copies, waits for them, and re-layouts  6.46 us (3%)
  other arithmetic  4.17 us (2%)
    ppermute x7, waiting for transfers between devices, share_weight(): pieces.append(lax.ppermute(line, 'groups', pairs))  37.5 us
    ppermute x6, waiting for transfers between devices, finish(): return (summed, lax.ppermute(summed[home_total:], 'fsdp', outward))  36.7 us
    ppermute x6, starting transfers between devices, start_weight(): return lax.ppermute(after(parts[c], *order), 'fsdp', inward)  33 us
    pallas_call x5, Pallas kernels, tail(): pl.pallas_call(tail_kernel, name='tail', out_shape=(jax.ShapeDtypeStruct(...  21.2 us
    ppermute x4, waiting for transfers between devices, ordered_pair(): theirs = lax.ppermute(mine, 'dp', across)  14.6 us
    dot_general x9, matrix products, multiply(): product = jnp.dot(rows, weight, preferred_element_type=jnp.float32)  13 us
    ppermute x7, starting transfers between devices, share_weight(): pieces.append(lax.ppermute(line, 'groups', pairs))  10.8 us
    dot_general x6, matrix products, finish(): summed = jnp.dot(rows, weights[c], preferred_element_type=jnp.float32)  10.1 us
  transfers between devices with their start and end apart: 58, of which 16 were waited for; matrix products, arithmetic and copies ran while one was open for 13% of the time, Pallas kernels for 7%

profile of v4, /device:TPU:0, one launch (start us, length us, event | category | flops | bytes accessed | tf_op | source)
XLA Modules:
  0.0 255.5 jit_solution(12457761515486178909)
XLA Ops:
  3.1 3.1 %collective-permute-start = (bf16[48,2048]{1,0:T(8,128)(2,1)S(1)}, bf16[48,2048]{1,0:T(8,128)(2,1)}, u32[]{:S(2)}, u32[]{:S(2)}) collective-permute-start(bf16[48,2048]{1,0:T(8,128)(2,1)S(1)} %get-tuple-element.73), channel_id=1, source_target_pairs={{0,8},{8,0},{4,12},{12,4},{1,9},{9,1},{5,13},{13,5},{2,10},{10,2},... | collective-permute-start | bytes 589832 | tf_op jit(solution)/shard_map/ppermute | solution.py:269
  7.5 4.7 %collective-permute-start.11 = (bf16[512,512]{1,0:T(8,128)(2,1)S(1)}, bf16[512,512]{1,0:T(8,128)(2,1)}, u32[]{:S(2)}, u32[]{:S(2)}) collective-permute-start(bf16[512,512]{1,0:T(8,128)(2,1)S(1)} %get-tuple-element.167), channel_id=1, source_target_pairs={{0,1},{3,2},{4,5},{7,6},{8,9},{11,10},{12,13},{15,14},{16,17},{19,... | collective-permute-start | bytes 1572872 | tf_op jit(solution)/shard_map/ppermute | solution.py:268
  13.5 1.8 collective-permute-done.1
  17.8 1.8 collective-permute-start.2
  19.8 3.5 %collective-permute-start.4 = (bf16[80,2048]{1,0:T(8,128)(2,1)S(1)}, bf16[80,2048]{1,0:T(8,128)(2,1)S(1)}, u32[]{:S(2)}, u32[]{:S(2)}) collective-permute-start(bf16[80,2048]{1,0:T(8,128)(2,1)S(1)} %select_select_fusion), channel_id=1, source_target_pairs={{0,1},{3,2},{4,5},{7,6},{8,9},{11,10},{12,13},{15,14},{16,17},{19,... | collective-permute-start | bytes 983048 | tf_op jit(solution)/shard_map/ppermute | solution.py:310
  23.9 4.0 %collective-permute-start.8 = (bf16[80,2048]{1,0:T(8,128)(2,1)S(1)}, bf16[80,2048]{1,0:T(8,128)(2,1)S(1)}, u32[]{:S(2)}, u32[]{:S(2)}) collective-permute-start(bf16[80,2048]{1,0:T(8,128)(2,1)S(1)} %select_select_fusion.1), channel_id=1, source_target_pairs={{0,2},{3,1},{4,6},{7,5},{8,10},{11,9},{12,14},{15,13},{16,18},{19,... | collective-permute-start | bytes 983048 | tf_op jit(solution)/shard_map/ppermute | solution.py:307
  28.8 7.0 %collective-permute-done.6 = bf16[80,2048]{1,0:T(8,128)(2,1)S(1)} collective-permute-done((bf16[80,2048]{1,0:T(8,128)(2,1)S(1)}, bf16[80,2048]{1,0:T(8,128)(2,1)S(1)}, u32[]{:S(2)}, u32[]{:S(2)}) %collective-permute-start.6) | collective-permute-done | bytes 327712 | tf_op jit(solution)/shard_map/ppermute | solution.py:293
  36.2 2.1 constant_dynamic-slice_fusion.1
  38.7 13.0 %collective-permute-start.13 = (bf16[512,512]{1,0:T(8,128)(2,1)S(1)}, bf16[512,512]{1,0:T(8,128)(2,1)S(1)}, u32[]{:S(2)}, u32[]{:S(2)}) collective-permute-start(bf16[512,512]{1,0:T(8,128)(2,1)S(1)} %get-tuple-element.87), channel_id=1, source_target_pairs={{0,1},{3,2},{4,5},{7,6},{8,9},{11,10},{12,13},{15,14},{16,17},{19,... | collective-permute-start | bytes 1572872 | tf_op jit(solution)/shard_map/ppermute | solution.py:281
  53.3 1.6 collective-permute-start.12
  54.9 7.6 %collective-permute-done.9 = bf16[80,2048]{1,0:T(8,128)(2,1)S(1)} collective-permute-done((bf16[80,2048]{1,0:T(8,128)(2,1)S(1)}, bf16[80,2048]{1,0:T(8,128)(2,1)S(1)}, u32[]{:S(2)}, u32[]{:S(2)}) %collective-permute-start.9) | collective-permute-done | bytes 327712 | tf_op jit(solution)/shard_map/ppermute | solution.py:293
  62.5 1.5 collective-permute-start.19
  64.3 2.9 %collective-permute-done.12 = bf16[512,512]{1,0:T(8,128)(2,1)S(1)} collective-permute-done((bf16[512,512]{1,0:T(8,128)(2,1)}, bf16[512,512]{1,0:T(8,128)(2,1)S(1)}, u32[]{:S(2)}, u32[]{:S(2)}) %collective-permute-start.12) | collective-permute-done | bytes 524320 | tf_op jit(solution)/shard_map/ppermute | solution.py:289
  67.2 1.9 convolution_convert_fusion.8
  70.0 1.6 collective-permute-start.14
  71.7 1.9 convolution_convert_fusion.7
  73.6 1.6 collective-permute-done.16
  75.9 8.5 %collective-permute-done.14 = bf16[512,512]{1,0:T(8,128)(2,1)S(1)} collective-permute-done((bf16[512,512]{1,0:T(8,128)(2,1)S(1)}, bf16[512,512]{1,0:T(8,128)(2,1)S(1)}, u32[]{:S(2)}, u32[]{:S(2)}) %collective-permute-start.14) | collective-permute-done | bytes 524320 | tf_op jit(solution)/shard_map/ppermute | solution.py:289
  87.4 1.8 collective-permute-start.15
  89.6 8.3 %collective-permute-done.17 = bf16[512,512]{1,0:T(8,128)(2,1)S(1)} collective-permute-done((bf16[512,512]{1,0:T(8,128)(2,1)S(1)}, bf16[512,512]{1,0:T(8,128)(2,1)S(1)}, u32[]{:S(2)}, u32[]{:S(2)}) %collective-permute-start.17) | collective-permute-done | bytes 524320 | tf_op jit(solution)/shard_map/ppermute | solution.py:289
  97.9 4.0 %collective-permute-start.25 = (bf16[512,512]{1,0:T(8,128)(2,1)S(1)}, bf16[512,512]{1,0:T(8,128)(2,1)S(1)}, u32[]{:S(2)}, u32[]{:S(2)}) collective-permute-start(bf16[512,512]{1,0:T(8,128)(2,1)S(1)} %get-tuple-element.101), channel_id=1, source_target_pairs={{0,1},{3,2},{4,5},{7,6},{8,9},{11,10},{12,13},{15,14},{16,17},{19,... | collective-permute-start | bytes 1572872 | tf_op jit(solution)/shard_map/ppermute | solution.py:281
  101.9 1.5 convolution_convert_fusion.3
  103.4 1.6 collective-permute-start.20
  105.2 10.3 %collective-permute-done.20 = bf16[512,512]{1,0:T(8,128)(2,1)S(1)} collective-permute-done((bf16[512,512]{1,0:T(8,128)(2,1)S(1)}, bf16[512,512]{1,0:T(8,128)(2,1)S(1)}, u32[]{:S(2)}, u32[]{:S(2)}) %collective-permute-start.20) | collective-permute-done | bytes 524320 | tf_op jit(solution)/shard_map/ppermute | solution.py:289
  118.5 6.0 %collective-permute-start.28 = (bf16[512,512]{1,0:T(8,128)(2,1)S(1)}, bf16[512,512]{1,0:T(8,128)(2,1)S(1)}, u32[]{:S(2)}, u32[]{:S(2)}) collective-permute-start(bf16[512,512]{1,0:T(8,128)(2,1)S(1)} %get-tuple-element.105), channel_id=1, source_target_pairs={{0,1},{3,2},{4,5},{7,6},{8,9},{11,10},{12,13},{15,14},{16,17},{19,... | collective-permute-start | bytes 1572872 | tf_op jit(solution)/shard_map/ppermute | solution.py:281
  125.3 1.6 collective-permute-start.26
  126.9 2.6 %fusion = bf16[640,512]{1,0:T(8,128)(2,1)S(1)} fusion(bf16[640,2048]{1,0:T(8,128)(2,1)S(1)} %constant_dynamic-update-slice_fusion.6, bf16[320,512]{1,0:T(8,128)(2,1)S(1)} %collective-permute-done.22, bf16[320,512]{1,0:T(8,128)(2,1)S(1)} %collective-permute-done.21, bf16[512,512]{1,0:T(8,128)(2,1)S(1)} %collective-permute-done.12, ...), kind=kOutput, calls=%fused_computation.14 | convolution fusion | flops 1350434816 | bytes 6029312 | tf_op jit(solution)/shard_map/dot_general | solution.py:387
  129.4 7.2 %collective-permute-start.38 = (bf16[512,512]{1,0:T(8,128)(2,1)S(1)}, bf16[512,512]{1,0:T(8,128)(2,1)S(1)}, u32[]{:S(2)}, u32[]{:S(2)}) collective-permute-start(bf16[512,512]{1,0:T(8,128)(2,1)S(1)} %get-tuple-element.112), channel_id=1, source_target_pairs={{0,1},{3,2},{4,5},{7,6},{8,9},{11,10},{12,13},{15,14},{16,17},{19,... | collective-permute-start | bytes 1572872 | tf_op jit(solution)/shard_map/ppermute | solution.py:281
  136.6 1.5 fusion.1
  139.8 1.6 collective-permute-start.29
  144.2 1.5 fusion.2
  146.4 7.6 %collective-permute-done.29 = bf16[512,512]{1,0:T(8,128)(2,1)S(1)} collective-permute-done((bf16[512,512]{1,0:T(8,128)(2,1)S(1)}, bf16[512,512]{1,0:T(8,128)(2,1)S(1)}, u32[]{:S(2)}, u32[]{:S(2)}) %collective-permute-start.29) | collective-permute-done | bytes 524320 | tf_op jit(solution)/shard_map/ppermute | solution.py:289
  158.3 1.5 fusion.3
  161.0 1.6 collective-permute-start.33
  162.6 1.5 fusion.4
  167.1 19.1 %collective-permute-done.40 = bf16[320,512]{1,0:T(8,128)(2,1)S(1)} collective-permute-done((bf16[320,512]{1,0:T(8,128)(2,1)S(1)}, bf16[320,512]{1,0:T(8,128)(2,1)S(1)}, u32[]{:S(2)}, u32[]{:S(2)}) %collective-permute-start.40) | collective-permute-done | bytes 327712 | tf_op jit(solution)/shard_map/ppermute | solution.py:389
  187.8 1.5 fusion.5
  191.6 15.2 %collective-permute-done.36 = bf16[320,512]{1,0:T(8,128)(2,1)S(1)} collective-permute-done((bf16[320,512]{1,0:T(8,128)(2,1)S(1)}, bf16[320,512]{1,0:T(8,128)(2,1)S(1)}, u32[]{:S(2)}, u32[]{:S(2)}) %collective-permute-start.36) | collective-permute-done | bytes 327712 | tf_op jit(solution)/shard_map/ppermute | solution.py:389
  210.1 5.7 %tail.5 = (bf16[128,14336]{1,0:T(8,128)(2,1)}, f32[32,14336]{1,0:T(8,128)}, f32[128,32]{1,0:T(8,128)S(1)}) custom-call(s32[4]{0:T(128)S(1)} %xor_multiply_fusion.slots_ref, s32[1]{0:T(128)} %copy.35.counts_ref, bf16[128,1024]{1,0:T(8,128)(2,1)S(1)} %get-tuple-element.175.own_ref, bf16[128,1024]{1,0:T(8,128)(2,1)S(1)} %collective-permute-done.32.beside_ref, ...), custom_call_target="tpu_custom_call" | custom-call | flops 234881024 | bytes 4194304 | tf_op jit(solution)/shard_map/tail/pallas_call | solution.py:143
  218.2 2.4 collective-permute-done.45
  220.7 7.0 %collective-permute-done.44 = bf16[320,512]{1,0:T(8,128)(2,1)S(1)} collective-permute-done((bf16[320,512]{1,0:T(8,128)(2,1)S(1)}, bf16[320,512]{1,0:T(8,128)(2,1)S(1)}, u32[]{:S(2)}, u32[]{:S(2)}) %collective-permute-start.44) | collective-permute-done | bytes 327712 | tf_op jit(solution)/shard_map/ppermute | solution.py:453
  228.6 1.7 collective-permute-start.51
  231.6 2.0 collective-permute-done.53.across_ref
  233.6 1.6 collective-permute-done.54.diagonal_ref
  238.8 5.8 %tail.6 = (bf16[128,14336]{1,0:T(8,128)(2,1)}, f32[32,14336]{1,0:T(8,128)}, f32[128,32]{1,0:T(8,128)S(1)}) custom-call(s32[4]{0:T(128)S(1)} %xor_multiply_fusion.slots_ref, s32[1]{0:T(128)} %copy.35.counts_ref, bf16[128,1024]{1,0:T(8,128)(2,1)S(1)} %get-tuple-element.171.own_ref, ...), custom_call_target="tpu_custom_call", output_to_operand_aliasing={{0}: (11, {}), {1}: (12, {})} | custom-call | flops 234881024 | bytes 4194304 | tf_op jit(solution)/shard_map/tail/pallas_call | solution.py:143
  244.6 3.2 %tail.7 = (bf16[128,14336]{1,0:T(8,128)(2,1)}, f32[32,14336]{1,0:T(8,128)}, f32[128,32]{1,0:T(8,128)S(1)}) custom-call(s32[4]{0:T(128)S(1)} %xor_multiply_fusion.slots_ref, s32[1]{0:T(128)} %copy.35.counts_ref, bf16[128,512]{1,0:T(8,128)(2,1)S(1)} %get-tuple-element.181.own_ref, ...), custom_call_target="tpu_custom_call", output_to_operand_aliasing={{0}: (11, {}), {1}: (12, {})} | custom-call | flops 117440512 | bytes 2097152 | tf_op jit(solution)/shard_map/tail/pallas_call | solution.py:143
  247.8 3.3 %tail.8 = (bf16[128,14336]{1,0:T(8,128)(2,1)}, f32[32,14336]{1,0:T(8,128)}, f32[128,32]{1,0:T(8,128)S(1)}) custom-call(s32[4]{0:T(128)S(1)} %xor_multiply_fusion.slots_ref, s32[1]{0:T(128)} %copy.35.counts_ref, bf16[128,512]{1,0:T(8,128)(2,1)S(1)} %get-tuple-element.185.own_ref, ...), custom_call_target="tpu_custom_call", output_to_operand_aliasing={{0}: (11, {}), {1}: (12, {})} | custom-call | flops 117440512 | bytes 2097152 | tf_op jit(solution)/shard_map/tail/pallas_call | solution.py:143
  251.1 3.3 %tail.9 = (bf16[128,14336]{1,0:T(8,128)(2,1)}, f32[32,14336]{1,0:T(8,128)}, f32[128,32]{1,0:T(8,128)S(1)}) custom-call(s32[4]{0:T(128)S(1)} %xor_multiply_fusion.slots_ref, s32[1]{0:T(128)} %copy.35.counts_ref, bf16[128,512]{1,0:T(8,128)(2,1)S(1)} %get-tuple-element.189.own_ref, ...), custom_call_target="tpu_custom_call", output_to_operand_aliasing={{0}: (11, {}), {1}: (12, {})} | custom-call | flops 117440512 | bytes 2097152 | tf_op jit(solution)/shard_map/tail/pallas_call | solution.py:143
  (166 shorter events, 49.8 us)
Async XLA Ops:
  3.1 13.4 %collective-permute-start = (bf16[48,2048]{1,0:T(8,128)(2,1)S(1)}, bf16[48,2048]{1,0:T(8,128)(2,1)}, u32[]{:S(2)}, u32[]{:S(2)}) collective-permute-start(bf16[48,2048]{1,0:T(8,128)(2,1)S(1)} %get-tuple-element.73), channel_id=1, source_target_pairs={{0,8},{8,0},{4,12},{12,4},{1,9},{9,1},{5,13},{13,5},{2,10},{10,2},... | collective-permute-start | bytes 589832 | tf_op jit(solution)/shard_map/ppermute | solution.py:269
  7.5 31.2 %collective-permute-start.11 = (bf16[512,512]{1,0:T(8,128)(2,1)S(1)}, bf16[512,512]{1,0:T(8,128)(2,1)}, u32[]{:S(2)}, u32[]{:S(2)}) collective-permute-start(bf16[512,512]{1,0:T(8,128)(2,1)S(1)} %get-tuple-element.167), channel_id=1, source_target_pairs={{0,1},{3,2},{4,5},{7,6},{8,9},{11,10},{12,13},{15,14},{16,17},{19,... | collective-permute-start | bytes 1572872 | tf_op jit(solution)/shard_map/ppermute | solution.py:268
  17.8 10.1 %collective-permute-start.2 = (bf16[80,2048]{1,0:T(8,128)(2,1)S(1)}, bf16[80,2048]{1,0:T(8,128)(2,1)S(1)}, u32[]{:S(2)}, u32[]{:S(2)}) collective-permute-start(bf16[80,2048]{1,0:T(8,128)(2,1)S(1)} %select_select_fusion), channel_id=1, source_target_pairs={{0,8},{8,0},{4,12},{12,4},{1,9},{9,1},{5,13},{13,5},{2,10},{10,2},... | collective-permute-start | bytes 983048 | tf_op jit(solution)/shard_map/ppermute | solution.py:293
  19.8 67.7 %collective-permute-start.4 = (bf16[80,2048]{1,0:T(8,128)(2,1)S(1)}, bf16[80,2048]{1,0:T(8,128)(2,1)S(1)}, u32[]{:S(2)}, u32[]{:S(2)}) collective-permute-start(bf16[80,2048]{1,0:T(8,128)(2,1)S(1)} %select_select_fusion), channel_id=1, source_target_pairs={{0,1},{3,2},{4,5},{7,6},{8,9},{11,10},{12,13},{15,14},{16,17},{19,... | collective-permute-start | bytes 983048 | tf_op jit(solution)/shard_map/ppermute | solution.py:310
  23.9 27.8 %collective-permute-start.8 = (bf16[80,2048]{1,0:T(8,128)(2,1)S(1)}, bf16[80,2048]{1,0:T(8,128)(2,1)S(1)}, u32[]{:S(2)}, u32[]{:S(2)}) collective-permute-start(bf16[80,2048]{1,0:T(8,128)(2,1)S(1)} %select_select_fusion.1), channel_id=1, source_target_pairs={{0,2},{3,1},{4,6},{7,5},{8,10},{11,9},{12,14},{15,13},{16,18},{19,... | collective-permute-start | bytes 983048 | tf_op jit(solution)/shard_map/ppermute | solution.py:307
  28.8 24.3 %collective-permute-start.3 = (bf16[160,2048]{1,0:T(8,128)(2,1)S(1)}, bf16[160,2048]{1,0:T(8,128)(2,1)S(1)}, u32[]{:S(2)}, u32[]{:S(2)}) collective-permute-start(bf16[160,2048]{1,0:T(8,128)(2,1)S(1)} %pad_maximum_fusion.21), channel_id=1, source_target_pairs={{0,4},{4,0},{8,12},{12,8},{1,5},{5,1},{9,13},{13,9},{2,6},{6,2},{1... | collective-permute-start | bytes 1966088 | tf_op jit(solution)/shard_map/ppermute | solution.py:314
  36.1 17.2 %collective-permute-start.7 = (bf16[160,2048]{1,0:T(8,128)(2,1)S(1)}, bf16[160,2048]{1,0:T(8,128)(2,1)S(1)}, u32[]{:S(2)}, u32[]{:S(2)}) collective-permute-start(bf16[160,2048]{1,0:T(8,128)(2,1)S(1)} %pad_maximum_fusion.22), channel_id=1, source_target_pairs={{0,4},{4,0},{8,12},{12,8},{1,5},{5,1},{9,13},{13,9},{2,6},{6,2},{1... | collective-permute-start | bytes 1966088 | tf_op jit(solution)/shard_map/ppermute | solution.py:312
  38.7 30.3 %collective-permute-start.13 = (bf16[512,512]{1,0:T(8,128)(2,1)S(1)}, bf16[512,512]{1,0:T(8,128)(2,1)S(1)}, u32[]{:S(2)}, u32[]{:S(2)}) collective-permute-start(bf16[512,512]{1,0:T(8,128)(2,1)S(1)} %get-tuple-element.87), channel_id=1, source_target_pairs={{0,1},{3,2},{4,5},{7,6},{8,9},{11,10},{12,13},{15,14},{16,17},{19,... | collective-permute-start | bytes 1572872 | tf_op jit(solution)/shard_map/ppermute | solution.py:281
  51.8 23.5 %collective-permute-start.16 = (bf16[512,512]{1,0:T(8,128)(2,1)S(1)}, bf16[512,512]{1,0:T(8,128)(2,1)S(1)}, u32[]{:S(2)}, u32[]{:S(2)}) collective-permute-start(bf16[512,512]{1,0:T(8,128)(2,1)S(1)} %get-tuple-element.91), channel_id=1, source_target_pairs={{0,1},{3,2},{4,5},{7,6},{8,9},{11,10},{12,13},{15,14},{16,17},{19,... | collective-permute-start | bytes 1572872 | tf_op jit(solution)/shard_map/ppermute | solution.py:281
  53.3 13.8 %collective-permute-start.12 = (bf16[512,512]{1,0:T(8,128)(2,1)}, bf16[512,512]{1,0:T(8,128)(2,1)S(1)}, u32[]{:S(2)}, u32[]{:S(2)}) collective-permute-start(bf16[512,512]{1,0:T(8,128)(2,1)} %collective-permute-done.11), channel_id=1, source_target_pairs={{0,16},{16,0},{1,17},{17,1},{2,18},{18,2},{3,19},{19,3},{4,20},{20... | collective-permute-start | bytes 1572872 | tf_op jit(solution)/shard_map/ppermute | solution.py:289
  62.5 40.9 %collective-permute-start.19 = (bf16[512,512]{1,0:T(8,128)(2,1)S(1)}, bf16[512,512]{1,0:T(8,128)(2,1)S(1)}, u32[]{:S(2)}, u32[]{:S(2)}) collective-permute-start(bf16[512,512]{1,0:T(8,128)(2,1)S(1)} %get-tuple-element.96), channel_id=1, source_target_pairs={{0,1},{3,2},{4,5},{7,6},{8,9},{11,10},{12,13},{15,14},{16,17},{19,... | collective-permute-start | bytes 1572872 | tf_op jit(solution)/shard_map/ppermute | solution.py:281
  69.1 55.5 %collective-permute-start.21 = (bf16[320,512]{1,0:T(8,128)(2,1)S(1)}, bf16[320,512]{1,0:T(8,128)(2,1)S(1)}, u32[]{:S(2)}, u32[]{:S(2)}) collective-permute-start(bf16[320,512]{1,0:T(8,128)(2,1)S(1)} %convolution_convert_fusion.8), channel_id=1, source_target_pairs={{1,2},{2,1},{5,6},{6,5},{9,10},{10,9},{13,14},{14,13},{17,18},{18,... | collective-permute-start | bytes 983048 | tf_op jit(solution)/shard_map/ppermute | solution.py:341
  70.0 14.4 %collective-permute-start.14 = (bf16[512,512]{1,0:T(8,128)(2,1)S(1)}, bf16[512,512]{1,0:T(8,128)(2,1)S(1)}, u32[]{:S(2)}, u32[]{:S(2)}) collective-permute-start(bf16[512,512]{1,0:T(8,128)(2,1)S(1)} %collective-permute-done.13), channel_id=1, source_target_pairs={{0,16},{16,0},{1,17},{17,1},{2,18},{18,2},{3,19},{19,3},{4,20},{20... | collective-permute-start | bytes 1572872 | tf_op jit(solution)/shard_map/ppermute | solution.py:289
  75.2 50.0 %collective-permute-start.22 = (bf16[320,512]{1,0:T(8,128)(2,1)S(1)}, bf16[320,512]{1,0:T(8,128)(2,1)S(1)}, u32[]{:S(2)}, u32[]{:S(2)}) collective-permute-start(bf16[320,512]{1,0:T(8,128)(2,1)S(1)} %convolution_convert_fusion.7), channel_id=1, source_target_pairs={{1,2},{2,1},{5,6},{6,5},{9,10},{10,9},{13,14},{14,13},{17,18},{18,... | collective-permute-start | bytes 983048 | tf_op jit(solution)/shard_map/ppermute | solution.py:346
  84.4 13.5 %collective-permute-start.17 = (bf16[512,512]{1,0:T(8,128)(2,1)S(1)}, bf16[512,512]{1,0:T(8,128)(2,1)S(1)}, u32[]{:S(2)}, u32[]{:S(2)}) collective-permute-start(bf16[512,512]{1,0:T(8,128)(2,1)S(1)} %collective-permute-done.16), channel_id=1, source_target_pairs={{0,16},{16,0},{1,17},{17,1},{2,18},{18,2},{3,19},{19,3},{4,20},{20... | collective-permute-start | bytes 1572872 | tf_op jit(solution)/shard_map/ppermute | solution.py:289
  87.4 17.5 %collective-permute-start.15 = (bf16[80,2048]{1,0:T(8,128)(2,1)S(1)}, bf16[80,2048]{1,0:T(8,128)(2,1)S(1)}, u32[]{:S(2)}, u32[]{:S(2)}) collective-permute-start(bf16[80,2048]{1,0:T(8,128)(2,1)S(1)} %collective-permute-done.4), channel_id=1, source_target_pairs={{0,8},{8,0},{4,12},{12,4},{1,9},{9,1},{5,13},{13,5},{2,10},{10,2},... | collective-permute-start | bytes 983048 | tf_op jit(solution)/shard_map/ppermute | solution.py:293
  97.9 19.9 %collective-permute-start.25 = (bf16[512,512]{1,0:T(8,128)(2,1)S(1)}, bf16[512,512]{1,0:T(8,128)(2,1)S(1)}, u32[]{:S(2)}, u32[]{:S(2)}) collective-permute-start(bf16[512,512]{1,0:T(8,128)(2,1)S(1)} %get-tuple-element.101), channel_id=1, source_target_pairs={{0,1},{3,2},{4,5},{7,6},{8,9},{11,10},{12,13},{15,14},{16,17},{19,... | collective-permute-start | bytes 1572872 | tf_op jit(solution)/shard_map/ppermute | solution.py:281
  103.4 12.1 %collective-permute-start.20 = (bf16[512,512]{1,0:T(8,128)(2,1)S(1)}, bf16[512,512]{1,0:T(8,128)(2,1)S(1)}, u32[]{:S(2)}, u32[]{:S(2)}) collective-permute-start(bf16[512,512]{1,0:T(8,128)(2,1)S(1)} %collective-permute-done.19), channel_id=1, source_target_pairs={{0,16},{16,0},{1,17},{17,1},{2,18},{18,2},{3,19},{19,3},{4,20},{20... | collective-permute-start | bytes 1572872 | tf_op jit(solution)/shard_map/ppermute | solution.py:289
  105.1 13.4 %collective-permute-start.18 = (bf16[160,2048]{1,0:T(8,128)(2,1)S(1)}, bf16[160,2048]{1,0:T(8,128)(2,1)S(1)}, u32[]{:S(2)}, u32[]{:S(2)}) collective-permute-start(bf16[160,2048]{1,0:T(8,128)(2,1)S(1)} %pad_maximum_fusion.24), channel_id=1, source_target_pairs={{0,4},{4,0},{8,12},{12,8},{1,5},{5,1},{9,13},{13,9},{2,6},{6,2},{1... | collective-permute-start | bytes 1966088 | tf_op jit(solution)/shard_map/ppermute | solution.py:379
  115.5 13.9 %collective-permute-start.24 = (bf16[640,512]{1,0:T(8,128)(2,1)S(1)}, bf16[640,512]{1,0:T(8,128)(2,1)S(1)}, u32[]{:S(2)}, u32[]{:S(2)}) collective-permute-start(bf16[640,512]{1,0:T(8,128)(2,1)S(1)} %convolution_convert_fusion.4), channel_id=1, source_target_pairs={{1,2},{2,1},{5,6},{6,5},{9,10},{10,9},{13,14},{14,13},{17,18},{18,... | collective-permute-start | bytes 1966088 | tf_op jit(solution)/shard_map/ppermute | solution.py:368
  117.8 25.1 %collective-permute-start.27 = (bf16[640,512]{1,0:T(8,128)(2,1)S(1)}, bf16[640,512]{1,0:T(8,128)(2,1)S(1)}, u32[]{:S(2)}, u32[]{:S(2)}) collective-permute-start(bf16[640,512]{1,0:T(8,128)(2,1)S(1)} %convolution_convert_fusion.3), channel_id=1, source_target_pairs={{1,2},{2,1},{5,6},{6,5},{9,10},{10,9},{13,14},{14,13},{17,18},{18,... | collective-permute-start | bytes 1966088 | tf_op jit(solution)/shard_map/ppermute | solution.py:368
  118.5 19.7 %collective-permute-start.28 = (bf16[512,512]{1,0:T(8,128)(2,1)S(1)}, bf16[512,512]{1,0:T(8,128)(2,1)S(1)}, u32[]{:S(2)}, u32[]{:S(2)}) collective-permute-start(bf16[512,512]{1,0:T(8,128)(2,1)S(1)} %get-tuple-element.105), channel_id=1, source_target_pairs={{0,1},{3,2},{4,5},{7,6},{8,9},{11,10},{12,13},{15,14},{16,17},{19,... | collective-permute-start | bytes 1572872 | tf_op jit(solution)/shard_map/ppermute | solution.py:281
  124.6 32.5 %collective-permute-start.30 = (bf16[640,512]{1,0:T(8,128)(2,1)S(1)}, bf16[640,512]{1,0:T(8,128)(2,1)S(1)}, u32[]{:S(2)}, u32[]{:S(2)}) collective-permute-start(bf16[640,512]{1,0:T(8,128)(2,1)S(1)} %convolution_convert_fusion.2), channel_id=1, source_target_pairs={{1,2},{2,1},{5,6},{6,5},{9,10},{10,9},{13,14},{14,13},{17,18},{18,... | collective-permute-start | bytes 1966088 | tf_op jit(solution)/shard_map/ppermute | solution.py:368
  125.3 14.5 %collective-permute-start.26 = (bf16[512,512]{1,0:T(8,128)(2,1)S(1)}, bf16[512,512]{1,0:T(8,128)(2,1)S(1)}, u32[]{:S(2)}, u32[]{:S(2)}) collective-permute-start(bf16[512,512]{1,0:T(8,128)(2,1)S(1)} %collective-permute-done.25), channel_id=1, source_target_pairs={{0,16},{16,0},{1,17},{17,1},{2,18},{18,2},{3,19},{19,3},{4,20},{20... | collective-permute-start | bytes 1572872 | tf_op jit(solution)/shard_map/ppermute | solution.py:289
  129.4 16.3 %collective-permute-start.38 = (bf16[512,512]{1,0:T(8,128)(2,1)S(1)}, bf16[512,512]{1,0:T(8,128)(2,1)S(1)}, u32[]{:S(2)}, u32[]{:S(2)}) collective-permute-start(bf16[512,512]{1,0:T(8,128)(2,1)S(1)} %get-tuple-element.112), channel_id=1, source_target_pairs={{0,1},{3,2},{4,5},{7,6},{8,9},{11,10},{12,13},{15,14},{16,17},{19,... | collective-permute-start | bytes 1572872 | tf_op jit(solution)/shard_map/ppermute | solution.py:281
  138.2 21.7 %collective-permute-start.31 = (bf16[320,512]{1,0:T(8,128)(2,1)S(1)}, bf16[320,512]{1,0:T(8,128)(2,1)S(1)}, u32[]{:S(2)}, u32[]{:S(2)}) collective-permute-start(bf16[320,512]{1,0:T(8,128)(2,1)S(1)} %slice.83), channel_id=1, source_target_pairs={{1,0},{2,3},{5,4},{6,7},{9,8},{10,11},{13,12},{14,15},{17,16},{18,... | collective-permute-start | bytes 983048 | tf_op jit(solution)/shard_map/ppermute | solution.py:389
  139.8 14.2 %collective-permute-start.29 = (bf16[512,512]{1,0:T(8,128)(2,1)S(1)}, bf16[512,512]{1,0:T(8,128)(2,1)S(1)}, u32[]{:S(2)}, u32[]{:S(2)}) collective-permute-start(bf16[512,512]{1,0:T(8,128)(2,1)S(1)} %collective-permute-done.28), channel_id=1, source_target_pairs={{0,16},{16,0},{1,17},{17,1},{2,18},{18,2},{3,19},{19,3},{4,20},{20... | collective-permute-start | bytes 1572872 | tf_op jit(solution)/shard_map/ppermute | solution.py:289
  142.9 17.7 %collective-permute-start.23 = (bf16[320,512]{1,0:T(8,128)(2,1)S(1)}, bf16[320,512]{1,0:T(8,128)(2,1)S(1)}, u32[]{:S(2)}, u32[]{:S(2)}) collective-permute-start(bf16[320,512]{1,0:T(8,128)(2,1)S(1)} %slice.81), channel_id=1, source_target_pairs={{1,0},{2,3},{5,4},{6,7},{9,8},{10,11},{13,12},{14,15},{17,16},{18,... | collective-permute-start | bytes 983048 | tf_op jit(solution)/shard_map/ppermute | solution.py:389
  145.7 15.2 %collective-permute-start.35 = (bf16[640,512]{1,0:T(8,128)(2,1)S(1)}, bf16[640,512]{1,0:T(8,128)(2,1)S(1)}, u32[]{:S(2)}, u32[]{:S(2)}) collective-permute-start(bf16[640,512]{1,0:T(8,128)(2,1)S(1)} %convolution_convert_fusion.1), channel_id=1, source_target_pairs={{1,2},{2,1},{5,6},{6,5},{9,10},{10,9},{13,14},{14,13},{17,18},{18,... | collective-permute-start | bytes 1966088 | tf_op jit(solution)/shard_map/ppermute | solution.py:368
  154.0 10.1 %collective-permute-start.39 = (bf16[512,512]{1,0:T(8,128)(2,1)S(1)}, bf16[512,512]{1,0:T(8,128)(2,1)S(1)}, u32[]{:S(2)}, u32[]{:S(2)}) collective-permute-start(bf16[512,512]{1,0:T(8,128)(2,1)S(1)} %collective-permute-done.38), channel_id=1, source_target_pairs={{0,16},{16,0},{1,17},{17,1},{2,18},{18,2},{3,19},{19,3},{4,20},{20... | collective-permute-start | bytes 1572872 | tf_op jit(solution)/shard_map/ppermute | solution.py:289
  157.0 29.1 %collective-permute-start.37 = (bf16[320,512]{1,0:T(8,128)(2,1)S(1)}, bf16[320,512]{1,0:T(8,128)(2,1)S(1)}, u32[]{:S(2)}, u32[]{:S(2)}) collective-permute-start(bf16[320,512]{1,0:T(8,128)(2,1)S(1)} %slice.87), channel_id=1, source_target_pairs={{1,0},{2,3},{5,4},{6,7},{9,8},{10,11},{13,12},{14,15},{17,16},{18,... | collective-permute-start | bytes 983048 | tf_op jit(solution)/shard_map/ppermute | solution.py:389
  159.9 27.2 %collective-permute-start.41 = (bf16[640,512]{1,0:T(8,128)(2,1)S(1)}, bf16[640,512]{1,0:T(8,128)(2,1)S(1)}, u32[]{:S(2)}, u32[]{:S(2)}) collective-permute-start(bf16[640,512]{1,0:T(8,128)(2,1)S(1)} %convolution_convert_fusion), channel_id=1, source_target_pairs={{1,2},{2,1},{5,6},{6,5},{9,10},{10,9},{13,14},{14,13},{17,18},{18,... | collective-permute-start | bytes 1966088 | tf_op jit(solution)/shard_map/ppermute | solution.py:368
  160.9 47.0 %collective-permute-start.32 = (bf16[128,1024]{1,0:T(8,128)(2,1)S(1)}, bf16[128,1024]{1,0:T(8,128)(2,1)S(1)}, u32[]{:S(2)}, u32[]{:S(2)}) collective-permute-start(bf16[128,1024]{1,0:T(8,128)(2,1)S(1)} %get-tuple-element.174), channel_id=1, source_target_pairs={{0,4},{4,0},{8,12},{12,8},{1,5},{5,1},{9,13},{13,9},{2,6},{6,2},{1... | collective-permute-start | bytes 786440 | tf_op jit(solution)/shard_map/ppermute | solution.py:407
  161.0 47.8 %collective-permute-start.33 = (bf16[128,1024]{1,0:T(8,128)(2,1)S(1)}, bf16[128,1024]{1,0:T(8,128)(2,1)S(1)}, u32[]{:S(2)}, u32[]{:S(2)}) collective-permute-start(bf16[128,1024]{1,0:T(8,128)(2,1)S(1)} %get-tuple-element.173), channel_id=1, source_target_pairs={{0,8},{8,0},{4,12},{12,4},{1,9},{9,1},{5,13},{13,5},{2,10},{10,2},... | collective-permute-start | bytes 786440 | tf_op jit(solution)/shard_map/ppermute | solution.py:405
  164.1 22.1 %collective-permute-start.40 = (bf16[320,512]{1,0:T(8,128)(2,1)S(1)}, bf16[320,512]{1,0:T(8,128)(2,1)S(1)}, u32[]{:S(2)}, u32[]{:S(2)}) collective-permute-start(bf16[320,512]{1,0:T(8,128)(2,1)S(1)} %slice.89), channel_id=1, source_target_pairs={{1,0},{2,3},{5,4},{6,7},{9,8},{10,11},{13,12},{14,15},{17,16},{18,... | collective-permute-start | bytes 983048 | tf_op jit(solution)/shard_map/ppermute | solution.py:389
  186.2 20.7 %collective-permute-start.34 = (bf16[128,1024]{1,0:T(8,128)(2,1)S(1)}, bf16[128,1024]{1,0:T(8,128)(2,1)S(1)}, u32[]{:S(2)}, u32[]{:S(2)}) collective-permute-start(bf16[128,1024]{1,0:T(8,128)(2,1)S(1)} %get-tuple-element.172), channel_id=1, source_target_pairs={{0,12},{12,0},{4,8},{8,4},{1,13},{13,1},{5,9},{9,5},{2,14},{14,2},... | collective-permute-start | bytes 786440 | tf_op jit(solution)/shard_map/ppermute | solution.py:406
  187.1 28.7 %collective-permute-start.43 = (bf16[320,512]{1,0:T(8,128)(2,1)S(1)}, bf16[320,512]{1,0:T(8,128)(2,1)S(1)}, u32[]{:S(2)}, u32[]{:S(2)}) collective-permute-start(bf16[320,512]{1,0:T(8,128)(2,1)S(1)} %convolution_convert_fusion.5), channel_id=1, source_target_pairs={{1,2},{2,1},{5,6},{6,5},{9,10},{10,9},{13,14},{14,13},{17,18},{18,... | collective-permute-start | bytes 983048 | tf_op jit(solution)/shard_map/ppermute | solution.py:358
  189.4 17.4 %collective-permute-start.36 = (bf16[320,512]{1,0:T(8,128)(2,1)S(1)}, bf16[320,512]{1,0:T(8,128)(2,1)S(1)}, u32[]{:S(2)}, u32[]{:S(2)}) collective-permute-start(bf16[320,512]{1,0:T(8,128)(2,1)S(1)} %slice.85), channel_id=1, source_target_pairs={{1,0},{2,3},{5,4},{6,7},{9,8},{10,11},{13,12},{14,15},{17,16},{18,... | collective-permute-start | bytes 983048 | tf_op jit(solution)/shard_map/ppermute | solution.py:389
  206.7 21.8 %collective-permute-start.55 = (bf16[128,1024]{1,0:T(8,128)(2,1)S(1)}, bf16[128,1024]{1,0:T(8,128)(2,1)S(1)}, u32[]{:S(2)}, u32[]{:S(2)}) collective-permute-start(bf16[128,1024]{1,0:T(8,128)(2,1)S(1)} %get-tuple-element.170), channel_id=1, source_target_pairs={{0,4},{4,0},{8,12},{12,8},{1,5},{5,1},{9,13},{13,9},{2,6},{6,2},{1... | collective-permute-start | bytes 786440 | tf_op jit(solution)/shard_map/ppermute | solution.py:407
  206.9 21.7 %collective-permute-start.56 = (bf16[128,1024]{1,0:T(8,128)(2,1)S(1)}, bf16[128,1024]{1,0:T(8,128)(2,1)S(1)}, u32[]{:S(2)}, u32[]{:S(2)}) collective-permute-start(bf16[128,1024]{1,0:T(8,128)(2,1)S(1)} %get-tuple-element.169), channel_id=1, source_target_pairs={{0,8},{8,0},{4,12},{12,4},{1,9},{9,1},{5,13},{13,5},{2,10},{10,2},... | collective-permute-start | bytes 786440 | tf_op jit(solution)/shard_map/ppermute | solution.py:405
  207.9 22.5 %collective-permute-start.57 = (bf16[128,1024]{1,0:T(8,128)(2,1)S(1)}, bf16[128,1024]{1,0:T(8,128)(2,1)S(1)}, u32[]{:S(2)}, u32[]{:S(2)}) collective-permute-start(bf16[128,1024]{1,0:T(8,128)(2,1)S(1)} %get-tuple-element.168), channel_id=1, source_target_pairs={{0,12},{12,0},{4,8},{8,4},{1,13},{13,1},{5,9},{9,5},{2,14},{14,2},... | collective-permute-start | bytes 786440 | tf_op jit(solution)/shard_map/ppermute | solution.py:406
  208.8 11.8 %collective-permute-start.45 = (bf16[320,512]{1,0:T(8,128)(2,1)S(1)}, bf16[320,512]{1,0:T(8,128)(2,1)S(1)}, u32[]{:S(2)}, u32[]{:S(2)}) collective-permute-start(bf16[320,512]{1,0:T(8,128)(2,1)S(1)} %slice.91), channel_id=1, source_target_pairs={{1,0},{2,3},{5,4},{6,7},{9,8},{10,11},{13,12},{14,15},{17,16},{18,... | collective-permute-start | bytes 983048 | tf_op jit(solution)/shard_map/ppermute | solution.py:389
  215.8 11.8 %collective-permute-start.44 = (bf16[320,512]{1,0:T(8,128)(2,1)S(1)}, bf16[320,512]{1,0:T(8,128)(2,1)S(1)}, u32[]{:S(2)}, u32[]{:S(2)}) collective-permute-start(bf16[320,512]{1,0:T(8,128)(2,1)S(1)} %fusion.6), channel_id=1, source_target_pairs={{1,0},{2,3},{5,4},{6,7},{9,8},{10,11},{13,12},{14,15},{17,16},{18,... | collective-permute-start | bytes 983048 | tf_op jit(solution)/shard_map/ppermute | solution.py:453
  230.4 17.4 %collective-permute-start.49 = (bf16[128,512]{1,0:T(8,128)(2,1)S(1)}, bf16[128,512]{1,0:T(8,128)(2,1)S(1)}, u32[]{:S(2)}, u32[]{:S(2)}) collective-permute-start(bf16[128,512]{1,0:T(8,128)(2,1)S(1)} %get-tuple-element.184), channel_id=1, source_target_pairs={{0,4},{4,0},{8,12},{12,8},{1,5},{5,1},{9,13},{13,9},{2,6},{6,2},{1... | collective-permute-start | bytes 393224 | tf_op jit(solution)/shard_map/ppermute | solution.py:407
  230.4 17.4 %collective-permute-start.50 = (bf16[128,512]{1,0:T(8,128)(2,1)S(1)}, bf16[128,512]{1,0:T(8,128)(2,1)S(1)}, u32[]{:S(2)}, u32[]{:S(2)}) collective-permute-start(bf16[128,512]{1,0:T(8,128)(2,1)S(1)} %get-tuple-element.183), channel_id=1, source_target_pairs={{0,8},{8,0},{4,12},{12,4},{1,9},{9,1},{5,13},{13,5},{2,10},{10,2},... | collective-permute-start | bytes 393224 | tf_op jit(solution)/shard_map/ppermute | solution.py:405
  233.6 17.4 %collective-permute-start.48 = (bf16[128,512]{1,0:T(8,128)(2,1)S(1)}, bf16[128,512]{1,0:T(8,128)(2,1)S(1)}, u32[]{:S(2)}, u32[]{:S(2)}) collective-permute-start(bf16[128,512]{1,0:T(8,128)(2,1)S(1)} %get-tuple-element.186), channel_id=1, source_target_pairs={{0,12},{12,0},{4,8},{8,4},{1,13},{13,1},{5,9},{9,5},{2,14},{14,2},... | collective-permute-start | bytes 393224 | tf_op jit(solution)/shard_map/ppermute | solution.py:406
  235.2 15.8 %collective-permute-start.46 = (bf16[128,512]{1,0:T(8,128)(2,1)S(1)}, bf16[128,512]{1,0:T(8,128)(2,1)S(1)}, u32[]{:S(2)}, u32[]{:S(2)}) collective-permute-start(bf16[128,512]{1,0:T(8,128)(2,1)S(1)} %get-tuple-element.188), channel_id=1, source_target_pairs={{0,4},{4,0},{8,12},{12,8},{1,5},{5,1},{9,13},{13,9},{2,6},{6,2},{1... | collective-permute-start | bytes 393224 | tf_op jit(solution)/shard_map/ppermute | solution.py:407
  238.1 13.0 %collective-permute-start.47 = (bf16[128,512]{1,0:T(8,128)(2,1)S(1)}, bf16[128,512]{1,0:T(8,128)(2,1)S(1)}, u32[]{:S(2)}, u32[]{:S(2)}) collective-permute-start(bf16[128,512]{1,0:T(8,128)(2,1)S(1)} %get-tuple-element.187), channel_id=1, source_target_pairs={{0,8},{8,0},{4,12},{12,4},{1,9},{9,1},{5,13},{13,5},{2,10},{10,2},... | collective-permute-start | bytes 393224 | tf_op jit(solution)/shard_map/ppermute | solution.py:405
  (18 other events, 160.5 us)
